TPU v7x, 256 devices: a whole 4x4x8 slice. The times are simulated.
256 devices in a mesh: gx: 4 (over x), gy: 8 (over y, core), gz: 8 (over z).
Axes of the slice: x: 4, y: 4, z: 8, core: 2. Of those that a mesh axis runs over, the one named last changes fastest.
Arguments:
- queries: bfloat16 [16384, 4096], P(('gx', 'gy'), 'gz'), may hold values from -6 to 6
- key_rows: bfloat16 [16384, 4096], P(('gx', 'gy'), 'gz'), may hold values from -24 to 24
- values: bfloat16 [16384, 4096], P(('gx', 'gy'), 'gz'), may hold values from -24 to 24
- tile_list: int32 [64, 32, 8], P(('gx', 'gy'), 'gz'), may hold values from 0 to 63, as said below
- out_weight: bfloat16 [4096, 4096], P('gz'), may hold values from -0.09375 to 0.09375
Outputs:
- projected: bfloat16 [16384, 4096], P(('gx', 'gy', 'gz'))
Inputs may be any that keep to these rules, and one draw needn't show every extreme that they name: `tile_list`: each (query block, head) lists 8 different key blocks, one of which is the query block itself.
All inputs are finite; a program needn't handle non-finite values.
Results may differ from a plain program's by a relative error of at most 0.012.
Values may be sent and summed in bfloat16 or wider, within the bound.
No kernel may reach another device: no remote copies, remote signals or barrier semaphores. Data moves between devices by JAX's collectives and lax.ppermute only.
A program may use at most 64 MiB of HBM per device.

v0:
```python
import jax
import jax.numpy as jnp
from jax import lax
from jax.experimental import pallas as pl
from jax.experimental.pallas import tpu as pltpu
from jax.sharding import PartitionSpec as P

BLOCK = 256
HD = 128
UNIT = 144
ROWS = 4 * UNIT
F32 = jnp.float32
BF16 = jnp.bfloat16


def call(kernel, out_shape, flops, vmem_mib):
    return pl.pallas_call(
        kernel,
        out_shape=out_shape,
        compiler_params=pltpu.CompilerParams(vmem_limit_bytes=vmem_mib << 20),
        cost_estimate=pl.CostEstimate(flops=flops, bytes_accessed=flops // 256, transcendentals=0),
    )


def features(source):
    widened = source.astype(F32)
    return jnp.where(widened > 0, widened + 1.0, jnp.exp(jnp.minimum(widened, 0.0))).astype(BF16)


def high_and_low(total):
    high = total.astype(BF16).astype(F32)
    row = lax.broadcasted_iota(jnp.int32, (16, HD), 0)
    return jnp.where(row == 0, high, jnp.where(row == 1, total - high, 0.0)).astype(BF16)


def head_columns(h):
    return pl.ds(pl.multiple_of(h * HD, HD), HD)


def chunk_rows(j):
    return pl.ds(pl.multiple_of(j * 64, 64), 64)


def states_kernel(kv_ref, own_ref, mate_ref, keep_ref, send_ref, lists_ref):
    core = lax.rem(lax.axis_index("gy"), 2)
    ones = jnp.ones((16, BLOCK), BF16)
    entry = lax.broadcasted_iota(jnp.int32, (8, HD), 0)
    lane = lax.broadcasted_iota(jnp.int32, (8, HD), 1)
    repeat = jnp.where(lane // 16 == entry, 1.0, 0.0).astype(BF16)
    for i, list_ref in enumerate((own_ref, mate_ref)):
        for b in range(2):
            listed = list_ref[b].astype(F32).astype(BF16)
            at = i * 8 + b * 4
            lists_ref[at : at + 4, :] = jnp.dot(listed, repeat, preferred_element_type=F32)
    row = lax.broadcasted_iota(jnp.int32, (16, HD), 0)
    for u_ref, role in ((keep_ref, core), (send_ref, 1 - core)):
        for b in range(2):
            rows = pl.ds(b * BLOCK, BLOCK)
            for hh in range(2):
                at = (b * 2 + hh) * UNIT
                columns = head_columns(2 * role + hh)
                kf = kv_ref[rows, columns]
                state = lax.dot_general(
                    kv_ref[pl.ds((2 + b) * BLOCK, BLOCK), columns], kf, (((0,), (0,)), ((), ())), preferred_element_type=F32
                )
                u_ref[at : at + HD, :] = state.astype(BF16)
                tail = high_and_low(jnp.dot(ones, kf, preferred_element_type=F32))
                if u_ref is keep_ref:
                    other = b * 4 + 2 * (1 - core) + hh
                    tail = jnp.where(row == 2, lists_ref[pl.ds(8 + other, 1), :], tail.astype(F32))
                    tail = jnp.where(row == 3, lists_ref[pl.ds(other, 1), :], tail).astype(BF16)
                u_ref[at + HD : at + UNIT, :] = tail


def key_blocks():
    gx, gy = lax.axis_index("gx"), lax.axis_index("gy")
    y, core = gy // 2, lax.rem(gy, 2)
    k = lax.rem(lax.broadcasted_iota(jnp.int32, (256, HD), 1), 16)
    back, other, b = k // 4, lax.rem(k // 2, 2), lax.rem(k, 2)
    key_x = lax.rem(gx - back * core + 4, 4)
    key_y = lax.rem(y - back * (1 - core) + 4, 4)
    key_core = core + other * (1 - 2 * core)
    return (2 * (key_x * 8 + key_y * 2 + key_core) + b).astype(F32)


def partial_kernel(*refs):
    lists, keys, outs = refs[:4], refs[4:12], refs[12:]
    core, kb = lax.rem(lax.axis_index("gy"), 2), key_blocks()
    lane = lax.broadcasted_iota(jnp.int32, (HD, 256), 0)
    col = lax.broadcasted_iota(jnp.int32, (HD, 256), 1)
    spread = jnp.where(lax.rem(lane, 16) == col // 16, 1.0, 0.0).astype(BF16)
    row = lax.broadcasted_iota(jnp.int32, (256, 256), 0)
    col = lax.broadcasted_iota(jnp.int32, (256, 256), 1)
    same = jnp.where(lax.rem(row, 16) == lax.rem(col, 16), 1.0, 0.0)
    blocks = [(d * 2 + c, b * 2 * UNIT) for d in range(4) for c in range(2) for b in range(2)]
    for hh in range(2):
        listed = []
        for d in range(4):
            for c in range(2):
                for b in range(2):
                    if d == 0:
                        one = lists[0][pl.ds(c * 8 + b * 4 + 2 * core + hh, 1), :]
                    else:
                        at = (b * 2 + hh) * UNIT + HD
                        one = lists[d][at : at + 16, :].astype(F32)[2 + c : 3 + c, :]
                    listed.append(jnp.broadcast_to(one, (16, HD)))
        hit = jnp.where(jnp.concatenate(listed, axis=0) == kb, 1.0, 0.0).astype(BF16)
        mix = (jnp.dot(hit, spread, preferred_element_type=F32) * same).astype(BF16)
        for g in range(9):
            shift = hh * UNIT + g * 16
            pieces = [keys[d][at + shift : at + shift + 16, :] for d, at in blocks]
            summed = jnp.dot(mix, jnp.concatenate(pieces, axis=0), preferred_element_type=F32)
            for q, (d, at) in enumerate(blocks):
                piece = summed[q * 16 : q * 16 + 16, :]
                if g == 8:
                    outs[d][at + shift : at + shift + 16, :] = high_and_low(piece[0:1] + piece[1:2])
                else:
                    outs[d][at + shift : at + shift + 16, :] = piece.astype(BF16)


def attend(q_ref, state_ref, sums_ref, at, rows, columns):
    dims = (((1,), (1,)), ((), ()))
    q = q_ref[rows, columns]
    num = lax.dot_general(q, state_ref[at, :], dims, preferred_element_type=F32)
    sums = sums_ref[at, :]
    return (num / lax.dot_general(q, sums, dims, preferred_element_type=F32)).astype(BF16)


def far_kernel(qf_ref, w_ref, *refs):
    parts, (right_ref, left_ref, state_ref, sums_ref, att_ref) = (refs[:4], refs[4:8]), refs[8:]
    core, far = lax.rem(lax.axis_index("gy"), 2), lax.rem(lax.axis_index("gz") + 4, 8)
    for side in range(2):
        role = core if side == 0 else 1 - core
        for u in range(4):
            at = u * UNIT
            total = sum(p[at : at + UNIT, :].astype(F32) for p in parts[side])
            to = pl.ds(pl.multiple_of((u // 2 * 4 + 2 * role + u % 2) * HD, HD), HD)
            state_ref[to, :] = total[:HD].astype(BF16)
            key_sum = total[HD : HD + 1] + total[HD + 1 : HD + 2]
            sums_ref[to, :] = jnp.broadcast_to(key_sum, (HD, HD)).astype(BF16)
    for h in range(4):
        at = pl.ds(pl.multiple_of((far // 4 * 4 + h) * HD, HD), HD)
        columns = slice(h * HD, (h + 1) * HD)
        att_ref[:, columns] = attend(qf_ref, state_ref, sums_ref, at, chunk_rows(far), columns)
    half = w_ref.shape[1] // 2
    right_ref[...] = jnp.dot(att_ref[...], w_ref[:, half:], preferred_element_type=F32).astype(BF16)
    left_ref[...] = jnp.dot(att_ref[...], w_ref[:, :half], preferred_element_type=F32).astype(BF16)


def project_kernel(qf_ref, w_ref, state_ref, sums_ref, *refs):
    r3_ref, l3_ref, f3_ref, e2_ref, f2_ref, e1_ref, f1_ref, own_ref, att_ref = refs
    gz = lax.axis_index("gz")
    for b in range(2):
        for h in range(4):
            at, columns = pl.ds((b * 4 + h) * HD, HD), slice(h * HD, (h + 1) * HD)
            rows = pl.ds(b * BLOCK, BLOCK)
            att_ref[rows, columns] = attend(qf_ref, state_ref, sums_ref, at, rows, columns)
    hops = (3, 5, 2, 6, 1, 7, 0)
    lhs = jnp.concatenate([att_ref[chunk_rows(lax.rem(gz + hop, 8)), :] for hop in hops], axis=0)
    half = w_ref.shape[1] // 2
    for i in range(2):
        for c in range(0, half, 512):
            out = jnp.dot(lhs, w_ref[:, i * half + c : i * half + c + 512], preferred_element_type=F32)
            cols = slice(c, c + 512)
            for n, (e_ref, f_ref) in enumerate(((None, f3_ref), (e2_ref, f2_ref), (e1_ref, f1_ref))):
                right, left = out[n * 128 : n * 128 + 64], out[n * 128 + 64 : n * 128 + 128]
                early = (right, left)[i]
                f_ref[(64, 0)[i] : (128, 64)[i], cols] = (left, right)[i]
                if e_ref is None:
                    (r3_ref, l3_ref)[i][:, cols] = early.astype(BF16)
                else:
                    e_ref[(0, 64)[i] : (64, 128)[i], cols] = early
            own_ref[:, i * half + c : i * half + c + 512] = out[384:448]


def hop_kernel(term_ref, from_left_ref, from_right_ref, right_ref, left_ref):
    right_ref[...] = (term_ref[:64, :] + from_left_ref[...].astype(F32)).astype(BF16)
    left_ref[...] = (term_ref[64:, :] + from_right_ref[...].astype(F32)).astype(BF16)


def last_kernel(own_ref, right0, left1, right1, left0, out_ref):
    half = own_ref.shape[1] // 2
    for i, (a, b) in enumerate(((right0, left0), (right1, left1))):
        out_ref[:, i * half : (i + 1) * half] = (
            own_ref[:, i * half : (i + 1) * half] + a[...].astype(F32) + b[...].astype(F32)
        ).astype(BF16)


def per_device(queries, key_rows, values, tile_list, out_weight):
    def by_role(a, d, axes, cross=False):
        pairs = []
        for i in range(4):
            for j in range(4):
                for c in range(2):
                    to = ((i + d) % 4, j) if axes[c] == "x" else (i, (j + d) % 4)
                    pairs.append((i * 8 + j * 2 + c, to[0] * 8 + to[1] * 2 + (c ^ cross)))
        return lax.ppermute(a, ("gx", "gy"), pairs)

    to_mate = lambda a: lax.ppermute(a, "gy", [(i, i ^ 1) for i in range(8)])
    along_z = lambda a, d: lax.ppermute(a, "gz", [(i, (i + d) % 8) for i in range(8)])

    unit = jax.ShapeDtypeStruct((ROWS, HD), BF16)
    kv = jnp.concatenate([features(key_rows), values])
    keep, send, lists = call(
        states_kernel, (unit, unit, jax.ShapeDtypeStruct((16, HD), F32)), 10**9, 8
    )(kv, tile_list, to_mate(tile_list))
    keys = {(0, 0): keep}
    for d in (2, 1, 3):
        keys[d, 0] = by_role(keep, d, "yx")
        keys[d, 1] = by_role(send, d, "xy", cross=True)
    keys[0, 1] = to_mate(send)

    lists = [lists] + [to_mate(keys[d, 0]) for d in (1, 2, 3)]
    order = [(d, c) for d in range(4) for c in range(2)]
    parts = call(partial_kernel, (unit,) * 8, 10**9, 16)(*lists, *(keys[i] for i in order))
    parts = dict(zip(order, parts))
    for d in (2, 1, 3):
        parts[d, 0] = by_role(parts[d, 0], -d, "xy")
        parts[d, 1] = by_role(parts[d, 1], -d, "xy", cross=True)
    parts[0, 1] = to_mate(parts[0, 1])

    qf = features(queries)
    half = out_weight.shape[1] // 2
    piece = jax.ShapeDtypeStruct((64, half), BF16)
    heads = jax.ShapeDtypeStruct((8 * HD, HD), BF16)
    right1, left0, states, sums, _ = call(
        far_kernel,
        (piece, piece, heads, heads, jax.ShapeDtypeStruct((64, queries.shape[1]), BF16)),
        10**9,
        16,
    )(qf, out_weight, *(parts[d, c] for c in range(2) for d in range(4)))
    right1, left0 = along_z(right1, 1), along_z(left0, -1)
    term = jax.ShapeDtypeStruct((128, half), F32)
    right0, left1, f3, e2, f2, e1, f1, own, _ = call(
        project_kernel,
        (piece, piece)
        + (term,) * 5
        + (jax.ShapeDtypeStruct((64, 2 * half), F32), jax.ShapeDtypeStruct(queries.shape, BF16)),
        4 * 10**9,
        20,
    )(qf, out_weight, states, sums)
    right0, left1 = along_z(right0, 1), along_z(left1, -1)

    def hop(term, from_left, from_right):
        right, left = call(hop_kernel, (piece, piece), 10**8, 4)(term, from_left, from_right)
        return along_z(right, 1), along_z(left, -1)

    right1, left0 = hop(f3, right1, left0)
    right0, left1 = hop(e2, right0, left1)
    right1, left0 = hop(f2, right1, left0)
    right0, left1 = hop(e1, right0, left1)
    right1, left0 = hop(f1, right1, left0)
    return call(last_kernel, jax.ShapeDtypeStruct((64, 2 * half), BF16), 10**8, 8)(
        own, right0, left1, right1, left0
    )


def solution(mesh):
    return jax.shard_map(
        per_device,
        mesh=mesh,
        in_specs=(
            P(("gx", "gy"), "gz"),
            P(("gx", "gy"), "gz"),
            P(("gx", "gy"), "gz"),
            P(("gx", "gy"), "gz", None),
            P("gz", None),
        ),
        out_specs=P(("gx", "gy", "gz"), None),
        check_vma=False,
    )
```

profile of v0, /device:TPU:1, one launch (start us, length us, event | category | flops | bytes accessed | tf_op | source)
XLA Modules:
  0.0 81.1 jit_solution(15158131681750145331)
XLA Ops:
  0.0 3.2 %collective-permute-start = (s32[2,4,8]{2,1,0:T(4,128)}, s32[2,4,8]{2,1,0:T(4,128)S(1)}, u32[]{:S(2)}, u32[]{:S(2)}) collective-permute-start(s32[2,4,8]{2,1,0:T(4,128)} %own_ref.1), channel_id=1, source_target_pairs={{0,8},{8,0},{16,24},{24,16},{32,40},{40,32},{48,56},{56,48},{1,9},... | collective-permute-start | bytes 776 | tf_op jit(solution)/shard_map/ppermute | solution.py:199
  3.2 1.3 %fusion.4 = bf16[512,512]{1,0:T(8,128)(2,1)S(1)} fusion(bf16[512,512]{1,0:T(8,128)(2,1)} %param.6), kind=kLoop, calls=%fused_computation.10 | loop fusion | flops 1572864 | bytes 1048576 | tf_op jit(solution)/shard_map/convert_element_type | solution.py:27
  4.5 1.1 %pad_maximum_fusion.kv_ref = bf16[1024,512]{1,0:T(8,128)(2,1)S(1)} fusion(bf16[512,512]{1,0:T(8,128)(2,1)} %param.7, bf16[512,512]{1,0:T(8,128)(2,1)S(1)} %fusion.4), kind=kLoop, calls=%fused_computation.12 | loop fusion | flops 2097152 | bytes 2097152 | tf_op jit(solution)/shard_map/concatenate | solution.py:203
  5.6 0.4 shard_map.55
  6.1 0.8 %collective-permute-start.5 = (bf16[576,128]{1,0:T(8,128)(2,1)S(1)}, bf16[576,128]{1,0:T(8,128)(2,1)S(1)}, u32[]{:S(2)}, u32[]{:S(2)}) collective-permute-start(bf16[576,128]{1,0:T(8,128)(2,1)S(1)} %get-tuple-element.39.refs_4_), channel_id=1, source_target_pairs={{0,48},{8,200},{16,0},{24,216},{32,16},{40,232},{48,32},{56,248},{... | collective-permute-start | bytes 442376 | tf_op jit(solution)/shard_map/ppermute | solution.py:197
  6.9 0.5 collective-permute-start.3
  7.4 0.6 collective-permute-start.1
  8.0 2.9 %collective-permute-start.10 = (bf16[576,128]{1,0:T(8,128)(2,1)S(1)}, bf16[576,128]{1,0:T(8,128)(2,1)S(1)}, u32[]{:S(2)}, u32[]{:S(2)}) collective-permute-start(bf16[576,128]{1,0:T(8,128)(2,1)S(1)} %get-tuple-element.40), channel_id=1, source_target_pairs={{0,200},{8,48},{16,216},{24,0},{32,232},{40,16},{48,248},{56,32},{... | collective-permute-start | bytes 442376 | tf_op jit(solution)/shard_map/ppermute | solution.py:197
  10.9 2.4 %collective-permute-start.9 = (bf16[576,128]{1,0:T(8,128)(2,1)S(1)}, bf16[576,128]{1,0:T(8,128)(2,1)S(1)}, u32[]{:S(2)}, u32[]{:S(2)}) collective-permute-start(bf16[576,128]{1,0:T(8,128)(2,1)S(1)} %get-tuple-element.40), channel_id=1, source_target_pairs={{0,136},{8,32},{16,152},{24,48},{32,168},{40,0},{48,184},{56,16},{... | collective-permute-start | bytes 442376 | tf_op jit(solution)/shard_map/ppermute | solution.py:197
  13.3 0.1 collective-permute-start.8
  13.4 0.8 collective-permute-start.7
  14.3 2.1 %collective-permute-start.6 = (bf16[576,128]{1,0:T(8,128)(2,1)S(1)}, bf16[576,128]{1,0:T(8,128)(2,1)S(1)}, u32[]{:S(2)}, u32[]{:S(2)}) collective-permute-start(bf16[576,128]{1,0:T(8,128)(2,1)S(1)} %collective-permute-done.5.refs_10_), channel_id=1, source_target_pairs={{0,8},{8,0},{16,24},{24,16},{32,40},{40,32},{48,56},{56,48},{1,9},... | collective-permute-start | bytes 442376 | tf_op jit(solution)/shard_map/ppermute | solution.py:199
  16.4 0.6 collective-permute-done.9.refs_9_
  17.0 0.3 collective-permute-start.2
  17.3 2.1 %collective-permute-done.8.refs_7_ = bf16[576,128]{1,0:T(8,128)(2,1)S(1)} collective-permute-done((bf16[576,128]{1,0:T(8,128)(2,1)S(1)}, bf16[576,128]{1,0:T(8,128)(2,1)S(1)}, u32[]{:S(2)}, u32[]{:S(2)}) %collective-permute-start.8) | collective-permute-done | bytes 147488 | tf_op jit(solution)/shard_map/ppermute | solution.py:197
  19.4 1.1 %shard_map.56 = (bf16[576,128]{1,0:T(8,128)(2,1)S(1)}, bf16[576,128]{1,0:T(8,128)(2,1)S(1)}, bf16[576,128]{1,0:T(8,128)(2,1)S(1)}, bf16[576,128]{1,0:T(8,128)(2,...) custom-call(f32[16,128]{1,0:T(8,128)S(1)} %get-tuple-element.38.refs, ...), custom_call_target="tpu_custom_call" | custom-call | flops 1000000000 | bytes 3906250 | tf_op jit(solution)/shard_map/pallas_call | solution.py:215
  20.5 1.0 %collective-permute-start.11 = (bf16[576,128]{1,0:T(8,128)(2,1)S(1)}, bf16[576,128]{1,0:T(8,128)(2,1)S(1)}, u32[]{:S(2)}, u32[]{:S(2)}) collective-permute-start(bf16[576,128]{1,0:T(8,128)(2,1)S(1)} %get-tuple-element.42), channel_id=1, source_target_pairs={{0,192},{8,56},{16,208},{24,8},{32,224},{40,24},{48,240},{56,40},{... | collective-permute-start | bytes 442376 | tf_op jit(solution)/shard_map/ppermute | solution.py:197
  21.5 1.0 %collective-permute-start.12 = (bf16[576,128]{1,0:T(8,128)(2,1)S(1)}, bf16[576,128]{1,0:T(8,128)(2,1)S(1)}, u32[]{:S(2)}, u32[]{:S(2)}) collective-permute-start(bf16[576,128]{1,0:T(8,128)(2,1)S(1)} %get-tuple-element.43), channel_id=1, source_target_pairs={{0,128},{8,40},{16,144},{24,56},{32,160},{40,8},{48,176},{56,24},{... | collective-permute-start | bytes 442376 | tf_op jit(solution)/shard_map/ppermute | solution.py:197
  22.5 0.1 collective-permute-start.13
  22.6 2.9 %collective-permute-start.14 = (bf16[576,128]{1,0:T(8,128)(2,1)S(1)}, bf16[576,128]{1,0:T(8,128)(2,1)S(1)}, u32[]{:S(2)}, u32[]{:S(2)}) collective-permute-start(bf16[576,128]{1,0:T(8,128)(2,1)S(1)} %get-tuple-element.45), channel_id=1, source_target_pairs={{0,8},{8,0},{16,24},{24,16},{32,40},{40,32},{48,56},{56,48},{1,9},... | collective-permute-start | bytes 442376 | tf_op jit(solution)/shard_map/ppermute | solution.py:199
  25.5 2.6 %collective-permute-start.16 = (bf16[576,128]{1,0:T(8,128)(2,1)S(1)}, bf16[576,128]{1,0:T(8,128)(2,1)S(1)}, u32[]{:S(2)}, u32[]{:S(2)}) collective-permute-start(bf16[576,128]{1,0:T(8,128)(2,1)S(1)} %get-tuple-element.47), channel_id=1, source_target_pairs={{0,136},{8,32},{16,152},{24,48},{32,168},{40,0},{48,184},{56,16},{... | collective-permute-start | bytes 442376 | tf_op jit(solution)/shard_map/ppermute | solution.py:197
  28.2 0.9 %collective-permute-start.17 = (bf16[576,128]{1,0:T(8,128)(2,1)S(1)}, bf16[576,128]{1,0:T(8,128)(2,1)S(1)}, u32[]{:S(2)}, u32[]{:S(2)}) collective-permute-start(bf16[576,128]{1,0:T(8,128)(2,1)S(1)} %get-tuple-element.48), channel_id=1, source_target_pairs={{0,72},{8,16},{16,88},{24,32},{32,104},{40,48},{48,120},{56,0},{64... | collective-permute-start | bytes 442376 | tf_op jit(solution)/shard_map/ppermute | solution.py:197
  29.0 0.3 fusion.1.qf_ref
  29.3 1.0 %collective-permute-done.15.refs_5_ = bf16[576,128]{1,0:T(8,128)(2,1)S(1)} collective-permute-done((bf16[576,128]{1,0:T(8,128)(2,1)S(1)}, bf16[576,128]{1,0:T(8,128)(2,1)S(1)}, u32[]{:S(2)}, u32[]{:S(2)}) %collective-permute-start.15) | collective-permute-done | bytes 147488 | tf_op jit(solution)/shard_map/ppermute | solution.py:197
  30.3 2.5 %collective-permute-done.16.refs_6_ = bf16[576,128]{1,0:T(8,128)(2,1)S(1)} collective-permute-done((bf16[576,128]{1,0:T(8,128)(2,1)S(1)}, bf16[576,128]{1,0:T(8,128)(2,1)S(1)}, u32[]{:S(2)}, u32[]{:S(2)}) %collective-permute-start.16) | collective-permute-done | bytes 147488 | tf_op jit(solution)/shard_map/ppermute | solution.py:197
  32.8 1.6 %collective-permute-done.17.refs_7_ = bf16[576,128]{1,0:T(8,128)(2,1)S(1)} collective-permute-done((bf16[576,128]{1,0:T(8,128)(2,1)S(1)}, bf16[576,128]{1,0:T(8,128)(2,1)S(1)}, u32[]{:S(2)}, u32[]{:S(2)}) %collective-permute-start.17) | collective-permute-done | bytes 147488 | tf_op jit(solution)/shard_map/ppermute | solution.py:197
  34.4 1.5 %shard_map.57 = (bf16[64,2048]{1,0:T(8,128)(2,1)S(1)}, bf16[64,2048]{1,0:T(8,128)(2,1)S(1)}, bf16[1024,128]{1,0:T(8,128)(2,1)S(1)}, bf16[1024,128]{1,0:T(8,128)(2,1)S(1)}, bf16[64,512]{1,0:T(8,128)(2,1)}) custom-call(bf16[512,512]{1,0:T(8,128)(2,1)S(1)} %fusion.1.qf_ref, bf16[512,4096]{1,0:T(8,128)(2,1)S(1)} %copy-done, ...), custom_call_target="tpu_custom_call" | custom-call | flops 1000000000 | bytes 3906250 | tf_op jit(solution)/shard_map/pallas_call | solution.py:226
  35.9 1.6 %collective-permute-start.24 = (bf16[64,2048]{1,0:T(8,128)(2,1)S(1)}, bf16[64,2048]{1,0:T(8,128)(2,1)S(1)}, u32[]{:S(2)}, u32[]{:S(2)}) collective-permute-start(bf16[64,2048]{1,0:T(8,128)(2,1)S(1)} %get-tuple-element.63), channel_id=1, source_target_pairs={{0,1},{1,2},{2,3},{3,4},{4,5},{5,6},{6,7},{7,0},{8,9},{9,10},{10,1... | collective-permute-start | bytes 786440 | tf_op jit(solution)/shard_map/ppermute | solution.py:200
  37.6 3.9 %collective-permute-start.25 = (bf16[64,2048]{1,0:T(8,128)(2,1)S(1)}, bf16[64,2048]{1,0:T(8,128)(2,1)S(1)}, u32[]{:S(2)}, u32[]{:S(2)}) collective-permute-start(bf16[64,2048]{1,0:T(8,128)(2,1)S(1)} %get-tuple-element.64), channel_id=1, source_target_pairs={{0,7},{1,0},{2,1},{3,2},{4,3},{5,4},{6,5},{7,6},{8,15},{9,8},{10,9... | collective-permute-start | bytes 786440 | tf_op jit(solution)/shard_map/ppermute | solution.py:200
  41.5 2.5 %shard_map.58 = (bf16[64,2048]{1,0:T(8,128)(2,1)S(1)}, bf16[64,2048]{1,0:T(8,128)(2,1)S(1)}, f32[128,2048]{1,0:T(8,128)S(1)}, f32[128,2048]{1,0:T(8,128)S(1)}, f...) custom-call(bf16[512,512]{1,0:T(8,128)(2,1)S(1)} %fusion.1.qf_ref, ...), custom_call_target="tpu_custom_call" | custom-call | flops 4000000000 | bytes 15625000 | tf_op jit(solution)/shard_map/pallas_call | solution.py:234
  44.1 2.7 %collective-permute-start.19 = (bf16[64,2048]{1,0:T(8,128)(2,1)S(1)}, bf16[64,2048]{1,0:T(8,128)(2,1)S(1)}, u32[]{:S(2)}, u32[]{:S(2)}) collective-permute-start(bf16[64,2048]{1,0:T(8,128)(2,1)S(1)} %get-tuple-element.55), channel_id=1, source_target_pairs={{0,7},{1,0},{2,1},{3,2},{4,3},{5,4},{6,5},{7,6},{8,15},{9,8},{10,9... | collective-permute-start | bytes 786440 | tf_op jit(solution)/shard_map/ppermute | solution.py:200
  46.8 0.1 shard_map.61
  46.9 2.7 %collective-permute-start.27 = (bf16[64,2048]{1,0:T(8,128)(2,1)S(1)}, bf16[64,2048]{1,0:T(8,128)(2,1)S(1)}, u32[]{:S(2)}, u32[]{:S(2)}) collective-permute-start(bf16[64,2048]{1,0:T(8,128)(2,1)S(1)} %get-tuple-element.66), channel_id=1, source_target_pairs={{0,7},{1,0},{2,1},{3,2},{4,3},{5,4},{6,5},{7,6},{8,15},{9,8},{10,9... | collective-permute-start | bytes 786440 | tf_op jit(solution)/shard_map/ppermute | solution.py:200
  49.6 2.5 %collective-permute-done.18.from_left_ref = bf16[64,2048]{1,0:T(8,128)(2,1)S(1)} collective-permute-done((bf16[64,2048]{1,0:T(8,128)(2,1)S(1)}, bf16[64,2048]{1,0:T(8,128)(2,1)S(1)}, u32[]{:S(2)}, u32[]{:S(2)}) %collective-permute-start.18) | collective-permute-done | bytes 262176 | tf_op jit(solution)/shard_map/ppermute | solution.py:200
  52.1 0.1 shard_map.59
  52.3 2.7 %collective-permute-start.21 = (bf16[64,2048]{1,0:T(8,128)(2,1)S(1)}, bf16[64,2048]{1,0:T(8,128)(2,1)S(1)}, u32[]{:S(2)}, u32[]{:S(2)}) collective-permute-start(bf16[64,2048]{1,0:T(8,128)(2,1)S(1)} %get-tuple-element.57), channel_id=1, source_target_pairs={{0,7},{1,0},{2,1},{3,2},{4,3},{5,4},{6,5},{7,6},{8,15},{9,8},{10,9... | collective-permute-start | bytes 786440 | tf_op jit(solution)/shard_map/ppermute | solution.py:200
  54.9 2.8 %collective-permute-done.26.from_left_ref = bf16[64,2048]{1,0:T(8,128)(2,1)S(1)} collective-permute-done((bf16[64,2048]{1,0:T(8,128)(2,1)S(1)}, bf16[64,2048]{1,0:T(8,128)(2,1)S(1)}, u32[]{:S(2)}, u32[]{:S(2)}) %collective-permute-start.26) | collective-permute-done | bytes 262176 | tf_op jit(solution)/shard_map/ppermute | solution.py:200
  57.7 0.1 shard_map.62
  57.9 2.7 %collective-permute-start.29 = (bf16[64,2048]{1,0:T(8,128)(2,1)S(1)}, bf16[64,2048]{1,0:T(8,128)(2,1)S(1)}, u32[]{:S(2)}, u32[]{:S(2)}) collective-permute-start(bf16[64,2048]{1,0:T(8,128)(2,1)S(1)} %get-tuple-element.68), channel_id=1, source_target_pairs={{0,7},{1,0},{2,1},{3,2},{4,3},{5,4},{6,5},{7,6},{8,15},{9,8},{10,9... | collective-permute-start | bytes 786440 | tf_op jit(solution)/shard_map/ppermute | solution.py:200
  60.6 2.8 %collective-permute-done.20.from_left_ref = bf16[64,2048]{1,0:T(8,128)(2,1)S(1)} collective-permute-done((bf16[64,2048]{1,0:T(8,128)(2,1)S(1)}, bf16[64,2048]{1,0:T(8,128)(2,1)S(1)}, u32[]{:S(2)}, u32[]{:S(2)}) %collective-permute-start.20) | collective-permute-done | bytes 262176 | tf_op jit(solution)/shard_map/ppermute | solution.py:200
  63.3 0.1 shard_map.60
  63.4 0.3 collective-permute-start.22
  63.7 2.7 %collective-permute-start.23 = (bf16[64,2048]{1,0:T(8,128)(2,1)S(1)}, bf16[64,2048]{1,0:T(8,128)(2,1)S(1)}, u32[]{:S(2)}, u32[]{:S(2)}) collective-permute-start(bf16[64,2048]{1,0:T(8,128)(2,1)S(1)} %get-tuple-element.59), channel_id=1, source_target_pairs={{0,7},{1,0},{2,1},{3,2},{4,3},{5,4},{6,5},{7,6},{8,15},{9,8},{10,9... | collective-permute-start | bytes 786440 | tf_op jit(solution)/shard_map/ppermute | solution.py:200
  66.4 2.5 %collective-permute-done.28.from_left_ref = bf16[64,2048]{1,0:T(8,128)(2,1)S(1)} collective-permute-done((bf16[64,2048]{1,0:T(8,128)(2,1)S(1)}, bf16[64,2048]{1,0:T(8,128)(2,1)S(1)}, u32[]{:S(2)}, u32[]{:S(2)}) %collective-permute-start.28) | collective-permute-done | bytes 262176 | tf_op jit(solution)/shard_map/ppermute | solution.py:200
  69.1 2.7 %collective-permute-start.31 = (bf16[64,2048]{1,0:T(8,128)(2,1)S(1)}, bf16[64,2048]{1,0:T(8,128)(2,1)S(1)}, u32[]{:S(2)}, u32[]{:S(2)}) collective-permute-start(bf16[64,2048]{1,0:T(8,128)(2,1)S(1)} %get-tuple-element.70), channel_id=1, source_target_pairs={{0,7},{1,0},{2,1},{3,2},{4,3},{5,4},{6,5},{7,6},{8,15},{9,8},{10,9... | collective-permute-start | bytes 786440 | tf_op jit(solution)/shard_map/ppermute | solution.py:200
  71.8 2.8 %collective-permute-done.22.right0 = bf16[64,2048]{1,0:T(8,128)(2,1)S(1)} collective-permute-done((bf16[64,2048]{1,0:T(8,128)(2,1)S(1)}, bf16[64,2048]{1,0:T(8,128)(2,1)S(1)}, u32[]{:S(2)}, u32[]{:S(2)}) %collective-permute-start.22) | collective-permute-done | bytes 262176 | tf_op jit(solution)/shard_map/ppermute | solution.py:200
  74.6 5.6 %collective-permute-done.30.right1 = bf16[64,2048]{1,0:T(8,128)(2,1)S(1)} collective-permute-done((bf16[64,2048]{1,0:T(8,128)(2,1)S(1)}, bf16[64,2048]{1,0:T(8,128)(2,1)S(1)}, u32[]{:S(2)}, u32[]{:S(2)}) %collective-permute-start.30) | collective-permute-done | bytes 262176 | tf_op jit(solution)/shard_map/ppermute | solution.py:200
  80.2 0.9 %shard_map.64 = bf16[64,4096]{1,0:T(8,128)(2,1)} custom-call(f32[64,4096]{1,0:T(8,128)S(1)} %get-tuple-element.51.own_ref, bf16[64,2048]{1,0:T(8,128)(2,1)S(1)} %collective-permute-done.22.right0, bf16[64,2048]{1,0:T(8,128)(2,1)S(1)} %collective-permute-done.23.left1, bf16[64,2048]{1,0:T(8,128)(2,1)S(1)} %collective-permute-done.30.right1, ...), custom_call_target="tpu_custom_call" | custom-call | flops 100000000 | bytes 390625 | tf_op jit(solution)/shard_map/pallas_call | solution.py:253
  (35 shorter events, 0.7 us)
Async XLA Ops:
  0.0 5.6 %copy-start.1 = (s32[2,4,8]{2,1,0:T(4,128)S(1)}, s32[2,4,8]{2,1,0:T(4,128)}, u32[]{:S(2)}) copy-start(s32[2,4,8]{2,1,0:T(4,128)} %own_ref.1) | copy-start | bytes 772
  0.0 5.6 %collective-permute-start = (s32[2,4,8]{2,1,0:T(4,128)}, s32[2,4,8]{2,1,0:T(4,128)S(1)}, u32[]{:S(2)}, u32[]{:S(2)}) collective-permute-start(s32[2,4,8]{2,1,0:T(4,128)} %own_ref.1), channel_id=1, source_target_pairs={{0,8},{8,0},{16,24},{24,16},{32,40},{40,32},{48,56},{56,48},{1,9},... | collective-permute-start | bytes 776 | tf_op jit(solution)/shard_map/ppermute | solution.py:199
  6.1 23.0 %copy-start.2 = (bf16[512,512]{1,0:T(8,128)(2,1)S(1)}, bf16[512,512]{1,0:T(8,128)(2,1)}, u32[]{:S(2)}) copy-start(bf16[512,512]{1,0:T(8,128)(2,1)} %param.5) | copy-start | bytes 1572868
  6.1 7.2 %collective-permute-start.5 = (bf16[576,128]{1,0:T(8,128)(2,1)S(1)}, bf16[576,128]{1,0:T(8,128)(2,1)S(1)}, u32[]{:S(2)}, u32[]{:S(2)}) collective-permute-start(bf16[576,128]{1,0:T(8,128)(2,1)S(1)} %get-tuple-element.39.refs_4_), channel_id=1, source_target_pairs={{0,48},{8,200},{16,0},{24,216},{32,16},{40,232},{48,32},{56,248},{... | collective-permute-start | bytes 442376 | tf_op jit(solution)/shard_map/ppermute | solution.py:197
  6.9 6.5 %collective-permute-start.3 = (bf16[576,128]{1,0:T(8,128)(2,1)S(1)}, bf16[576,128]{1,0:T(8,128)(2,1)S(1)}, u32[]{:S(2)}, u32[]{:S(2)}) collective-permute-start(bf16[576,128]{1,0:T(8,128)(2,1)S(1)} %get-tuple-element.39.refs_4_), channel_id=1, source_target_pairs={{0,32},{8,136},{16,48},{24,152},{32,0},{40,168},{48,16},{56,184},{... | collective-permute-start | bytes 442376 | tf_op jit(solution)/shard_map/ppermute | solution.py:197
  7.4 6.9 %collective-permute-start.1 = (bf16[576,128]{1,0:T(8,128)(2,1)S(1)}, bf16[576,128]{1,0:T(8,128)(2,1)S(1)}, u32[]{:S(2)}, u32[]{:S(2)}) collective-permute-start(bf16[576,128]{1,0:T(8,128)(2,1)S(1)} %get-tuple-element.39.refs_4_), channel_id=1, source_target_pairs={{0,16},{8,72},{16,32},{24,88},{32,48},{40,104},{48,0},{56,120},{64... | collective-permute-start | bytes 442376 | tf_op jit(solution)/shard_map/ppermute | solution.py:197
  8.0 8.3 %collective-permute-start.10 = (bf16[576,128]{1,0:T(8,128)(2,1)S(1)}, bf16[576,128]{1,0:T(8,128)(2,1)S(1)}, u32[]{:S(2)}, u32[]{:S(2)}) collective-permute-start(bf16[576,128]{1,0:T(8,128)(2,1)S(1)} %get-tuple-element.40), channel_id=1, source_target_pairs={{0,200},{8,48},{16,216},{24,0},{32,232},{40,16},{48,248},{56,32},{... | collective-permute-start | bytes 442376 | tf_op jit(solution)/shard_map/ppermute | solution.py:197
  10.9 6.1 %collective-permute-start.9 = (bf16[576,128]{1,0:T(8,128)(2,1)S(1)}, bf16[576,128]{1,0:T(8,128)(2,1)S(1)}, u32[]{:S(2)}, u32[]{:S(2)}) collective-permute-start(bf16[576,128]{1,0:T(8,128)(2,1)S(1)} %get-tuple-element.40), channel_id=1, source_target_pairs={{0,136},{8,32},{16,152},{24,48},{32,168},{40,0},{48,184},{56,16},{... | collective-permute-start | bytes 442376 | tf_op jit(solution)/shard_map/ppermute | solution.py:197
  13.3 6.1 %collective-permute-start.8 = (bf16[576,128]{1,0:T(8,128)(2,1)S(1)}, bf16[576,128]{1,0:T(8,128)(2,1)S(1)}, u32[]{:S(2)}, u32[]{:S(2)}) collective-permute-start(bf16[576,128]{1,0:T(8,128)(2,1)S(1)} %get-tuple-element.40), channel_id=1, source_target_pairs={{0,72},{8,16},{16,88},{24,32},{32,104},{40,48},{48,120},{56,0},{64... | collective-permute-start | bytes 442376 | tf_op jit(solution)/shard_map/ppermute | solution.py:197
  13.4 5.9 %collective-permute-start.7 = (bf16[576,128]{1,0:T(8,128)(2,1)S(1)}, bf16[576,128]{1,0:T(8,128)(2,1)S(1)}, u32[]{:S(2)}, u32[]{:S(2)}) collective-permute-start(bf16[576,128]{1,0:T(8,128)(2,1)S(1)} %get-tuple-element.40), channel_id=1, source_target_pairs={{0,8},{8,0},{16,24},{24,16},{32,40},{40,32},{48,56},{56,48},{1,9},... | collective-permute-start | bytes 442376 | tf_op jit(solution)/shard_map/ppermute | solution.py:199
  14.3 5.1 %collective-permute-start.6 = (bf16[576,128]{1,0:T(8,128)(2,1)S(1)}, bf16[576,128]{1,0:T(8,128)(2,1)S(1)}, u32[]{:S(2)}, u32[]{:S(2)}) collective-permute-start(bf16[576,128]{1,0:T(8,128)(2,1)S(1)} %collective-permute-done.5.refs_10_), channel_id=1, source_target_pairs={{0,8},{8,0},{16,24},{24,16},{32,40},{40,32},{48,56},{56,48},{1,9},... | collective-permute-start | bytes 442376 | tf_op jit(solution)/shard_map/ppermute | solution.py:199
  16.4 3.0 %collective-permute-start.4 = (bf16[576,128]{1,0:T(8,128)(2,1)S(1)}, bf16[576,128]{1,0:T(8,128)(2,1)S(1)}, u32[]{:S(2)}, u32[]{:S(2)}) collective-permute-start(bf16[576,128]{1,0:T(8,128)(2,1)S(1)} %collective-permute-done.3.refs_8_), channel_id=1, source_target_pairs={{0,8},{8,0},{16,24},{24,16},{32,40},{40,32},{48,56},{56,48},{1,9},... | collective-permute-start | bytes 442376 | tf_op jit(solution)/shard_map/ppermute | solution.py:199
  17.0 2.4 %collective-permute-start.2 = (bf16[576,128]{1,0:T(8,128)(2,1)S(1)}, bf16[576,128]{1,0:T(8,128)(2,1)S(1)}, u32[]{:S(2)}, u32[]{:S(2)}) collective-permute-start(bf16[576,128]{1,0:T(8,128)(2,1)S(1)} %collective-permute-done.1.refs_6_), channel_id=1, source_target_pairs={{0,8},{8,0},{16,24},{24,16},{32,40},{40,32},{48,56},{56,48},{1,9},... | collective-permute-start | bytes 442376 | tf_op jit(solution)/shard_map/ppermute | solution.py:199
  19.4 15.0 %copy-start = (bf16[512,4096]{1,0:T(8,128)(2,1)S(1)}, bf16[512,4096]{1,0:T(8,128)(2,1)}, u32[]{:S(2)}) copy-start(bf16[512,4096]{1,0:T(8,128)(2,1)} %w_ref.3) | copy-start | bytes 12582916
  20.5 5.0 %collective-permute-start.11 = (bf16[576,128]{1,0:T(8,128)(2,1)S(1)}, bf16[576,128]{1,0:T(8,128)(2,1)S(1)}, u32[]{:S(2)}, u32[]{:S(2)}) collective-permute-start(bf16[576,128]{1,0:T(8,128)(2,1)S(1)} %get-tuple-element.42), channel_id=1, source_target_pairs={{0,192},{8,56},{16,208},{24,8},{32,224},{40,24},{48,240},{56,40},{... | collective-permute-start | bytes 442376 | tf_op jit(solution)/shard_map/ppermute | solution.py:197
  21.5 6.7 %collective-permute-start.12 = (bf16[576,128]{1,0:T(8,128)(2,1)S(1)}, bf16[576,128]{1,0:T(8,128)(2,1)S(1)}, u32[]{:S(2)}, u32[]{:S(2)}) collective-permute-start(bf16[576,128]{1,0:T(8,128)(2,1)S(1)} %get-tuple-element.43), channel_id=1, source_target_pairs={{0,128},{8,40},{16,144},{24,56},{32,160},{40,8},{48,176},{56,24},{... | collective-permute-start | bytes 442376 | tf_op jit(solution)/shard_map/ppermute | solution.py:197
  22.5 6.8 %collective-permute-start.13 = (bf16[576,128]{1,0:T(8,128)(2,1)S(1)}, bf16[576,128]{1,0:T(8,128)(2,1)S(1)}, u32[]{:S(2)}, u32[]{:S(2)}) collective-permute-start(bf16[576,128]{1,0:T(8,128)(2,1)S(1)} %get-tuple-element.44), channel_id=1, source_target_pairs={{0,64},{8,24},{16,80},{24,40},{32,96},{40,56},{48,112},{56,8},{64,... | collective-permute-start | bytes 442376 | tf_op jit(solution)/shard_map/ppermute | solution.py:197
  22.6 6.7 %collective-permute-start.14 = (bf16[576,128]{1,0:T(8,128)(2,1)S(1)}, bf16[576,128]{1,0:T(8,128)(2,1)S(1)}, u32[]{:S(2)}, u32[]{:S(2)}) collective-permute-start(bf16[576,128]{1,0:T(8,128)(2,1)S(1)} %get-tuple-element.45), channel_id=1, source_target_pairs={{0,8},{8,0},{16,24},{24,16},{32,40},{40,32},{48,56},{56,48},{1,9},... | collective-permute-start | bytes 442376 | tf_op jit(solution)/shard_map/ppermute | solution.py:199
  25.5 4.9 %collective-permute-start.15 = (bf16[576,128]{1,0:T(8,128)(2,1)S(1)}, bf16[576,128]{1,0:T(8,128)(2,1)S(1)}, u32[]{:S(2)}, u32[]{:S(2)}) collective-permute-start(bf16[576,128]{1,0:T(8,128)(2,1)S(1)} %get-tuple-element.46), channel_id=1, source_target_pairs={{0,200},{8,48},{16,216},{24,0},{32,232},{40,16},{48,248},{56,32},{... | collective-permute-start | bytes 442376 | tf_op jit(solution)/shard_map/ppermute | solution.py:197
  25.5 7.3 %collective-permute-start.16 = (bf16[576,128]{1,0:T(8,128)(2,1)S(1)}, bf16[576,128]{1,0:T(8,128)(2,1)S(1)}, u32[]{:S(2)}, u32[]{:S(2)}) collective-permute-start(bf16[576,128]{1,0:T(8,128)(2,1)S(1)} %get-tuple-element.47), channel_id=1, source_target_pairs={{0,136},{8,32},{16,152},{24,48},{32,168},{40,0},{48,184},{56,16},{... | collective-permute-start | bytes 442376 | tf_op jit(solution)/shard_map/ppermute | solution.py:197
  28.2 6.2 %collective-permute-start.17 = (bf16[576,128]{1,0:T(8,128)(2,1)S(1)}, bf16[576,128]{1,0:T(8,128)(2,1)S(1)}, u32[]{:S(2)}, u32[]{:S(2)}) collective-permute-start(bf16[576,128]{1,0:T(8,128)(2,1)S(1)} %get-tuple-element.48), channel_id=1, source_target_pairs={{0,72},{8,16},{16,88},{24,32},{32,104},{40,48},{48,120},{56,0},{64... | collective-permute-start | bytes 442376 | tf_op jit(solution)/shard_map/ppermute | solution.py:197
  35.9 10.8 %collective-permute-start.24 = (bf16[64,2048]{1,0:T(8,128)(2,1)S(1)}, bf16[64,2048]{1,0:T(8,128)(2,1)S(1)}, u32[]{:S(2)}, u32[]{:S(2)}) collective-permute-start(bf16[64,2048]{1,0:T(8,128)(2,1)S(1)} %get-tuple-element.63), channel_id=1, source_target_pairs={{0,1},{1,2},{2,3},{3,4},{4,5},{5,6},{6,7},{7,0},{8,9},{9,10},{10,1... | collective-permute-start | bytes 786440 | tf_op jit(solution)/shard_map/ppermute | solution.py:200
  37.6 9.2 %collective-permute-start.25 = (bf16[64,2048]{1,0:T(8,128)(2,1)S(1)}, bf16[64,2048]{1,0:T(8,128)(2,1)S(1)}, u32[]{:S(2)}, u32[]{:S(2)}) collective-permute-start(bf16[64,2048]{1,0:T(8,128)(2,1)S(1)} %get-tuple-element.64), channel_id=1, source_target_pairs={{0,7},{1,0},{2,1},{3,2},{4,3},{5,4},{6,5},{7,6},{8,15},{9,8},{10,9... | collective-permute-start | bytes 786440 | tf_op jit(solution)/shard_map/ppermute | solution.py:200
  44.0 8.1 %collective-permute-start.18 = (bf16[64,2048]{1,0:T(8,128)(2,1)S(1)}, bf16[64,2048]{1,0:T(8,128)(2,1)S(1)}, u32[]{:S(2)}, u32[]{:S(2)}) collective-permute-start(bf16[64,2048]{1,0:T(8,128)(2,1)S(1)} %get-tuple-element.54), channel_id=1, source_target_pairs={{0,1},{1,2},{2,3},{3,4},{4,5},{5,6},{6,7},{7,0},{8,9},{9,10},{10,1... | collective-permute-start | bytes 786440 | tf_op jit(solution)/shard_map/ppermute | solution.py:200
  44.1 8.0 %collective-permute-start.19 = (bf16[64,2048]{1,0:T(8,128)(2,1)S(1)}, bf16[64,2048]{1,0:T(8,128)(2,1)S(1)}, u32[]{:S(2)}, u32[]{:S(2)}) collective-permute-start(bf16[64,2048]{1,0:T(8,128)(2,1)S(1)} %get-tuple-element.55), channel_id=1, source_target_pairs={{0,7},{1,0},{2,1},{3,2},{4,3},{5,4},{6,5},{7,6},{8,15},{9,8},{10,9... | collective-permute-start | bytes 786440 | tf_op jit(solution)/shard_map/ppermute | solution.py:200
  46.9 10.9 %collective-permute-start.26 = (bf16[64,2048]{1,0:T(8,128)(2,1)S(1)}, bf16[64,2048]{1,0:T(8,128)(2,1)S(1)}, u32[]{:S(2)}, u32[]{:S(2)}) collective-permute-start(bf16[64,2048]{1,0:T(8,128)(2,1)S(1)} %get-tuple-element.65), channel_id=1, source_target_pairs={{0,1},{1,2},{2,3},{3,4},{4,5},{5,6},{6,7},{7,0},{8,9},{9,10},{10,1... | collective-permute-start | bytes 786440 | tf_op jit(solution)/shard_map/ppermute | solution.py:200
  46.9 10.8 %collective-permute-start.27 = (bf16[64,2048]{1,0:T(8,128)(2,1)S(1)}, bf16[64,2048]{1,0:T(8,128)(2,1)S(1)}, u32[]{:S(2)}, u32[]{:S(2)}) collective-permute-start(bf16[64,2048]{1,0:T(8,128)(2,1)S(1)} %get-tuple-element.66), channel_id=1, source_target_pairs={{0,7},{1,0},{2,1},{3,2},{4,3},{5,4},{6,5},{7,6},{8,15},{9,8},{10,9... | collective-permute-start | bytes 786440 | tf_op jit(solution)/shard_map/ppermute | solution.py:200
  52.2 11.1 %collective-permute-start.20 = (bf16[64,2048]{1,0:T(8,128)(2,1)S(1)}, bf16[64,2048]{1,0:T(8,128)(2,1)S(1)}, u32[]{:S(2)}, u32[]{:S(2)}) collective-permute-start(bf16[64,2048]{1,0:T(8,128)(2,1)S(1)} %get-tuple-element.56), channel_id=1, source_target_pairs={{0,1},{1,2},{2,3},{3,4},{4,5},{5,6},{6,7},{7,0},{8,9},{9,10},{10,1... | collective-permute-start | bytes 786440 | tf_op jit(solution)/shard_map/ppermute | solution.py:200
  52.3 11.1 %collective-permute-start.21 = (bf16[64,2048]{1,0:T(8,128)(2,1)S(1)}, bf16[64,2048]{1,0:T(8,128)(2,1)S(1)}, u32[]{:S(2)}, u32[]{:S(2)}) collective-permute-start(bf16[64,2048]{1,0:T(8,128)(2,1)S(1)} %get-tuple-element.57), channel_id=1, source_target_pairs={{0,7},{1,0},{2,1},{3,2},{4,3},{5,4},{6,5},{7,6},{8,15},{9,8},{10,9... | collective-permute-start | bytes 786440 | tf_op jit(solution)/shard_map/ppermute | solution.py:200
  57.8 11.1 %collective-permute-start.28 = (bf16[64,2048]{1,0:T(8,128)(2,1)S(1)}, bf16[64,2048]{1,0:T(8,128)(2,1)S(1)}, u32[]{:S(2)}, u32[]{:S(2)}) collective-permute-start(bf16[64,2048]{1,0:T(8,128)(2,1)S(1)} %get-tuple-element.67), channel_id=1, source_target_pairs={{0,1},{1,2},{2,3},{3,4},{4,5},{5,6},{6,7},{7,0},{8,9},{9,10},{10,1... | collective-permute-start | bytes 786440 | tf_op jit(solution)/shard_map/ppermute | solution.py:200
  57.9 11.1 %collective-permute-start.29 = (bf16[64,2048]{1,0:T(8,128)(2,1)S(1)}, bf16[64,2048]{1,0:T(8,128)(2,1)S(1)}, u32[]{:S(2)}, u32[]{:S(2)}) collective-permute-start(bf16[64,2048]{1,0:T(8,128)(2,1)S(1)} %get-tuple-element.68), channel_id=1, source_target_pairs={{0,7},{1,0},{2,1},{3,2},{4,3},{5,4},{6,5},{7,6},{8,15},{9,8},{10,9... | collective-permute-start | bytes 786440 | tf_op jit(solution)/shard_map/ppermute | solution.py:200
  63.4 11.1 %collective-permute-start.22 = (bf16[64,2048]{1,0:T(8,128)(2,1)S(1)}, bf16[64,2048]{1,0:T(8,128)(2,1)S(1)}, u32[]{:S(2)}, u32[]{:S(2)}) collective-permute-start(bf16[64,2048]{1,0:T(8,128)(2,1)S(1)} %get-tuple-element.58), channel_id=1, source_target_pairs={{0,1},{1,2},{2,3},{3,4},{4,5},{5,6},{6,7},{7,0},{8,9},{9,10},{10,1... | collective-permute-start | bytes 786440 | tf_op jit(solution)/shard_map/ppermute | solution.py:200
  63.7 10.8 %collective-permute-start.23 = (bf16[64,2048]{1,0:T(8,128)(2,1)S(1)}, bf16[64,2048]{1,0:T(8,128)(2,1)S(1)}, u32[]{:S(2)}, u32[]{:S(2)}) collective-permute-start(bf16[64,2048]{1,0:T(8,128)(2,1)S(1)} %get-tuple-element.59), channel_id=1, source_target_pairs={{0,7},{1,0},{2,1},{3,2},{4,3},{5,4},{6,5},{7,6},{8,15},{9,8},{10,9... | collective-permute-start | bytes 786440 | tf_op jit(solution)/shard_map/ppermute | solution.py:200
  69.0 11.1 %collective-permute-start.30 = (bf16[64,2048]{1,0:T(8,128)(2,1)S(1)}, bf16[64,2048]{1,0:T(8,128)(2,1)S(1)}, u32[]{:S(2)}, u32[]{:S(2)}) collective-permute-start(bf16[64,2048]{1,0:T(8,128)(2,1)S(1)} %get-tuple-element.69), channel_id=1, source_target_pairs={{0,1},{1,2},{2,3},{3,4},{4,5},{5,6},{6,7},{7,0},{8,9},{9,10},{10,1... | collective-permute-start | bytes 786440 | tf_op jit(solution)/shard_map/ppermute | solution.py:200
  69.1 11.1 %collective-permute-start.31 = (bf16[64,2048]{1,0:T(8,128)(2,1)S(1)}, bf16[64,2048]{1,0:T(8,128)(2,1)S(1)}, u32[]{:S(2)}, u32[]{:S(2)}) collective-permute-start(bf16[64,2048]{1,0:T(8,128)(2,1)S(1)} %get-tuple-element.70), channel_id=1, source_target_pairs={{0,7},{1,0},{2,1},{3,2},{4,3},{5,4},{6,5},{7,6},{8,15},{9,8},{10,9... | collective-permute-start | bytes 786440 | tf_op jit(solution)/shard_map/ppermute | solution.py:200
where the time goes:
time: 82 us; the launch traced here: 81.1 us
  starting transfers between devices  44.5 us (54%)
  waiting for transfers between devices  26.9 us (33%)
  Pallas kernels  6.85 us (8%)
  other arithmetic  2.67 us (3%)
    ppermute x14, starting transfers between devices, per_device(): lax.ppermute(a, 'gz', [(i, (i + d) % 8) for i in range(8)])  22.3 us
    ppermute x14, waiting for transfers between devices, per_device(): lax.ppermute(a, 'gz', [(i, (i + d) % 8) for i in range(8)])  19 us
    ppermute x12, starting transfers between devices, by_role(): return lax.ppermute(a, ('gx', 'gy'), pairs)  13 us
    ppermute x6, starting transfers between devices, per_device(): to_mate = lambda a: lax.ppermute(a, 'gy', [(i, i ^ 1) for i in range(8)])  9.19 us
    ppermute x12, waiting for transfers between devices, by_role(): return lax.ppermute(a, ('gx', 'gy'), pairs)  7.93 us
    pallas_call x1, Pallas kernels, per_device(): call(project_kernel, (piece, piece) + (term,) * 5 + (jax.ShapeDtypeStruct...  2.48 us
  transfers between devices with their start and end apart: 32, of which 12 were waited for; matrix products, arithmetic and copies ran while one was open for 3% of the time, Pallas kernels for 4%

commit v1 on v0

--- a/solution.py
+++ b/solution.py
@@ -7,8 +7,8 @@
 
 BLOCK = 256
 HD = 128
-UNIT = 144
-ROWS = 4 * UNIT
+STATES = 4 * HD
+ROWS = STATES + 16
 F32 = jnp.float32
 BF16 = jnp.bfloat16
 
@@ -29,8 +29,14 @@
 
 def high_and_low(total):
     high = total.astype(BF16).astype(F32)
+    return high, total - high
+
+
+def with_rows(tail, at, rows):
     row = lax.broadcasted_iota(jnp.int32, (16, HD), 0)
-    return jnp.where(row == 0, high, jnp.where(row == 1, total - high, 0.0)).astype(BF16)
+    for i, one in enumerate(rows):
+        tail = jnp.where(row == at + i, one, tail)
+    return tail
 
 
 def head_columns(h):
@@ -52,24 +58,28 @@
             listed = list_ref[b].astype(F32).astype(BF16)
             at = i * 8 + b * 4
             lists_ref[at : at + 4, :] = jnp.dot(listed, repeat, preferred_element_type=F32)
-    row = lax.broadcasted_iota(jnp.int32, (16, HD), 0)
     for u_ref, role in ((keep_ref, core), (send_ref, 1 - core)):
+        tail = jnp.zeros((16, HD), F32)
         for b in range(2):
             rows = pl.ds(b * BLOCK, BLOCK)
             for hh in range(2):
-                at = (b * 2 + hh) * UNIT
+                u = b * 2 + hh
                 columns = head_columns(2 * role + hh)
                 kf = kv_ref[rows, columns]
                 state = lax.dot_general(
-                    kv_ref[pl.ds((2 + b) * BLOCK, BLOCK), columns], kf, (((0,), (0,)), ((), ())), preferred_element_type=F32
+                    kv_ref[pl.ds((2 + b) * BLOCK, BLOCK), columns],
+                    kf,
+                    (((0,), (0,)), ((), ())),
+                    preferred_element_type=F32,
                 )
-                u_ref[at : at + HD, :] = state.astype(BF16)
-                tail = high_and_low(jnp.dot(ones, kf, preferred_element_type=F32))
+                u_ref[u * HD : (u + 1) * HD, :] = state.astype(BF16)
+                total = jnp.dot(ones, kf, preferred_element_type=F32)[:1]
+                tail = with_rows(tail, 2 * u, high_and_low(total))
                 if u_ref is keep_ref:
                     other = b * 4 + 2 * (1 - core) + hh
-                    tail = jnp.where(row == 2, lists_ref[pl.ds(8 + other, 1), :], tail.astype(F32))
-                    tail = jnp.where(row == 3, lists_ref[pl.ds(other, 1), :], tail).astype(BF16)
-                u_ref[at + HD : at + UNIT, :] = tail
+                    both = [lists_ref[pl.ds(8 * i + other, 1), :] for i in (1, 0)]
+                    tail = with_rows(tail, 8 + 2 * u, both)
+        u_ref[STATES:, :] = tail.astype(BF16)
 
 
 def key_blocks():
@@ -92,30 +102,37 @@
     row = lax.broadcasted_iota(jnp.int32, (256, 256), 0)
     col = lax.broadcasted_iota(jnp.int32, (256, 256), 1)
     same = jnp.where(lax.rem(row, 16) == lax.rem(col, 16), 1.0, 0.0)
-    blocks = [(d * 2 + c, b * 2 * UNIT) for d in range(4) for c in range(2) for b in range(2)]
+    blocks = [(d * 2 + c, b) for d in range(4) for c in range(2) for b in range(2)]
+    tile_row = lax.broadcasted_iota(jnp.int32, (16, HD), 0)
+    tails = [ref[STATES:, :].astype(F32) for ref in keys]
+    out_tails = [jnp.zeros((16, HD), F32)] * 8
     for hh in range(2):
         listed = []
-        for d in range(4):
-            for c in range(2):
-                for b in range(2):
-                    if d == 0:
-                        one = lists[0][pl.ds(c * 8 + b * 4 + 2 * core + hh, 1), :]
-                    else:
-                        at = (b * 2 + hh) * UNIT + HD
-                        one = lists[d][at : at + 16, :].astype(F32)[2 + c : 3 + c, :]
-                    listed.append(jnp.broadcast_to(one, (16, HD)))
+        for i, b in blocks:
+            if i < 2:
+                one = lists[0][pl.ds(i * 8 + b * 4 + 2 * core + hh, 1), :]
+            else:
+                at = 8 + 2 * (b * 2 + hh) + i % 2
+                one = lists[i // 2][STATES:, :].astype(F32)[at : at + 1, :]
+            listed.append(jnp.broadcast_to(one, (16, HD)))
         hit = jnp.where(jnp.concatenate(listed, axis=0) == kb, 1.0, 0.0).astype(BF16)
         mix = (jnp.dot(hit, spread, preferred_element_type=F32) * same).astype(BF16)
-        for g in range(9):
-            shift = hh * UNIT + g * 16
-            pieces = [keys[d][at + shift : at + shift + 16, :] for d, at in blocks]
+        for g in range(8):
+            shift = hh * HD + g * 16
+            pieces = [keys[i][b * 2 * HD + shift : b * 2 * HD + shift + 16, :] for i, b in blocks]
             summed = jnp.dot(mix, jnp.concatenate(pieces, axis=0), preferred_element_type=F32)
-            for q, (d, at) in enumerate(blocks):
-                piece = summed[q * 16 : q * 16 + 16, :]
-                if g == 8:
-                    outs[d][at + shift : at + shift + 16, :] = high_and_low(piece[0:1] + piece[1:2])
-                else:
-                    outs[d][at + shift : at + shift + 16, :] = piece.astype(BF16)
+            for q, (i, b) in enumerate(blocks):
+                at = b * 2 * HD + shift
+                outs[i][at : at + 16, :] = summed[q * 16 : q * 16 + 16, :].astype(BF16)
+        pieces = [
+            jnp.where(tile_row // 2 == b * 2 + hh, tails[i], 0.0).astype(BF16) for i, b in blocks
+        ]
+        summed = jnp.dot(mix, jnp.concatenate(pieces, axis=0), preferred_element_type=F32)
+        for q, (i, b) in enumerate(blocks):
+            total = jnp.sum(summed[q * 16 : q * 16 + 8, :], axis=0, keepdims=True)
+            out_tails[i] = with_rows(out_tails[i], 2 * (b * 2 + hh), high_and_low(total))
+    for out_ref, tail in zip(outs, out_tails):
+        out_ref[STATES:, :] = tail.astype(BF16)
 
 
 def attend(q_ref, state_ref, sums_ref, at, rows, columns):
@@ -131,12 +148,12 @@
     core, far = lax.rem(lax.axis_index("gy"), 2), lax.rem(lax.axis_index("gz") + 4, 8)
     for side in range(2):
         role = core if side == 0 else 1 - core
+        tail = sum(p[STATES:, :].astype(F32) for p in parts[side])
         for u in range(4):
-            at = u * UNIT
-            total = sum(p[at : at + UNIT, :].astype(F32) for p in parts[side])
+            total = sum(p[u * HD : (u + 1) * HD, :].astype(F32) for p in parts[side])
             to = pl.ds(pl.multiple_of((u // 2 * 4 + 2 * role + u % 2) * HD, HD), HD)
-            state_ref[to, :] = total[:HD].astype(BF16)
-            key_sum = total[HD : HD + 1] + total[HD + 1 : HD + 2]
+            state_ref[to, :] = total.astype(BF16)
+            key_sum = tail[2 * u : 2 * u + 1] + tail[2 * u + 1 : 2 * u + 2]
             sums_ref[to, :] = jnp.broadcast_to(key_sum, (HD, HD)).astype(BF16)
     for h in range(4):
         at = pl.ds(pl.multiple_of((far // 4 * 4 + h) * HD, HD), HD)
@@ -178,12 +195,22 @@
     left_ref[...] = (term_ref[64:, :] + from_right_ref[...].astype(F32)).astype(BF16)
 
 
-def last_kernel(own_ref, right0, left1, right1, left0, out_ref):
-    half = own_ref.shape[1] // 2
+def last_kernel(own_ref, right0, left1, right1, left0, out_hbm, out_ref, sems):
+    half, step = own_ref.shape[1] // 2, own_ref.shape[1] // 4
+    copies = []
     for i, (a, b) in enumerate(((right0, left0), (right1, left1))):
-        out_ref[:, i * half : (i + 1) * half] = (
-            own_ref[:, i * half : (i + 1) * half] + a[...].astype(F32) + b[...].astype(F32)
-        ).astype(BF16)
+        for c in range(0, half, step):
+            cols = slice(i * half + c, i * half + c + step)
+            out_ref[:, cols] = (
+                own_ref[:, cols] + a[:, c : c + step].astype(F32) + b[:, c : c + step].astype(F32)
+            ).astype(BF16)
+            to = pl.ds(i * half + c, step)
+            copies.append(
+                pltpu.make_async_copy(out_ref.at[:, to], out_hbm.at[:, to], sems.at[len(copies)])
+            )
+            copies[-1].start()
+    for copy in copies:
+        copy.wait()
 
 
 def per_device(queries, key_rows, values, tile_list, out_weight):
@@ -205,12 +232,17 @@
         states_kernel, (unit, unit, jax.ShapeDtypeStruct((16, HD), F32)), 10**9, 8
     )(kv, tile_list, to_mate(tile_list))
     keys = {(0, 0): keep}
-    for d in (2, 1, 3):
-        keys[d, 0] = by_role(keep, d, "yx")
-        keys[d, 1] = by_role(send, d, "xy", cross=True)
+    keys[1, 0] = by_role(keep, 1, "yx")
+    keys[3, 1] = by_role(send, 3, "xy", cross=True)
+    keys[3, 0] = by_role(keep, 3, "yx")
+    keys[1, 1] = by_role(send, 1, "xy", cross=True)
+    keys[2, 0] = by_role(keys[1, 0], 1, "yx")
+    keys[2, 1] = by_role(keys[3, 1], 3, "yx")
     keys[0, 1] = to_mate(send)
 
-    lists = [lists] + [to_mate(keys[d, 0]) for d in (1, 2, 3)]
+    lists = [lists]
+    for d in (1, 2, 3):
+        lists.append(to_mate(keys[d, 0]))
     order = [(d, c) for d in range(4) for c in range(2)]
     parts = call(partial_kernel, (unit,) * 8, 10**9, 16)(*lists, *(keys[i] for i in order))
     parts = dict(zip(order, parts))
@@ -250,9 +282,15 @@
     right1, left0 = hop(f2, right1, left0)
     right0, left1 = hop(e1, right0, left1)
     right1, left0 = hop(f1, right1, left0)
-    return call(last_kernel, jax.ShapeDtypeStruct((64, 2 * half), BF16), 10**8, 8)(
-        own, right0, left1, right1, left0
-    )
+    return pl.pallas_call(
+        last_kernel,
+        out_shape=jax.ShapeDtypeStruct((64, 2 * half), BF16),
+        out_specs=pl.BlockSpec(memory_space=pltpu.HBM),
+        scratch_shapes=[pltpu.VMEM((64, 2 * half), BF16), pltpu.SemaphoreType.DMA((4,))],
+        compiler_params=pltpu.CompilerParams(vmem_limit_bytes=8 << 20),
+        cost_estimate=pl.CostEstimate(flops=10**8, bytes_accessed=10**6, transcendentals=0),
+        name="last",
+    )(own, right0, left1, right1, left0)
 
 
 def solution(mesh):

time: 82 us -> 82.2 us (level)
  waiting for transfers between devices: 26.9 us -> 28.3 us
    ppermute x12, starting transfers between devices: 13 us -> 15.8 us  [by_role(): return lax.ppermute(a, ('gx', 'gy'), pairs)]
    ppermute x6, starting transfers between devices: 9.19 us -> 6.82 us  [per_device(): to_mate = lambda a: lax.ppermute(a, 'gy', [(i, i ^ 1) for i in range(8)])]
    ppermute x14, starting transfers between devices: 22.3 us -> 21.2 us  [per_device(): lax.ppermute(a, 'gz', [(i, (i + d) % 8) for i in range(8)])]
    ppermute x14, waiting for transfers between devices: 19 us -> 19.8 us  [per_device(): lax.ppermute(a, 'gz', [(i, (i + d) % 8) for i in range(8)])]
  transfers between devices with their start and end apart: 32 -> 32, of which waited for: 12 -> 14; matrix products, arithmetic and copies ran while one was open for 3% -> 3% of each run, Pallas kernels for 4% -> 4%
where the time goes in v1:
time: 82.2 us; the launch traced here: 82 us
  starting transfers between devices  43.8 us (53%)
  waiting for transfers between devices  28.3 us (34%)
  Pallas kernels  6.75 us (8%)
  other arithmetic  2.67 us (3%)
    ppermute x14, starting transfers between devices, per_device(): lax.ppermute(a, 'gz', [(i, (i + d) % 8) for i in range(8)])  21.2 us
    ppermute x14, waiting for transfers between devices, per_device(): lax.ppermute(a, 'gz', [(i, (i + d) % 8) for i in range(8)])  19.8 us
    ppermute x12, starting transfers between devices, by_role(): return lax.ppermute(a, ('gx', 'gy'), pairs)  15.8 us
    ppermute x12, waiting for transfers between devices, by_role(): return lax.ppermute(a, ('gx', 'gy'), pairs)  7.78 us
    ppermute x6, starting transfers between devices, per_device(): to_mate = lambda a: lax.ppermute(a, 'gy', [(i, i ^ 1) for i in range(8)])  6.82 us
    pallas_call x1, Pallas kernels, per_device(): call(project_kernel, (piece, piece) + (term,) * 5 + (jax.ShapeDtypeStruct...  2.48 us
  transfers between devices with their start and end apart: 32, of which 14 were waited for; matrix products, arithmetic and copies ran while one was open for 3% of the time, Pallas kernels for 4%

profile of v1, /device:TPU:1, one launch (start us, length us, event | category | flops | bytes accessed | tf_op | source)
XLA Modules:
  0.0 82.0 jit_solution(6877907591662193831)
XLA Ops:
  0.0 3.2 %collective-permute-start = (s32[2,4,8]{2,1,0:T(4,128)}, s32[2,4,8]{2,1,0:T(4,128)S(1)}, u32[]{:S(2)}, u32[]{:S(2)}) collective-permute-start(s32[2,4,8]{2,1,0:T(4,128)} %own_ref.1), channel_id=1, source_target_pairs={{0,8},{8,0},{16,24},{24,16},{32,40},{40,32},{48,56},{56,48},{1,9},... | collective-permute-start | bytes 776 | tf_op jit(solution)/shard_map/ppermute | solution.py:226
  3.2 1.3 %fusion.4 = bf16[512,512]{1,0:T(8,128)(2,1)S(1)} fusion(bf16[512,512]{1,0:T(8,128)(2,1)} %param.6), kind=kLoop, calls=%fused_computation.10 | loop fusion | flops 1572864 | bytes 1048576 | tf_op jit(solution)/shard_map/convert_element_type | solution.py:27
  4.5 1.1 %pad_maximum_fusion.kv_ref = bf16[1024,512]{1,0:T(8,128)(2,1)S(1)} fusion(bf16[512,512]{1,0:T(8,128)(2,1)} %param.7, bf16[512,512]{1,0:T(8,128)(2,1)S(1)} %fusion.4), kind=kLoop, calls=%fused_computation.12 | loop fusion | flops 2097152 | bytes 2097152 | tf_op jit(solution)/shard_map/concatenate | solution.py:230
  5.6 0.4 shard_map.55
  6.2 2.7 %collective-permute-start.5 = (bf16[528,128]{1,0:T(8,128)(2,1)S(1)}, bf16[528,128]{1,0:T(8,128)(2,1)S(1)}, u32[]{:S(2)}, u32[]{:S(2)}) collective-permute-start(bf16[528,128]{1,0:T(8,128)(2,1)S(1)} %get-tuple-element.39.refs_4_), channel_id=1, source_target_pairs={{0,48},{8,200},{16,0},{24,216},{32,16},{40,232},{48,32},{56,248},{... | collective-permute-start | bytes 405512 | tf_op jit(solution)/shard_map/ppermute | solution.py:224
  8.8 0.3 collective-permute-start.9
  9.1 0.9 %collective-permute-start.8 = (bf16[528,128]{1,0:T(8,128)(2,1)S(1)}, bf16[528,128]{1,0:T(8,128)(2,1)S(1)}, u32[]{:S(2)}, u32[]{:S(2)}) collective-permute-start(bf16[528,128]{1,0:T(8,128)(2,1)S(1)} %get-tuple-element.40), channel_id=1, source_target_pairs={{0,72},{8,16},{16,88},{24,32},{32,104},{40,48},{48,120},{56,0},{64... | collective-permute-start | bytes 405512 | tf_op jit(solution)/shard_map/ppermute | solution.py:224
  10.0 1.6 %collective-permute-done.1.refs_6_ = bf16[528,128]{1,0:T(8,128)(2,1)S(1)} collective-permute-done((bf16[528,128]{1,0:T(8,128)(2,1)S(1)}, bf16[528,128]{1,0:T(8,128)(2,1)S(1)}, u32[]{:S(2)}, u32[]{:S(2)}) %collective-permute-start.1) | collective-permute-done | bytes 135200 | tf_op jit(solution)/shard_map/ppermute | solution.py:224
  11.5 0.9 %collective-permute-start.7 = (bf16[528,128]{1,0:T(8,128)(2,1)S(1)}, bf16[528,128]{1,0:T(8,128)(2,1)S(1)}, u32[]{:S(2)}, u32[]{:S(2)}) collective-permute-start(bf16[528,128]{1,0:T(8,128)(2,1)S(1)} %get-tuple-element.40), channel_id=1, source_target_pairs={{0,8},{8,0},{16,24},{24,16},{32,40},{40,32},{48,56},{56,48},{1,9},... | collective-permute-start | bytes 405512 | tf_op jit(solution)/shard_map/ppermute | solution.py:226
  12.4 0.5 collective-permute-start.2
  12.9 0.7 collective-permute-done.9.refs_11_
  13.6 0.3 collective-permute-start.6
  13.8 0.9 %collective-permute-done.8.refs_7_ = bf16[528,128]{1,0:T(8,128)(2,1)S(1)} collective-permute-done((bf16[528,128]{1,0:T(8,128)(2,1)S(1)}, bf16[528,128]{1,0:T(8,128)(2,1)S(1)}, u32[]{:S(2)}, u32[]{:S(2)}) %collective-permute-start.8) | collective-permute-done | bytes 135200 | tf_op jit(solution)/shard_map/ppermute | solution.py:224
  14.7 2.1 %collective-permute-start.10 = (bf16[528,128]{1,0:T(8,128)(2,1)S(1)}, bf16[528,128]{1,0:T(8,128)(2,1)S(1)}, u32[]{:S(2)}, u32[]{:S(2)}) collective-permute-start(bf16[528,128]{1,0:T(8,128)(2,1)S(1)} %collective-permute-done.9.refs_11_), channel_id=1, source_target_pairs={{0,48},{8,200},{16,0},{24,216},{32,16},{40,232},{48,32},{56,248},{... | collective-permute-start | bytes 405512 | tf_op jit(solution)/shard_map/ppermute | solution.py:224
  16.9 1.7 %collective-permute-start.4 = (bf16[528,128]{1,0:T(8,128)(2,1)S(1)}, bf16[528,128]{1,0:T(8,128)(2,1)S(1)}, u32[]{:S(2)}, u32[]{:S(2)}) collective-permute-start(bf16[528,128]{1,0:T(8,128)(2,1)S(1)} %collective-permute-done.3.refs_8_), channel_id=1, source_target_pairs={{0,8},{8,0},{16,24},{24,16},{32,40},{40,32},{48,56},{56,48},{1,9},... | collective-permute-start | bytes 405512 | tf_op jit(solution)/shard_map/ppermute | solution.py:226
  18.6 0.3 collective-permute-done.10.refs_9_
  18.9 0.7 collective-permute-done.4.refs_2_
  19.6 1.1 %shard_map.56 = (bf16[528,128]{1,0:T(8,128)(2,1)S(1)}, bf16[528,128]{1,0:T(8,128)(2,1)S(1)}, bf16[528,128]{1,0:T(8,128)(2,1)S(1)}, bf16[528,128]{1,0:T(8,128)(2,...) custom-call(f32[16,128]{1,0:T(8,128)S(1)} %get-tuple-element.38.refs, ...), custom_call_target="tpu_custom_call" | custom-call | flops 1000000000 | bytes 3906250 | tf_op jit(solution)/shard_map/pallas_call | solution.py:247
  20.7 0.7 collective-permute-start.11
  21.4 3.2 %collective-permute-start.12 = (bf16[528,128]{1,0:T(8,128)(2,1)S(1)}, bf16[528,128]{1,0:T(8,128)(2,1)S(1)}, u32[]{:S(2)}, u32[]{:S(2)}) collective-permute-start(bf16[528,128]{1,0:T(8,128)(2,1)S(1)} %get-tuple-element.43), channel_id=1, source_target_pairs={{0,128},{8,40},{16,144},{24,56},{32,160},{40,8},{48,176},{56,24},{... | collective-permute-start | bytes 405512 | tf_op jit(solution)/shard_map/ppermute | solution.py:224
  24.6 0.3 collective-permute-start.14
  24.9 2.8 %collective-permute-start.15 = (bf16[528,128]{1,0:T(8,128)(2,1)S(1)}, bf16[528,128]{1,0:T(8,128)(2,1)S(1)}, u32[]{:S(2)}, u32[]{:S(2)}) collective-permute-start(bf16[528,128]{1,0:T(8,128)(2,1)S(1)} %get-tuple-element.46), channel_id=1, source_target_pairs={{0,200},{8,48},{16,216},{24,0},{32,232},{40,16},{48,248},{56,32},{... | collective-permute-start | bytes 405512 | tf_op jit(solution)/shard_map/ppermute | solution.py:224
  27.7 0.8 collective-permute-start.16
  28.5 2.2 %collective-permute-start.17 = (bf16[528,128]{1,0:T(8,128)(2,1)S(1)}, bf16[528,128]{1,0:T(8,128)(2,1)S(1)}, u32[]{:S(2)}, u32[]{:S(2)}) collective-permute-start(bf16[528,128]{1,0:T(8,128)(2,1)S(1)} %get-tuple-element.48), channel_id=1, source_target_pairs={{0,72},{8,16},{16,88},{24,32},{32,104},{40,48},{48,120},{56,0},{64... | collective-permute-start | bytes 405512 | tf_op jit(solution)/shard_map/ppermute | solution.py:224
  30.7 0.3 fusion.1.qf_ref
  31.0 2.8 %collective-permute-done.16.refs_6_ = bf16[528,128]{1,0:T(8,128)(2,1)S(1)} collective-permute-done((bf16[528,128]{1,0:T(8,128)(2,1)S(1)}, bf16[528,128]{1,0:T(8,128)(2,1)S(1)}, u32[]{:S(2)}, u32[]{:S(2)}) %collective-permute-start.16) | collective-permute-done | bytes 135200 | tf_op jit(solution)/shard_map/ppermute | solution.py:224
  33.8 1.6 %collective-permute-done.17.refs_7_ = bf16[528,128]{1,0:T(8,128)(2,1)S(1)} collective-permute-done((bf16[528,128]{1,0:T(8,128)(2,1)S(1)}, bf16[528,128]{1,0:T(8,128)(2,1)S(1)}, u32[]{:S(2)}, u32[]{:S(2)}) %collective-permute-start.17) | collective-permute-done | bytes 135200 | tf_op jit(solution)/shard_map/ppermute | solution.py:224
  35.4 1.5 %shard_map.57 = (bf16[64,2048]{1,0:T(8,128)(2,1)S(1)}, bf16[64,2048]{1,0:T(8,128)(2,1)S(1)}, bf16[1024,128]{1,0:T(8,128)(2,1)S(1)}, bf16[1024,128]{1,0:T(8,128)(2,1)S(1)}, bf16[64,512]{1,0:T(8,128)(2,1)}) custom-call(bf16[512,512]{1,0:T(8,128)(2,1)S(1)} %fusion.1.qf_ref, bf16[512,4096]{1,0:T(8,128)(2,1)S(1)} %copy-done, ...), custom_call_target="tpu_custom_call" | custom-call | flops 1000000000 | bytes 3906250 | tf_op jit(solution)/shard_map/pallas_call | solution.py:258
  36.9 0.8 collective-permute-start.24
  37.6 3.9 %collective-permute-start.25 = (bf16[64,2048]{1,0:T(8,128)(2,1)S(1)}, bf16[64,2048]{1,0:T(8,128)(2,1)S(1)}, u32[]{:S(2)}, u32[]{:S(2)}) collective-permute-start(bf16[64,2048]{1,0:T(8,128)(2,1)S(1)} %get-tuple-element.64), channel_id=1, source_target_pairs={{0,7},{1,0},{2,1},{3,2},{4,3},{5,4},{6,5},{7,6},{8,15},{9,8},{10,9... | collective-permute-start | bytes 786440 | tf_op jit(solution)/shard_map/ppermute | solution.py:227
  41.6 2.5 %shard_map.58 = (bf16[64,2048]{1,0:T(8,128)(2,1)S(1)}, bf16[64,2048]{1,0:T(8,128)(2,1)S(1)}, f32[128,2048]{1,0:T(8,128)S(1)}, f32[128,2048]{1,0:T(8,128)S(1)}, f...) custom-call(bf16[512,512]{1,0:T(8,128)(2,1)S(1)} %fusion.1.qf_ref, ...), custom_call_target="tpu_custom_call" | custom-call | flops 4000000000 | bytes 15625000 | tf_op jit(solution)/shard_map/pallas_call | solution.py:266
  44.1 2.7 %collective-permute-start.19 = (bf16[64,2048]{1,0:T(8,128)(2,1)S(1)}, bf16[64,2048]{1,0:T(8,128)(2,1)S(1)}, u32[]{:S(2)}, u32[]{:S(2)}) collective-permute-start(bf16[64,2048]{1,0:T(8,128)(2,1)S(1)} %get-tuple-element.55), channel_id=1, source_target_pairs={{0,7},{1,0},{2,1},{3,2},{4,3},{5,4},{6,5},{7,6},{8,15},{9,8},{10,9... | collective-permute-start | bytes 786440 | tf_op jit(solution)/shard_map/ppermute | solution.py:227
  46.8 0.6 collective-permute-done.24.from_left_ref
  47.4 0.1 shard_map.61
  47.6 2.7 %collective-permute-start.27 = (bf16[64,2048]{1,0:T(8,128)(2,1)S(1)}, bf16[64,2048]{1,0:T(8,128)(2,1)S(1)}, u32[]{:S(2)}, u32[]{:S(2)}) collective-permute-start(bf16[64,2048]{1,0:T(8,128)(2,1)S(1)} %get-tuple-element.66), channel_id=1, source_target_pairs={{0,7},{1,0},{2,1},{3,2},{4,3},{5,4},{6,5},{7,6},{8,15},{9,8},{10,9... | collective-permute-start | bytes 786440 | tf_op jit(solution)/shard_map/ppermute | solution.py:227
  50.2 2.6 %collective-permute-done.18.from_left_ref = bf16[64,2048]{1,0:T(8,128)(2,1)S(1)} collective-permute-done((bf16[64,2048]{1,0:T(8,128)(2,1)S(1)}, bf16[64,2048]{1,0:T(8,128)(2,1)S(1)}, u32[]{:S(2)}, u32[]{:S(2)}) %collective-permute-start.18) | collective-permute-done | bytes 262176 | tf_op jit(solution)/shard_map/ppermute | solution.py:227
  52.8 0.1 shard_map.59
  53.0 2.7 %collective-permute-start.21 = (bf16[64,2048]{1,0:T(8,128)(2,1)S(1)}, bf16[64,2048]{1,0:T(8,128)(2,1)S(1)}, u32[]{:S(2)}, u32[]{:S(2)}) collective-permute-start(bf16[64,2048]{1,0:T(8,128)(2,1)S(1)} %get-tuple-element.57), channel_id=1, source_target_pairs={{0,7},{1,0},{2,1},{3,2},{4,3},{5,4},{6,5},{7,6},{8,15},{9,8},{10,9... | collective-permute-start | bytes 786440 | tf_op jit(solution)/shard_map/ppermute | solution.py:227
  55.7 2.8 %collective-permute-done.26.from_left_ref = bf16[64,2048]{1,0:T(8,128)(2,1)S(1)} collective-permute-done((bf16[64,2048]{1,0:T(8,128)(2,1)S(1)}, bf16[64,2048]{1,0:T(8,128)(2,1)S(1)}, u32[]{:S(2)}, u32[]{:S(2)}) %collective-permute-start.26) | collective-permute-done | bytes 262176 | tf_op jit(solution)/shard_map/ppermute | solution.py:227
  58.4 0.1 shard_map.62
  58.6 2.7 %collective-permute-start.29 = (bf16[64,2048]{1,0:T(8,128)(2,1)S(1)}, bf16[64,2048]{1,0:T(8,128)(2,1)S(1)}, u32[]{:S(2)}, u32[]{:S(2)}) collective-permute-start(bf16[64,2048]{1,0:T(8,128)(2,1)S(1)} %get-tuple-element.68), channel_id=1, source_target_pairs={{0,7},{1,0},{2,1},{3,2},{4,3},{5,4},{6,5},{7,6},{8,15},{9,8},{10,9... | collective-permute-start | bytes 786440 | tf_op jit(solution)/shard_map/ppermute | solution.py:227
  61.3 2.7 %collective-permute-done.20.from_left_ref = bf16[64,2048]{1,0:T(8,128)(2,1)S(1)} collective-permute-done((bf16[64,2048]{1,0:T(8,128)(2,1)S(1)}, bf16[64,2048]{1,0:T(8,128)(2,1)S(1)}, u32[]{:S(2)}, u32[]{:S(2)}) %collective-permute-start.20) | collective-permute-done | bytes 262176 | tf_op jit(solution)/shard_map/ppermute | solution.py:227
  64.3 2.7 %collective-permute-start.23 = (bf16[64,2048]{1,0:T(8,128)(2,1)S(1)}, bf16[64,2048]{1,0:T(8,128)(2,1)S(1)}, u32[]{:S(2)}, u32[]{:S(2)}) collective-permute-start(bf16[64,2048]{1,0:T(8,128)(2,1)S(1)} %get-tuple-element.59), channel_id=1, source_target_pairs={{0,7},{1,0},{2,1},{3,2},{4,3},{5,4},{6,5},{7,6},{8,15},{9,8},{10,9... | collective-permute-start | bytes 786440 | tf_op jit(solution)/shard_map/ppermute | solution.py:227
  66.9 2.8 %collective-permute-done.28.from_left_ref = bf16[64,2048]{1,0:T(8,128)(2,1)S(1)} collective-permute-done((bf16[64,2048]{1,0:T(8,128)(2,1)S(1)}, bf16[64,2048]{1,0:T(8,128)(2,1)S(1)}, u32[]{:S(2)}, u32[]{:S(2)}) %collective-permute-start.28) | collective-permute-done | bytes 262176 | tf_op jit(solution)/shard_map/ppermute | solution.py:227
  69.9 2.7 %collective-permute-start.31 = (bf16[64,2048]{1,0:T(8,128)(2,1)S(1)}, bf16[64,2048]{1,0:T(8,128)(2,1)S(1)}, u32[]{:S(2)}, u32[]{:S(2)}) collective-permute-start(bf16[64,2048]{1,0:T(8,128)(2,1)S(1)} %get-tuple-element.70), channel_id=1, source_target_pairs={{0,7},{1,0},{2,1},{3,2},{4,3},{5,4},{6,5},{7,6},{8,15},{9,8},{10,9... | collective-permute-start | bytes 786440 | tf_op jit(solution)/shard_map/ppermute | solution.py:227
  72.5 2.8 %collective-permute-done.22.right0 = bf16[64,2048]{1,0:T(8,128)(2,1)S(1)} collective-permute-done((bf16[64,2048]{1,0:T(8,128)(2,1)S(1)}, bf16[64,2048]{1,0:T(8,128)(2,1)S(1)}, u32[]{:S(2)}, u32[]{:S(2)}) %collective-permute-start.22) | collective-permute-done | bytes 262176 | tf_op jit(solution)/shard_map/ppermute | solution.py:227
  75.3 5.6 %collective-permute-done.30.right1 = bf16[64,2048]{1,0:T(8,128)(2,1)S(1)} collective-permute-done((bf16[64,2048]{1,0:T(8,128)(2,1)S(1)}, bf16[64,2048]{1,0:T(8,128)(2,1)S(1)}, u32[]{:S(2)}, u32[]{:S(2)}) %collective-permute-start.30) | collective-permute-done | bytes 262176 | tf_op jit(solution)/shard_map/ppermute | solution.py:227
  80.9 0.9 %last.1 = bf16[64,4096]{1,0:T(8,128)(2,1)} custom-call(f32[64,4096]{1,0:T(8,128)S(1)} %get-tuple-element.51.own_ref, bf16[64,2048]{1,0:T(8,128)(2,1)S(1)} %collective-permute-done.22.right0, bf16[64,2048]{1,0:T(8,128)(2,1)S(1)} %collective-permute-done.23.left1, bf16[64,2048]{1,0:T(8,128)(2,1)S(1)} %collective-permute-done.30.right1, ...), custom_call_target="tpu_custom_call" | custom-call | flops 100000000 | bytes 1000000 | tf_op jit(solution)/shard_map/last/pallas_call | solution.py:285
  (35 shorter events, 0.8 us)
Async XLA Ops:
  0.0 5.6 %copy-start.1 = (s32[2,4,8]{2,1,0:T(4,128)S(1)}, s32[2,4,8]{2,1,0:T(4,128)}, u32[]{:S(2)}) copy-start(s32[2,4,8]{2,1,0:T(4,128)} %own_ref.1) | copy-start | bytes 772
  0.0 5.6 %collective-permute-start = (s32[2,4,8]{2,1,0:T(4,128)}, s32[2,4,8]{2,1,0:T(4,128)S(1)}, u32[]{:S(2)}, u32[]{:S(2)}) collective-permute-start(s32[2,4,8]{2,1,0:T(4,128)} %own_ref.1), channel_id=1, source_target_pairs={{0,8},{8,0},{16,24},{24,16},{32,40},{40,32},{48,56},{56,48},{1,9},... | collective-permute-start | bytes 776 | tf_op jit(solution)/shard_map/ppermute | solution.py:226
  6.1 24.6 %copy-start.2 = (bf16[512,512]{1,0:T(8,128)(2,1)S(1)}, bf16[512,512]{1,0:T(8,128)(2,1)}, u32[]{:S(2)}) copy-start(bf16[512,512]{1,0:T(8,128)(2,1)} %param.5) | copy-start | bytes 1572868
  6.1 5.4 %collective-permute-start.1 = (bf16[528,128]{1,0:T(8,128)(2,1)S(1)}, bf16[528,128]{1,0:T(8,128)(2,1)S(1)}, u32[]{:S(2)}, u32[]{:S(2)}) collective-permute-start(bf16[528,128]{1,0:T(8,128)(2,1)S(1)} %get-tuple-element.39.refs_4_), channel_id=1, source_target_pairs={{0,16},{8,72},{16,32},{24,88},{32,48},{40,104},{48,0},{56,120},{64... | collective-permute-start | bytes 405512 | tf_op jit(solution)/shard_map/ppermute | solution.py:224
  6.2 6.2 %collective-permute-start.5 = (bf16[528,128]{1,0:T(8,128)(2,1)S(1)}, bf16[528,128]{1,0:T(8,128)(2,1)S(1)}, u32[]{:S(2)}, u32[]{:S(2)}) collective-permute-start(bf16[528,128]{1,0:T(8,128)(2,1)S(1)} %get-tuple-element.39.refs_4_), channel_id=1, source_target_pairs={{0,48},{8,200},{16,0},{24,216},{32,16},{40,232},{48,32},{56,248},{... | collective-permute-start | bytes 405512 | tf_op jit(solution)/shard_map/ppermute | solution.py:224
  8.8 4.7 %collective-permute-start.9 = (bf16[528,128]{1,0:T(8,128)(2,1)S(1)}, bf16[528,128]{1,0:T(8,128)(2,1)S(1)}, u32[]{:S(2)}, u32[]{:S(2)}) collective-permute-start(bf16[528,128]{1,0:T(8,128)(2,1)S(1)} %get-tuple-element.40), channel_id=1, source_target_pairs={{0,200},{8,48},{16,216},{24,0},{32,232},{40,16},{48,248},{56,32},{... | collective-permute-start | bytes 405512 | tf_op jit(solution)/shard_map/ppermute | solution.py:224
  9.1 5.6 %collective-permute-start.8 = (bf16[528,128]{1,0:T(8,128)(2,1)S(1)}, bf16[528,128]{1,0:T(8,128)(2,1)S(1)}, u32[]{:S(2)}, u32[]{:S(2)}) collective-permute-start(bf16[528,128]{1,0:T(8,128)(2,1)S(1)} %get-tuple-element.40), channel_id=1, source_target_pairs={{0,72},{8,16},{16,88},{24,32},{32,104},{40,48},{48,120},{56,0},{64... | collective-permute-start | bytes 405512 | tf_op jit(solution)/shard_map/ppermute | solution.py:224
  11.5 5.4 %collective-permute-start.3 = (bf16[528,128]{1,0:T(8,128)(2,1)S(1)}, bf16[528,128]{1,0:T(8,128)(2,1)S(1)}, u32[]{:S(2)}, u32[]{:S(2)}) collective-permute-start(bf16[528,128]{1,0:T(8,128)(2,1)S(1)} %collective-permute-done.1.refs_6_), channel_id=1, source_target_pairs={{0,16},{8,72},{16,32},{24,88},{32,48},{40,104},{48,0},{56,120},{64... | collective-permute-start | bytes 405512 | tf_op jit(solution)/shard_map/ppermute | solution.py:224
  11.5 7.1 %collective-permute-start.7 = (bf16[528,128]{1,0:T(8,128)(2,1)S(1)}, bf16[528,128]{1,0:T(8,128)(2,1)S(1)}, u32[]{:S(2)}, u32[]{:S(2)}) collective-permute-start(bf16[528,128]{1,0:T(8,128)(2,1)S(1)} %get-tuple-element.40), channel_id=1, source_target_pairs={{0,8},{8,0},{16,24},{24,16},{32,40},{40,32},{48,56},{56,48},{1,9},... | collective-permute-start | bytes 405512 | tf_op jit(solution)/shard_map/ppermute | solution.py:226
  12.4 6.2 %collective-permute-start.2 = (bf16[528,128]{1,0:T(8,128)(2,1)S(1)}, bf16[528,128]{1,0:T(8,128)(2,1)S(1)}, u32[]{:S(2)}, u32[]{:S(2)}) collective-permute-start(bf16[528,128]{1,0:T(8,128)(2,1)S(1)} %collective-permute-done.1.refs_6_), channel_id=1, source_target_pairs={{0,8},{8,0},{16,24},{24,16},{32,40},{40,32},{48,56},{56,48},{1,9},... | collective-permute-start | bytes 405512 | tf_op jit(solution)/shard_map/ppermute | solution.py:226
  13.6 5.1 %collective-permute-start.6 = (bf16[528,128]{1,0:T(8,128)(2,1)S(1)}, bf16[528,128]{1,0:T(8,128)(2,1)S(1)}, u32[]{:S(2)}, u32[]{:S(2)}) collective-permute-start(bf16[528,128]{1,0:T(8,128)(2,1)S(1)} %collective-permute-done.5.refs_10_), channel_id=1, source_target_pairs={{0,8},{8,0},{16,24},{24,16},{32,40},{40,32},{48,56},{56,48},{1,9},... | collective-permute-start | bytes 405512 | tf_op jit(solution)/shard_map/ppermute | solution.py:226
  14.7 4.2 %collective-permute-start.10 = (bf16[528,128]{1,0:T(8,128)(2,1)S(1)}, bf16[528,128]{1,0:T(8,128)(2,1)S(1)}, u32[]{:S(2)}, u32[]{:S(2)}) collective-permute-start(bf16[528,128]{1,0:T(8,128)(2,1)S(1)} %collective-permute-done.9.refs_11_), channel_id=1, source_target_pairs={{0,48},{8,200},{16,0},{24,216},{32,16},{40,232},{48,32},{56,248},{... | collective-permute-start | bytes 405512 | tf_op jit(solution)/shard_map/ppermute | solution.py:224
  16.9 2.7 %collective-permute-start.4 = (bf16[528,128]{1,0:T(8,128)(2,1)S(1)}, bf16[528,128]{1,0:T(8,128)(2,1)S(1)}, u32[]{:S(2)}, u32[]{:S(2)}) collective-permute-start(bf16[528,128]{1,0:T(8,128)(2,1)S(1)} %collective-permute-done.3.refs_8_), channel_id=1, source_target_pairs={{0,8},{8,0},{16,24},{24,16},{32,40},{40,32},{48,56},{56,48},{1,9},... | collective-permute-start | bytes 405512 | tf_op jit(solution)/shard_map/ppermute | solution.py:226
  19.6 15.8 %copy-start = (bf16[512,4096]{1,0:T(8,128)(2,1)S(1)}, bf16[512,4096]{1,0:T(8,128)(2,1)}, u32[]{:S(2)}) copy-start(bf16[512,4096]{1,0:T(8,128)(2,1)} %w_ref.3) | copy-start | bytes 12582916
  20.7 7.0 %collective-permute-start.11 = (bf16[528,128]{1,0:T(8,128)(2,1)S(1)}, bf16[528,128]{1,0:T(8,128)(2,1)S(1)}, u32[]{:S(2)}, u32[]{:S(2)}) collective-permute-start(bf16[528,128]{1,0:T(8,128)(2,1)S(1)} %get-tuple-element.42), channel_id=1, source_target_pairs={{0,192},{8,56},{16,208},{24,8},{32,224},{40,24},{48,240},{56,40},{... | collective-permute-start | bytes 405512 | tf_op jit(solution)/shard_map/ppermute | solution.py:224
  21.4 7.0 %collective-permute-start.12 = (bf16[528,128]{1,0:T(8,128)(2,1)S(1)}, bf16[528,128]{1,0:T(8,128)(2,1)S(1)}, u32[]{:S(2)}, u32[]{:S(2)}) collective-permute-start(bf16[528,128]{1,0:T(8,128)(2,1)S(1)} %get-tuple-element.43), channel_id=1, source_target_pairs={{0,128},{8,40},{16,144},{24,56},{32,160},{40,8},{48,176},{56,24},{... | collective-permute-start | bytes 405512 | tf_op jit(solution)/shard_map/ppermute | solution.py:224
  24.6 6.4 %collective-permute-start.13 = (bf16[528,128]{1,0:T(8,128)(2,1)S(1)}, bf16[528,128]{1,0:T(8,128)(2,1)S(1)}, u32[]{:S(2)}, u32[]{:S(2)}) collective-permute-start(bf16[528,128]{1,0:T(8,128)(2,1)S(1)} %get-tuple-element.44), channel_id=1, source_target_pairs={{0,64},{8,24},{16,80},{24,40},{32,96},{40,56},{48,112},{56,8},{64,... | collective-permute-start | bytes 405512 | tf_op jit(solution)/shard_map/ppermute | solution.py:224
  24.6 6.4 %collective-permute-start.14 = (bf16[528,128]{1,0:T(8,128)(2,1)S(1)}, bf16[528,128]{1,0:T(8,128)(2,1)S(1)}, u32[]{:S(2)}, u32[]{:S(2)}) collective-permute-start(bf16[528,128]{1,0:T(8,128)(2,1)S(1)} %get-tuple-element.45), channel_id=1, source_target_pairs={{0,8},{8,0},{16,24},{24,16},{32,40},{40,32},{48,56},{56,48},{1,9},... | collective-permute-start | bytes 405512 | tf_op jit(solution)/shard_map/ppermute | solution.py:226
  24.9 6.1 %collective-permute-start.15 = (bf16[528,128]{1,0:T(8,128)(2,1)S(1)}, bf16[528,128]{1,0:T(8,128)(2,1)S(1)}, u32[]{:S(2)}, u32[]{:S(2)}) collective-permute-start(bf16[528,128]{1,0:T(8,128)(2,1)S(1)} %get-tuple-element.46), channel_id=1, source_target_pairs={{0,200},{8,48},{16,216},{24,0},{32,232},{40,16},{48,248},{56,32},{... | collective-permute-start | bytes 405512 | tf_op jit(solution)/shard_map/ppermute | solution.py:224
  27.7 6.1 %collective-permute-start.16 = (bf16[528,128]{1,0:T(8,128)(2,1)S(1)}, bf16[528,128]{1,0:T(8,128)(2,1)S(1)}, u32[]{:S(2)}, u32[]{:S(2)}) collective-permute-start(bf16[528,128]{1,0:T(8,128)(2,1)S(1)} %get-tuple-element.47), channel_id=1, source_target_pairs={{0,136},{8,32},{16,152},{24,48},{32,168},{40,0},{48,184},{56,16},{... | collective-permute-start | bytes 405512 | tf_op jit(solution)/shard_map/ppermute | solution.py:224
  28.5 6.9 %collective-permute-start.17 = (bf16[528,128]{1,0:T(8,128)(2,1)S(1)}, bf16[528,128]{1,0:T(8,128)(2,1)S(1)}, u32[]{:S(2)}, u32[]{:S(2)}) collective-permute-start(bf16[528,128]{1,0:T(8,128)(2,1)S(1)} %get-tuple-element.48), channel_id=1, source_target_pairs={{0,72},{8,16},{16,88},{24,32},{32,104},{40,48},{48,120},{56,0},{64... | collective-permute-start | bytes 405512 | tf_op jit(solution)/shard_map/ppermute | solution.py:224
  36.9 10.5 %collective-permute-start.24 = (bf16[64,2048]{1,0:T(8,128)(2,1)S(1)}, bf16[64,2048]{1,0:T(8,128)(2,1)S(1)}, u32[]{:S(2)}, u32[]{:S(2)}) collective-permute-start(bf16[64,2048]{1,0:T(8,128)(2,1)S(1)} %get-tuple-element.63), channel_id=1, source_target_pairs={{0,1},{1,2},{2,3},{3,4},{4,5},{5,6},{6,7},{7,0},{8,9},{9,10},{10,1... | collective-permute-start | bytes 786440 | tf_op jit(solution)/shard_map/ppermute | solution.py:227
  37.6 9.8 %collective-permute-start.25 = (bf16[64,2048]{1,0:T(8,128)(2,1)S(1)}, bf16[64,2048]{1,0:T(8,128)(2,1)S(1)}, u32[]{:S(2)}, u32[]{:S(2)}) collective-permute-start(bf16[64,2048]{1,0:T(8,128)(2,1)S(1)} %get-tuple-element.64), channel_id=1, source_target_pairs={{0,7},{1,0},{2,1},{3,2},{4,3},{5,4},{6,5},{7,6},{8,15},{9,8},{10,9... | collective-permute-start | bytes 786440 | tf_op jit(solution)/shard_map/ppermute | solution.py:227
  44.1 8.8 %collective-permute-start.18 = (bf16[64,2048]{1,0:T(8,128)(2,1)S(1)}, bf16[64,2048]{1,0:T(8,128)(2,1)S(1)}, u32[]{:S(2)}, u32[]{:S(2)}) collective-permute-start(bf16[64,2048]{1,0:T(8,128)(2,1)S(1)} %get-tuple-element.54), channel_id=1, source_target_pairs={{0,1},{1,2},{2,3},{3,4},{4,5},{5,6},{6,7},{7,0},{8,9},{9,10},{10,1... | collective-permute-start | bytes 786440 | tf_op jit(solution)/shard_map/ppermute | solution.py:227
  44.1 8.7 %collective-permute-start.19 = (bf16[64,2048]{1,0:T(8,128)(2,1)S(1)}, bf16[64,2048]{1,0:T(8,128)(2,1)S(1)}, u32[]{:S(2)}, u32[]{:S(2)}) collective-permute-start(bf16[64,2048]{1,0:T(8,128)(2,1)S(1)} %get-tuple-element.55), channel_id=1, source_target_pairs={{0,7},{1,0},{2,1},{3,2},{4,3},{5,4},{6,5},{7,6},{8,15},{9,8},{10,9... | collective-permute-start | bytes 786440 | tf_op jit(solution)/shard_map/ppermute | solution.py:227
  47.5 11.0 %collective-permute-start.26 = (bf16[64,2048]{1,0:T(8,128)(2,1)S(1)}, bf16[64,2048]{1,0:T(8,128)(2,1)S(1)}, u32[]{:S(2)}, u32[]{:S(2)}) collective-permute-start(bf16[64,2048]{1,0:T(8,128)(2,1)S(1)} %get-tuple-element.65), channel_id=1, source_target_pairs={{0,1},{1,2},{2,3},{3,4},{4,5},{5,6},{6,7},{7,0},{8,9},{9,10},{10,1... | collective-permute-start | bytes 786440 | tf_op jit(solution)/shard_map/ppermute | solution.py:227
  47.6 10.9 %collective-permute-start.27 = (bf16[64,2048]{1,0:T(8,128)(2,1)S(1)}, bf16[64,2048]{1,0:T(8,128)(2,1)S(1)}, u32[]{:S(2)}, u32[]{:S(2)}) collective-permute-start(bf16[64,2048]{1,0:T(8,128)(2,1)S(1)} %get-tuple-element.66), channel_id=1, source_target_pairs={{0,7},{1,0},{2,1},{3,2},{4,3},{5,4},{6,5},{7,6},{8,15},{9,8},{10,9... | collective-permute-start | bytes 786440 | tf_op jit(solution)/shard_map/ppermute | solution.py:227
  52.9 11.1 %collective-permute-start.20 = (bf16[64,2048]{1,0:T(8,128)(2,1)S(1)}, bf16[64,2048]{1,0:T(8,128)(2,1)S(1)}, u32[]{:S(2)}, u32[]{:S(2)}) collective-permute-start(bf16[64,2048]{1,0:T(8,128)(2,1)S(1)} %get-tuple-element.56), channel_id=1, source_target_pairs={{0,1},{1,2},{2,3},{3,4},{4,5},{5,6},{6,7},{7,0},{8,9},{9,10},{10,1... | collective-permute-start | bytes 786440 | tf_op jit(solution)/shard_map/ppermute | solution.py:227
  53.0 11.1 %collective-permute-start.21 = (bf16[64,2048]{1,0:T(8,128)(2,1)S(1)}, bf16[64,2048]{1,0:T(8,128)(2,1)S(1)}, u32[]{:S(2)}, u32[]{:S(2)}) collective-permute-start(bf16[64,2048]{1,0:T(8,128)(2,1)S(1)} %get-tuple-element.57), channel_id=1, source_target_pairs={{0,7},{1,0},{2,1},{3,2},{4,3},{5,4},{6,5},{7,6},{8,15},{9,8},{10,9... | collective-permute-start | bytes 786440 | tf_op jit(solution)/shard_map/ppermute | solution.py:227
  58.5 11.1 %collective-permute-start.28 = (bf16[64,2048]{1,0:T(8,128)(2,1)S(1)}, bf16[64,2048]{1,0:T(8,128)(2,1)S(1)}, u32[]{:S(2)}, u32[]{:S(2)}) collective-permute-start(bf16[64,2048]{1,0:T(8,128)(2,1)S(1)} %get-tuple-element.67), channel_id=1, source_target_pairs={{0,1},{1,2},{2,3},{3,4},{4,5},{5,6},{6,7},{7,0},{8,9},{9,10},{10,1... | collective-permute-start | bytes 786440 | tf_op jit(solution)/shard_map/ppermute | solution.py:227
  58.6 11.1 %collective-permute-start.29 = (bf16[64,2048]{1,0:T(8,128)(2,1)S(1)}, bf16[64,2048]{1,0:T(8,128)(2,1)S(1)}, u32[]{:S(2)}, u32[]{:S(2)}) collective-permute-start(bf16[64,2048]{1,0:T(8,128)(2,1)S(1)} %get-tuple-element.68), channel_id=1, source_target_pairs={{0,7},{1,0},{2,1},{3,2},{4,3},{5,4},{6,5},{7,6},{8,15},{9,8},{10,9... | collective-permute-start | bytes 786440 | tf_op jit(solution)/shard_map/ppermute | solution.py:227
  64.2 11.1 %collective-permute-start.22 = (bf16[64,2048]{1,0:T(8,128)(2,1)S(1)}, bf16[64,2048]{1,0:T(8,128)(2,1)S(1)}, u32[]{:S(2)}, u32[]{:S(2)}) collective-permute-start(bf16[64,2048]{1,0:T(8,128)(2,1)S(1)} %get-tuple-element.58), channel_id=1, source_target_pairs={{0,1},{1,2},{2,3},{3,4},{4,5},{5,6},{6,7},{7,0},{8,9},{9,10},{10,1... | collective-permute-start | bytes 786440 | tf_op jit(solution)/shard_map/ppermute | solution.py:227
  64.3 11.1 %collective-permute-start.23 = (bf16[64,2048]{1,0:T(8,128)(2,1)S(1)}, bf16[64,2048]{1,0:T(8,128)(2,1)S(1)}, u32[]{:S(2)}, u32[]{:S(2)}) collective-permute-start(bf16[64,2048]{1,0:T(8,128)(2,1)S(1)} %get-tuple-element.59), channel_id=1, source_target_pairs={{0,7},{1,0},{2,1},{3,2},{4,3},{5,4},{6,5},{7,6},{8,15},{9,8},{10,9... | collective-permute-start | bytes 786440 | tf_op jit(solution)/shard_map/ppermute | solution.py:227
  69.8 11.1 %collective-permute-start.30 = (bf16[64,2048]{1,0:T(8,128)(2,1)S(1)}, bf16[64,2048]{1,0:T(8,128)(2,1)S(1)}, u32[]{:S(2)}, u32[]{:S(2)}) collective-permute-start(bf16[64,2048]{1,0:T(8,128)(2,1)S(1)} %get-tuple-element.69), channel_id=1, source_target_pairs={{0,1},{1,2},{2,3},{3,4},{4,5},{5,6},{6,7},{7,0},{8,9},{9,10},{10,1... | collective-permute-start | bytes 786440 | tf_op jit(solution)/shard_map/ppermute | solution.py:227
  69.9 11.1 %collective-permute-start.31 = (bf16[64,2048]{1,0:T(8,128)(2,1)S(1)}, bf16[64,2048]{1,0:T(8,128)(2,1)S(1)}, u32[]{:S(2)}, u32[]{:S(2)}) collective-permute-start(bf16[64,2048]{1,0:T(8,128)(2,1)S(1)} %get-tuple-element.70), channel_id=1, source_target_pairs={{0,7},{1,0},{2,1},{3,2},{4,3},{5,4},{6,5},{7,6},{8,15},{9,8},{10,9... | collective-permute-start | bytes 786440 | tf_op jit(solution)/shard_map/ppermute | solution.py:227

commit v2 on v1

--- a/solution.py
+++ b/solution.py
@@ -94,7 +94,8 @@
 
 
 def partial_kernel(*refs):
-    lists, keys, outs = refs[:4], refs[4:12], refs[12:]
+    lists, keys, outs = refs[:4], refs[4:12], list(refs[12:])
+    outs[4:5] = [outs[4].at[:ROWS], outs[4].at[ROWS:]]
     core, kb = lax.rem(lax.axis_index("gy"), 2), key_blocks()
     lane = lax.broadcasted_iota(jnp.int32, (HD, 256), 0)
     col = lax.broadcasted_iota(jnp.int32, (HD, 256), 1)
@@ -146,6 +147,7 @@
 def far_kernel(qf_ref, w_ref, *refs):
     parts, (right_ref, left_ref, state_ref, sums_ref, att_ref) = (refs[:4], refs[4:8]), refs[8:]
     core, far = lax.rem(lax.axis_index("gy"), 2), lax.rem(lax.axis_index("gz") + 4, 8)
+    parts = [[*p[:2], p[2].at[side * ROWS : (side + 1) * ROWS], p[3]] for side, p in enumerate(parts)]
     for side in range(2):
         role = core if side == 0 else 1 - core
         tail = sum(p[STATES:, :].astype(F32) for p in parts[side])
@@ -244,9 +246,14 @@
     for d in (1, 2, 3):
         lists.append(to_mate(keys[d, 0]))
     order = [(d, c) for d in range(4) for c in range(2)]
-    parts = call(partial_kernel, (unit,) * 8, 10**9, 16)(*lists, *(keys[i] for i in order))
-    parts = dict(zip(order, parts))
-    for d in (2, 1, 3):
+    pair = jax.ShapeDtypeStruct((2 * ROWS, HD), BF16)
+    parts = call(partial_kernel, (unit,) * 4 + (pair,) + (unit,) * 2, 10**9, 16)(
+        *lists, *(keys[i] for i in order)
+    )
+    parts = dict(zip(order[:5] + order[6:], parts))
+    parts[2, 0] = by_role(parts[2, 0], 2, "xy")
+    parts[2, 1] = to_mate(parts[2, 0])
+    for d in (1, 3):
         parts[d, 0] = by_role(parts[d, 0], -d, "xy")
         parts[d, 1] = by_role(parts[d, 1], -d, "xy", cross=True)
     parts[0, 1] = to_mate(parts[0, 1])

time: 82.2 us -> 86 us (1.046)
  waiting for transfers between devices: 28.3 us -> 31.7 us
    ppermute x12 -> x11, waiting for transfers between devices: 7.78 us -> 10.6 us  [by_role(): return lax.ppermute(a, ('gx', 'gy'), pairs)]
    ppermute x6 -> x7, starting transfers between devices: 6.82 us -> 9.08 us  [per_device(): to_mate = lambda a: lax.ppermute(a, 'gy', [(i, i ^ 1) for i in range(8)])]
    ppermute x12 -> x11, starting transfers between devices: 15.8 us -> 13.6 us  [by_role(): return lax.ppermute(a, ('gx', 'gy'), pairs)]
  transfers between devices with their start and end apart: 32 -> 32, of which waited for: 14 -> 16; matrix products, arithmetic and copies ran while one was open for 3% -> 3% of each run, Pallas kernels for 4% -> 3%
where the time goes in v2:
time: 86 us; the launch traced here: 85.8 us
  starting transfers between devices  44.3 us (52%)
  waiting for transfers between devices  31.7 us (37%)
  Pallas kernels  6.78 us (8%)
  other arithmetic  2.67 us (3%)
    ppermute x14, starting transfers between devices, per_device(): lax.ppermute(a, 'gz', [(i, (i + d) % 8) for i in range(8)])  21.6 us
    ppermute x14, waiting for transfers between devices, per_device(): lax.ppermute(a, 'gz', [(i, (i + d) % 8) for i in range(8)])  20.4 us
    ppermute x11, starting transfers between devices, by_role(): return lax.ppermute(a, ('gx', 'gy'), pairs)  13.6 us
    ppermute x11, waiting for transfers between devices, by_role(): return lax.ppermute(a, ('gx', 'gy'), pairs)  10.6 us
    ppermute x7, starting transfers between devices, per_device(): to_mate = lambda a: lax.ppermute(a, 'gy', [(i, i ^ 1) for i in range(8)])  9.08 us
    pallas_call x1, Pallas kernels, per_device(): call(project_kernel, (piece, piece) + (term,) * 5 + (jax.ShapeDtypeStruct...  2.48 us
  transfers between devices with their start and end apart: 32, of which 16 were waited for; matrix products, arithmetic and copies ran while one was open for 3% of the time, Pallas kernels for 3%

profile of v2, /device:TPU:1, one launch (start us, length us, event | category | flops | bytes accessed | tf_op | source)
XLA Modules:
  0.0 85.8 jit_solution(3960983487043087895)
XLA Ops:
  0.0 3.2 %collective-permute-start = (s32[2,4,8]{2,1,0:T(4,128)}, s32[2,4,8]{2,1,0:T(4,128)S(1)}, u32[]{:S(2)}, u32[]{:S(2)}) collective-permute-start(s32[2,4,8]{2,1,0:T(4,128)} %own_ref.1), channel_id=1, source_target_pairs={{0,8},{8,0},{16,24},{24,16},{32,40},{40,32},{48,56},{56,48},{1,9},... | collective-permute-start | bytes 776 | tf_op jit(solution)/shard_map/ppermute | solution.py:228
  3.2 1.3 %fusion.4 = bf16[512,512]{1,0:T(8,128)(2,1)S(1)} fusion(bf16[512,512]{1,0:T(8,128)(2,1)} %param.6), kind=kLoop, calls=%fused_computation.10 | loop fusion | flops 1572864 | bytes 1048576 | tf_op jit(solution)/shard_map/convert_element_type | solution.py:27
  4.5 1.1 %pad_maximum_fusion.kv_ref = bf16[1024,512]{1,0:T(8,128)(2,1)S(1)} fusion(bf16[512,512]{1,0:T(8,128)(2,1)} %param.7, bf16[512,512]{1,0:T(8,128)(2,1)S(1)} %fusion.4), kind=kLoop, calls=%fused_computation.12 | loop fusion | flops 2097152 | bytes 2097152 | tf_op jit(solution)/shard_map/concatenate | solution.py:232
  5.6 0.4 shard_map.55
  6.2 2.7 %collective-permute-start.5 = (bf16[528,128]{1,0:T(8,128)(2,1)S(1)}, bf16[528,128]{1,0:T(8,128)(2,1)S(1)}, u32[]{:S(2)}, u32[]{:S(2)}) collective-permute-start(bf16[528,128]{1,0:T(8,128)(2,1)S(1)} %get-tuple-element.38.refs_4_), channel_id=1, source_target_pairs={{0,48},{8,200},{16,0},{24,216},{32,16},{40,232},{48,32},{56,248},{... | collective-permute-start | bytes 405512 | tf_op jit(solution)/shard_map/ppermute | solution.py:226
  8.8 0.3 collective-permute-start.9
  9.1 0.9 %collective-permute-start.8 = (bf16[528,128]{1,0:T(8,128)(2,1)S(1)}, bf16[528,128]{1,0:T(8,128)(2,1)S(1)}, u32[]{:S(2)}, u32[]{:S(2)}) collective-permute-start(bf16[528,128]{1,0:T(8,128)(2,1)S(1)} %get-tuple-element.39), channel_id=1, source_target_pairs={{0,72},{8,16},{16,88},{24,32},{32,104},{40,48},{48,120},{56,0},{64... | collective-permute-start | bytes 405512 | tf_op jit(solution)/shard_map/ppermute | solution.py:226
  10.0 1.6 %collective-permute-done.1.refs_6_ = bf16[528,128]{1,0:T(8,128)(2,1)S(1)} collective-permute-done((bf16[528,128]{1,0:T(8,128)(2,1)S(1)}, bf16[528,128]{1,0:T(8,128)(2,1)S(1)}, u32[]{:S(2)}, u32[]{:S(2)}) %collective-permute-start.1) | collective-permute-done | bytes 135200 | tf_op jit(solution)/shard_map/ppermute | solution.py:226
  11.5 0.9 %collective-permute-start.7 = (bf16[528,128]{1,0:T(8,128)(2,1)S(1)}, bf16[528,128]{1,0:T(8,128)(2,1)S(1)}, u32[]{:S(2)}, u32[]{:S(2)}) collective-permute-start(bf16[528,128]{1,0:T(8,128)(2,1)S(1)} %get-tuple-element.39), channel_id=1, source_target_pairs={{0,8},{8,0},{16,24},{24,16},{32,40},{40,32},{48,56},{56,48},{1,9},... | collective-permute-start | bytes 405512 | tf_op jit(solution)/shard_map/ppermute | solution.py:228
  12.4 0.5 collective-permute-start.2
  12.9 0.7 collective-permute-done.9.refs_11_
  13.6 0.3 collective-permute-start.6
  13.8 0.9 %collective-permute-done.8.refs_7_ = bf16[528,128]{1,0:T(8,128)(2,1)S(1)} collective-permute-done((bf16[528,128]{1,0:T(8,128)(2,1)S(1)}, bf16[528,128]{1,0:T(8,128)(2,1)S(1)}, u32[]{:S(2)}, u32[]{:S(2)}) %collective-permute-start.8) | collective-permute-done | bytes 135200 | tf_op jit(solution)/shard_map/ppermute | solution.py:226
  14.7 2.1 %collective-permute-start.10 = (bf16[528,128]{1,0:T(8,128)(2,1)S(1)}, bf16[528,128]{1,0:T(8,128)(2,1)S(1)}, u32[]{:S(2)}, u32[]{:S(2)}) collective-permute-start(bf16[528,128]{1,0:T(8,128)(2,1)S(1)} %collective-permute-done.9.refs_11_), channel_id=1, source_target_pairs={{0,48},{8,200},{16,0},{24,216},{32,16},{40,232},{48,32},{56,248},{... | collective-permute-start | bytes 405512 | tf_op jit(solution)/shard_map/ppermute | solution.py:226
  16.9 1.7 %collective-permute-start.4 = (bf16[528,128]{1,0:T(8,128)(2,1)S(1)}, bf16[528,128]{1,0:T(8,128)(2,1)S(1)}, u32[]{:S(2)}, u32[]{:S(2)}) collective-permute-start(bf16[528,128]{1,0:T(8,128)(2,1)S(1)} %collective-permute-done.3.refs_8_), channel_id=1, source_target_pairs={{0,8},{8,0},{16,24},{24,16},{32,40},{40,32},{48,56},{56,48},{1,9},... | collective-permute-start | bytes 405512 | tf_op jit(solution)/shard_map/ppermute | solution.py:228
  18.6 0.3 collective-permute-done.10.refs_9_
  18.9 0.7 collective-permute-done.4.refs_2_
  19.6 1.1 %shard_map.56 = (bf16[528,128]{1,0:T(8,128)(2,1)S(1)}, bf16[528,128]{1,0:T(8,128)(2,1)S(1)}, bf16[528,128]{1,0:T(8,128)(2,1)S(1)}, bf16[528,128]{1,0:T(8,128)(2,...) custom-call(f32[16,128]{1,0:T(8,128)S(1)} %get-tuple-element.37.refs_0_, ...), custom_call_target="tpu_custom_call" | custom-call | flops 1000000000 | bytes 3906250 | tf_op jit(solution)/shard_map/pallas_call | solution.py:250
  20.7 0.3 collective-permute-start.12
  21.0 4.2 %collective-permute-start.11 = (bf16[528,128]{1,0:T(8,128)(2,1)S(1)}, bf16[528,128]{1,0:T(8,128)(2,1)S(1)}, u32[]{:S(2)}, u32[]{:S(2)}) collective-permute-start(bf16[528,128]{1,0:T(8,128)(2,1)S(1)} %get-tuple-element.41), channel_id=1, source_target_pairs={{0,192},{8,56},{16,208},{24,8},{32,224},{40,24},{48,240},{56,40},{... | collective-permute-start | bytes 405512 | tf_op jit(solution)/shard_map/ppermute | solution.py:226
  25.2 2.7 %collective-permute-done.12.refs_2_ = bf16[1056,128]{1,0:T(8,128)(2,1)S(1)} collective-permute-done((bf16[1056,128]{1,0:T(8,128)(2,1)S(1)}, bf16[1056,128]{1,0:T(8,128)(2,1)S(1)}, u32[]{:S(2)}, u32[]{:S(2)}) %collective-permute-start.12) | collective-permute-done | bytes 270368 | tf_op jit(solution)/shard_map/ppermute | solution.py:226
  27.9 1.3 %collective-permute-start.16 = (bf16[1056,128]{1,0:T(8,128)(2,1)S(1)}, bf16[1056,128]{1,0:T(8,128)(2,1)S(1)}, u32[]{:S(2)}, u32[]{:S(2)}) collective-permute-start(bf16[1056,128]{1,0:T(8,128)(2,1)S(1)} %collective-permute-done.12.refs_2_), channel_id=1, source_target_pairs={{0,8},{8,0},{16,24},{24,16},{32,40},{40,32},{48,56},{56,48},{1,9},... | collective-permute-start | bytes 811016 | tf_op jit(solution)/shard_map/ppermute | solution.py:228
  29.2 0.5 collective-permute-start.13
  29.7 1.2 %collective-permute-start.14 = (bf16[528,128]{1,0:T(8,128)(2,1)S(1)}, bf16[528,128]{1,0:T(8,128)(2,1)S(1)}, u32[]{:S(2)}, u32[]{:S(2)}) collective-permute-start(bf16[528,128]{1,0:T(8,128)(2,1)S(1)} %get-tuple-element.44), channel_id=1, source_target_pairs={{0,8},{8,0},{16,24},{24,16},{32,40},{40,32},{48,56},{56,48},{1,9},... | collective-permute-start | bytes 405512 | tf_op jit(solution)/shard_map/ppermute | solution.py:228
  30.9 1.7 %collective-permute-start.15 = (bf16[528,128]{1,0:T(8,128)(2,1)S(1)}, bf16[528,128]{1,0:T(8,128)(2,1)S(1)}, u32[]{:S(2)}, u32[]{:S(2)}) collective-permute-start(bf16[528,128]{1,0:T(8,128)(2,1)S(1)} %get-tuple-element.45), channel_id=1, source_target_pairs={{0,200},{8,48},{16,216},{24,0},{32,232},{40,16},{48,248},{56,32},{... | collective-permute-start | bytes 405512 | tf_op jit(solution)/shard_map/ppermute | solution.py:226
  32.6 0.8 collective-permute-start.17
  33.7 1.2 %collective-permute-done.13.refs_3_ = bf16[528,128]{1,0:T(8,128)(2,1)S(1)} collective-permute-done((bf16[528,128]{1,0:T(8,128)(2,1)S(1)}, bf16[528,128]{1,0:T(8,128)(2,1)S(1)}, u32[]{:S(2)}, u32[]{:S(2)}) %collective-permute-start.13) | collective-permute-done | bytes 135200 | tf_op jit(solution)/shard_map/ppermute | solution.py:226
  34.9 0.4 collective-permute-done.15.refs_5_
  35.3 2.9 %collective-permute-done.17.refs_7_ = bf16[528,128]{1,0:T(8,128)(2,1)S(1)} collective-permute-done((bf16[528,128]{1,0:T(8,128)(2,1)S(1)}, bf16[528,128]{1,0:T(8,128)(2,1)S(1)}, u32[]{:S(2)}, u32[]{:S(2)}) %collective-permute-start.17) | collective-permute-done | bytes 135200 | tf_op jit(solution)/shard_map/ppermute | solution.py:226
  38.2 1.5 %shard_map.57 = (bf16[64,2048]{1,0:T(8,128)(2,1)S(1)}, bf16[64,2048]{1,0:T(8,128)(2,1)S(1)}, bf16[1024,128]{1,0:T(8,128)(2,1)S(1)}, bf16[1024,128]{1,0:T(8,128)(2,1)S(1)}, bf16[64,512]{1,0:T(8,128)(2,1)}) custom-call(bf16[512,512]{1,0:T(8,128)(2,1)S(1)} %fusion.1.qf_ref, bf16[512,4096]{1,0:T(8,128)(2,1)S(1)} %copy-done, ...), custom_call_target="tpu_custom_call" | custom-call | flops 1000000000 | bytes 3906250 | tf_op jit(solution)/shard_map/pallas_call | solution.py:265
  39.7 1.0 %collective-permute-start.24 = (bf16[64,2048]{1,0:T(8,128)(2,1)S(1)}, bf16[64,2048]{1,0:T(8,128)(2,1)S(1)}, u32[]{:S(2)}, u32[]{:S(2)}) collective-permute-start(bf16[64,2048]{1,0:T(8,128)(2,1)S(1)} %get-tuple-element.61), channel_id=1, source_target_pairs={{0,1},{1,2},{2,3},{3,4},{4,5},{5,6},{6,7},{7,0},{8,9},{9,10},{10,1... | collective-permute-start | bytes 786440 | tf_op jit(solution)/shard_map/ppermute | solution.py:229
  40.7 3.9 %collective-permute-start.25 = (bf16[64,2048]{1,0:T(8,128)(2,1)S(1)}, bf16[64,2048]{1,0:T(8,128)(2,1)S(1)}, u32[]{:S(2)}, u32[]{:S(2)}) collective-permute-start(bf16[64,2048]{1,0:T(8,128)(2,1)S(1)} %get-tuple-element.62), channel_id=1, source_target_pairs={{0,7},{1,0},{2,1},{3,2},{4,3},{5,4},{6,5},{7,6},{8,15},{9,8},{10,9... | collective-permute-start | bytes 786440 | tf_op jit(solution)/shard_map/ppermute | solution.py:229
  44.7 2.5 %shard_map.58 = (bf16[64,2048]{1,0:T(8,128)(2,1)S(1)}, bf16[64,2048]{1,0:T(8,128)(2,1)S(1)}, f32[128,2048]{1,0:T(8,128)S(1)}, f32[128,2048]{1,0:T(8,128)S(1)}, f...) custom-call(bf16[512,512]{1,0:T(8,128)(2,1)S(1)} %fusion.1.qf_ref, ...), custom_call_target="tpu_custom_call" | custom-call | flops 4000000000 | bytes 15625000 | tf_op jit(solution)/shard_map/pallas_call | solution.py:273
  47.2 2.7 %collective-permute-start.19 = (bf16[64,2048]{1,0:T(8,128)(2,1)S(1)}, bf16[64,2048]{1,0:T(8,128)(2,1)S(1)}, u32[]{:S(2)}, u32[]{:S(2)}) collective-permute-start(bf16[64,2048]{1,0:T(8,128)(2,1)S(1)} %get-tuple-element.53), channel_id=1, source_target_pairs={{0,7},{1,0},{2,1},{3,2},{4,3},{5,4},{6,5},{7,6},{8,15},{9,8},{10,9... | collective-permute-start | bytes 786440 | tf_op jit(solution)/shard_map/ppermute | solution.py:229
  49.9 1.3 %collective-permute-done.24.from_left_ref = bf16[64,2048]{1,0:T(8,128)(2,1)S(1)} collective-permute-done((bf16[64,2048]{1,0:T(8,128)(2,1)S(1)}, bf16[64,2048]{1,0:T(8,128)(2,1)S(1)}, u32[]{:S(2)}, u32[]{:S(2)}) %collective-permute-start.24) | collective-permute-done | bytes 262176 | tf_op jit(solution)/shard_map/ppermute | solution.py:229
  51.4 2.7 %collective-permute-start.27 = (bf16[64,2048]{1,0:T(8,128)(2,1)S(1)}, bf16[64,2048]{1,0:T(8,128)(2,1)S(1)}, u32[]{:S(2)}, u32[]{:S(2)}) collective-permute-start(bf16[64,2048]{1,0:T(8,128)(2,1)S(1)} %get-tuple-element.64), channel_id=1, source_target_pairs={{0,7},{1,0},{2,1},{3,2},{4,3},{5,4},{6,5},{7,6},{8,15},{9,8},{10,9... | collective-permute-start | bytes 786440 | tf_op jit(solution)/shard_map/ppermute | solution.py:229
  54.1 2.6 %collective-permute-done.18.from_left_ref = bf16[64,2048]{1,0:T(8,128)(2,1)S(1)} collective-permute-done((bf16[64,2048]{1,0:T(8,128)(2,1)S(1)}, bf16[64,2048]{1,0:T(8,128)(2,1)S(1)}, u32[]{:S(2)}, u32[]{:S(2)}) %collective-permute-start.18) | collective-permute-done | bytes 262176 | tf_op jit(solution)/shard_map/ppermute | solution.py:229
  56.8 2.7 %collective-permute-start.21 = (bf16[64,2048]{1,0:T(8,128)(2,1)S(1)}, bf16[64,2048]{1,0:T(8,128)(2,1)S(1)}, u32[]{:S(2)}, u32[]{:S(2)}) collective-permute-start(bf16[64,2048]{1,0:T(8,128)(2,1)S(1)} %get-tuple-element.55), channel_id=1, source_target_pairs={{0,7},{1,0},{2,1},{3,2},{4,3},{5,4},{6,5},{7,6},{8,15},{9,8},{10,9... | collective-permute-start | bytes 786440 | tf_op jit(solution)/shard_map/ppermute | solution.py:229
  59.5 2.8 %collective-permute-done.26.from_left_ref = bf16[64,2048]{1,0:T(8,128)(2,1)S(1)} collective-permute-done((bf16[64,2048]{1,0:T(8,128)(2,1)S(1)}, bf16[64,2048]{1,0:T(8,128)(2,1)S(1)}, u32[]{:S(2)}, u32[]{:S(2)}) %collective-permute-start.26) | collective-permute-done | bytes 262176 | tf_op jit(solution)/shard_map/ppermute | solution.py:229
  62.5 2.7 %collective-permute-start.29 = (bf16[64,2048]{1,0:T(8,128)(2,1)S(1)}, bf16[64,2048]{1,0:T(8,128)(2,1)S(1)}, u32[]{:S(2)}, u32[]{:S(2)}) collective-permute-start(bf16[64,2048]{1,0:T(8,128)(2,1)S(1)} %get-tuple-element.66), channel_id=1, source_target_pairs={{0,7},{1,0},{2,1},{3,2},{4,3},{5,4},{6,5},{7,6},{8,15},{9,8},{10,9... | collective-permute-start | bytes 786440 | tf_op jit(solution)/shard_map/ppermute | solution.py:229
  65.1 2.8 %collective-permute-done.20.from_left_ref = bf16[64,2048]{1,0:T(8,128)(2,1)S(1)} collective-permute-done((bf16[64,2048]{1,0:T(8,128)(2,1)S(1)}, bf16[64,2048]{1,0:T(8,128)(2,1)S(1)}, u32[]{:S(2)}, u32[]{:S(2)}) %collective-permute-start.20) | collective-permute-done | bytes 262176 | tf_op jit(solution)/shard_map/ppermute | solution.py:229
  68.0 0.3 collective-permute-start.22
  68.3 2.7 %collective-permute-start.23 = (bf16[64,2048]{1,0:T(8,128)(2,1)S(1)}, bf16[64,2048]{1,0:T(8,128)(2,1)S(1)}, u32[]{:S(2)}, u32[]{:S(2)}) collective-permute-start(bf16[64,2048]{1,0:T(8,128)(2,1)S(1)} %get-tuple-element.57), channel_id=1, source_target_pairs={{0,7},{1,0},{2,1},{3,2},{4,3},{5,4},{6,5},{7,6},{8,15},{9,8},{10,9... | collective-permute-start | bytes 786440 | tf_op jit(solution)/shard_map/ppermute | solution.py:229
  71.0 2.5 %collective-permute-done.28.from_left_ref = bf16[64,2048]{1,0:T(8,128)(2,1)S(1)} collective-permute-done((bf16[64,2048]{1,0:T(8,128)(2,1)S(1)}, bf16[64,2048]{1,0:T(8,128)(2,1)S(1)}, u32[]{:S(2)}, u32[]{:S(2)}) %collective-permute-start.28) | collective-permute-done | bytes 262176 | tf_op jit(solution)/shard_map/ppermute | solution.py:229
  73.7 2.7 %collective-permute-start.31 = (bf16[64,2048]{1,0:T(8,128)(2,1)S(1)}, bf16[64,2048]{1,0:T(8,128)(2,1)S(1)}, u32[]{:S(2)}, u32[]{:S(2)}) collective-permute-start(bf16[64,2048]{1,0:T(8,128)(2,1)S(1)} %get-tuple-element.68), channel_id=1, source_target_pairs={{0,7},{1,0},{2,1},{3,2},{4,3},{5,4},{6,5},{7,6},{8,15},{9,8},{10,9... | collective-permute-start | bytes 786440 | tf_op jit(solution)/shard_map/ppermute | solution.py:229
  76.4 2.8 %collective-permute-done.22.right0 = bf16[64,2048]{1,0:T(8,128)(2,1)S(1)} collective-permute-done((bf16[64,2048]{1,0:T(8,128)(2,1)S(1)}, bf16[64,2048]{1,0:T(8,128)(2,1)S(1)}, u32[]{:S(2)}, u32[]{:S(2)}) %collective-permute-start.22) | collective-permute-done | bytes 262176 | tf_op jit(solution)/shard_map/ppermute | solution.py:229
  79.1 5.6 %collective-permute-done.30.right1 = bf16[64,2048]{1,0:T(8,128)(2,1)S(1)} collective-permute-done((bf16[64,2048]{1,0:T(8,128)(2,1)S(1)}, bf16[64,2048]{1,0:T(8,128)(2,1)S(1)}, u32[]{:S(2)}, u32[]{:S(2)}) %collective-permute-start.30) | collective-permute-done | bytes 262176 | tf_op jit(solution)/shard_map/ppermute | solution.py:229
  84.8 0.9 %last.1 = bf16[64,4096]{1,0:T(8,128)(2,1)} custom-call(f32[64,4096]{1,0:T(8,128)S(1)} %get-tuple-element.49.own_ref, bf16[64,2048]{1,0:T(8,128)(2,1)S(1)} %collective-permute-done.22.right0, bf16[64,2048]{1,0:T(8,128)(2,1)S(1)} %collective-permute-done.23.left1, bf16[64,2048]{1,0:T(8,128)(2,1)S(1)} %collective-permute-done.30.right1, ...), custom_call_target="tpu_custom_call" | custom-call | flops 100000000 | bytes 1000000 | tf_op jit(solution)/shard_map/last/pallas_call | solution.py:292
  (35 shorter events, 1.3 us)
Async XLA Ops:
  0.0 5.6 %copy-start.1 = (s32[2,4,8]{2,1,0:T(4,128)S(1)}, s32[2,4,8]{2,1,0:T(4,128)}, u32[]{:S(2)}) copy-start(s32[2,4,8]{2,1,0:T(4,128)} %own_ref.1) | copy-start | bytes 772
  0.0 5.6 %collective-permute-start = (s32[2,4,8]{2,1,0:T(4,128)}, s32[2,4,8]{2,1,0:T(4,128)S(1)}, u32[]{:S(2)}, u32[]{:S(2)}) collective-permute-start(s32[2,4,8]{2,1,0:T(4,128)} %own_ref.1), channel_id=1, source_target_pairs={{0,8},{8,0},{16,24},{24,16},{32,40},{40,32},{48,56},{56,48},{1,9},... | collective-permute-start | bytes 776 | tf_op jit(solution)/shard_map/ppermute | solution.py:228
  6.1 27.4 %copy-start.2 = (bf16[512,512]{1,0:T(8,128)(2,1)S(1)}, bf16[512,512]{1,0:T(8,128)(2,1)}, u32[]{:S(2)}) copy-start(bf16[512,512]{1,0:T(8,128)(2,1)} %param.5) | copy-start | bytes 1572868
  6.1 5.4 %collective-permute-start.1 = (bf16[528,128]{1,0:T(8,128)(2,1)S(1)}, bf16[528,128]{1,0:T(8,128)(2,1)S(1)}, u32[]{:S(2)}, u32[]{:S(2)}) collective-permute-start(bf16[528,128]{1,0:T(8,128)(2,1)S(1)} %get-tuple-element.38.refs_4_), channel_id=1, source_target_pairs={{0,16},{8,72},{16,32},{24,88},{32,48},{40,104},{48,0},{56,120},{64... | collective-permute-start | bytes 405512 | tf_op jit(solution)/shard_map/ppermute | solution.py:226
  6.2 6.2 %collective-permute-start.5 = (bf16[528,128]{1,0:T(8,128)(2,1)S(1)}, bf16[528,128]{1,0:T(8,128)(2,1)S(1)}, u32[]{:S(2)}, u32[]{:S(2)}) collective-permute-start(bf16[528,128]{1,0:T(8,128)(2,1)S(1)} %get-tuple-element.38.refs_4_), channel_id=1, source_target_pairs={{0,48},{8,200},{16,0},{24,216},{32,16},{40,232},{48,32},{56,248},{... | collective-permute-start | bytes 405512 | tf_op jit(solution)/shard_map/ppermute | solution.py:226
  8.8 4.7 %collective-permute-start.9 = (bf16[528,128]{1,0:T(8,128)(2,1)S(1)}, bf16[528,128]{1,0:T(8,128)(2,1)S(1)}, u32[]{:S(2)}, u32[]{:S(2)}) collective-permute-start(bf16[528,128]{1,0:T(8,128)(2,1)S(1)} %get-tuple-element.39), channel_id=1, source_target_pairs={{0,200},{8,48},{16,216},{24,0},{32,232},{40,16},{48,248},{56,32},{... | collective-permute-start | bytes 405512 | tf_op jit(solution)/shard_map/ppermute | solution.py:226
  9.1 5.6 %collective-permute-start.8 = (bf16[528,128]{1,0:T(8,128)(2,1)S(1)}, bf16[528,128]{1,0:T(8,128)(2,1)S(1)}, u32[]{:S(2)}, u32[]{:S(2)}) collective-permute-start(bf16[528,128]{1,0:T(8,128)(2,1)S(1)} %get-tuple-element.39), channel_id=1, source_target_pairs={{0,72},{8,16},{16,88},{24,32},{32,104},{40,48},{48,120},{56,0},{64... | collective-permute-start | bytes 405512 | tf_op jit(solution)/shard_map/ppermute | solution.py:226
  11.5 5.4 %collective-permute-start.3 = (bf16[528,128]{1,0:T(8,128)(2,1)S(1)}, bf16[528,128]{1,0:T(8,128)(2,1)S(1)}, u32[]{:S(2)}, u32[]{:S(2)}) collective-permute-start(bf16[528,128]{1,0:T(8,128)(2,1)S(1)} %collective-permute-done.1.refs_6_), channel_id=1, source_target_pairs={{0,16},{8,72},{16,32},{24,88},{32,48},{40,104},{48,0},{56,120},{64... | collective-permute-start | bytes 405512 | tf_op jit(solution)/shard_map/ppermute | solution.py:226
  11.5 7.1 %collective-permute-start.7 = (bf16[528,128]{1,0:T(8,128)(2,1)S(1)}, bf16[528,128]{1,0:T(8,128)(2,1)S(1)}, u32[]{:S(2)}, u32[]{:S(2)}) collective-permute-start(bf16[528,128]{1,0:T(8,128)(2,1)S(1)} %get-tuple-element.39), channel_id=1, source_target_pairs={{0,8},{8,0},{16,24},{24,16},{32,40},{40,32},{48,56},{56,48},{1,9},... | collective-permute-start | bytes 405512 | tf_op jit(solution)/shard_map/ppermute | solution.py:228
  12.4 6.2 %collective-permute-start.2 = (bf16[528,128]{1,0:T(8,128)(2,1)S(1)}, bf16[528,128]{1,0:T(8,128)(2,1)S(1)}, u32[]{:S(2)}, u32[]{:S(2)}) collective-permute-start(bf16[528,128]{1,0:T(8,128)(2,1)S(1)} %collective-permute-done.1.refs_6_), channel_id=1, source_target_pairs={{0,8},{8,0},{16,24},{24,16},{32,40},{40,32},{48,56},{56,48},{1,9},... | collective-permute-start | bytes 405512 | tf_op jit(solution)/shard_map/ppermute | solution.py:228
  13.6 5.1 %collective-permute-start.6 = (bf16[528,128]{1,0:T(8,128)(2,1)S(1)}, bf16[528,128]{1,0:T(8,128)(2,1)S(1)}, u32[]{:S(2)}, u32[]{:S(2)}) collective-permute-start(bf16[528,128]{1,0:T(8,128)(2,1)S(1)} %collective-permute-done.5.refs_10_), channel_id=1, source_target_pairs={{0,8},{8,0},{16,24},{24,16},{32,40},{40,32},{48,56},{56,48},{1,9},... | collective-permute-start | bytes 405512 | tf_op jit(solution)/shard_map/ppermute | solution.py:228
  14.7 4.2 %collective-permute-start.10 = (bf16[528,128]{1,0:T(8,128)(2,1)S(1)}, bf16[528,128]{1,0:T(8,128)(2,1)S(1)}, u32[]{:S(2)}, u32[]{:S(2)}) collective-permute-start(bf16[528,128]{1,0:T(8,128)(2,1)S(1)} %collective-permute-done.9.refs_11_), channel_id=1, source_target_pairs={{0,48},{8,200},{16,0},{24,216},{32,16},{40,232},{48,32},{56,248},{... | collective-permute-start | bytes 405512 | tf_op jit(solution)/shard_map/ppermute | solution.py:226
  16.9 2.7 %collective-permute-start.4 = (bf16[528,128]{1,0:T(8,128)(2,1)S(1)}, bf16[528,128]{1,0:T(8,128)(2,1)S(1)}, u32[]{:S(2)}, u32[]{:S(2)}) collective-permute-start(bf16[528,128]{1,0:T(8,128)(2,1)S(1)} %collective-permute-done.3.refs_8_), channel_id=1, source_target_pairs={{0,8},{8,0},{16,24},{24,16},{32,40},{40,32},{48,56},{56,48},{1,9},... | collective-permute-start | bytes 405512 | tf_op jit(solution)/shard_map/ppermute | solution.py:228
  19.6 18.6 %copy-start = (bf16[512,4096]{1,0:T(8,128)(2,1)S(1)}, bf16[512,4096]{1,0:T(8,128)(2,1)}, u32[]{:S(2)}) copy-start(bf16[512,4096]{1,0:T(8,128)(2,1)} %w_ref.3) | copy-start | bytes 12582916
  20.7 7.2 %collective-permute-start.12 = (bf16[1056,128]{1,0:T(8,128)(2,1)S(1)}, bf16[1056,128]{1,0:T(8,128)(2,1)S(1)}, u32[]{:S(2)}, u32[]{:S(2)}) collective-permute-start(bf16[1056,128]{1,0:T(8,128)(2,1)S(1)} %get-tuple-element.42), channel_id=1, source_target_pairs={{0,128},{8,40},{16,144},{24,56},{32,160},{40,8},{48,176},{56,24},{... | collective-permute-start | bytes 811016 | tf_op jit(solution)/shard_map/ppermute | solution.py:226
  21.0 11.6 %collective-permute-start.11 = (bf16[528,128]{1,0:T(8,128)(2,1)S(1)}, bf16[528,128]{1,0:T(8,128)(2,1)S(1)}, u32[]{:S(2)}, u32[]{:S(2)}) collective-permute-start(bf16[528,128]{1,0:T(8,128)(2,1)S(1)} %get-tuple-element.41), channel_id=1, source_target_pairs={{0,192},{8,56},{16,208},{24,8},{32,224},{40,24},{48,240},{56,40},{... | collective-permute-start | bytes 405512 | tf_op jit(solution)/shard_map/ppermute | solution.py:226
  27.9 10.4 %collective-permute-start.16 = (bf16[1056,128]{1,0:T(8,128)(2,1)S(1)}, bf16[1056,128]{1,0:T(8,128)(2,1)S(1)}, u32[]{:S(2)}, u32[]{:S(2)}) collective-permute-start(bf16[1056,128]{1,0:T(8,128)(2,1)S(1)} %collective-permute-done.12.refs_2_), channel_id=1, source_target_pairs={{0,8},{8,0},{16,24},{24,16},{32,40},{40,32},{48,56},{56,48},{1,9},... | collective-permute-start | bytes 811016 | tf_op jit(solution)/shard_map/ppermute | solution.py:228
  29.2 5.7 %collective-permute-start.13 = (bf16[528,128]{1,0:T(8,128)(2,1)S(1)}, bf16[528,128]{1,0:T(8,128)(2,1)S(1)}, u32[]{:S(2)}, u32[]{:S(2)}) collective-permute-start(bf16[528,128]{1,0:T(8,128)(2,1)S(1)} %get-tuple-element.43), channel_id=1, source_target_pairs={{0,64},{8,24},{16,80},{24,40},{32,96},{40,56},{48,112},{56,8},{64,... | collective-permute-start | bytes 405512 | tf_op jit(solution)/shard_map/ppermute | solution.py:226
  29.7 5.2 %collective-permute-start.14 = (bf16[528,128]{1,0:T(8,128)(2,1)S(1)}, bf16[528,128]{1,0:T(8,128)(2,1)S(1)}, u32[]{:S(2)}, u32[]{:S(2)}) collective-permute-start(bf16[528,128]{1,0:T(8,128)(2,1)S(1)} %get-tuple-element.44), channel_id=1, source_target_pairs={{0,8},{8,0},{16,24},{24,16},{32,40},{40,32},{48,56},{56,48},{1,9},... | collective-permute-start | bytes 405512 | tf_op jit(solution)/shard_map/ppermute | solution.py:228
  30.9 4.4 %collective-permute-start.15 = (bf16[528,128]{1,0:T(8,128)(2,1)S(1)}, bf16[528,128]{1,0:T(8,128)(2,1)S(1)}, u32[]{:S(2)}, u32[]{:S(2)}) collective-permute-start(bf16[528,128]{1,0:T(8,128)(2,1)S(1)} %get-tuple-element.45), channel_id=1, source_target_pairs={{0,200},{8,48},{16,216},{24,0},{32,232},{40,16},{48,248},{56,32},{... | collective-permute-start | bytes 405512 | tf_op jit(solution)/shard_map/ppermute | solution.py:226
  32.6 5.6 %collective-permute-start.17 = (bf16[528,128]{1,0:T(8,128)(2,1)S(1)}, bf16[528,128]{1,0:T(8,128)(2,1)S(1)}, u32[]{:S(2)}, u32[]{:S(2)}) collective-permute-start(bf16[528,128]{1,0:T(8,128)(2,1)S(1)} %get-tuple-element.46), channel_id=1, source_target_pairs={{0,72},{8,16},{16,88},{24,32},{32,104},{40,48},{48,120},{56,0},{64... | collective-permute-start | bytes 405512 | tf_op jit(solution)/shard_map/ppermute | solution.py:226
  39.7 11.5 %collective-permute-start.24 = (bf16[64,2048]{1,0:T(8,128)(2,1)S(1)}, bf16[64,2048]{1,0:T(8,128)(2,1)S(1)}, u32[]{:S(2)}, u32[]{:S(2)}) collective-permute-start(bf16[64,2048]{1,0:T(8,128)(2,1)S(1)} %get-tuple-element.61), channel_id=1, source_target_pairs={{0,1},{1,2},{2,3},{3,4},{4,5},{5,6},{6,7},{7,0},{8,9},{9,10},{10,1... | collective-permute-start | bytes 786440 | tf_op jit(solution)/shard_map/ppermute | solution.py:229
  40.7 10.5 %collective-permute-start.25 = (bf16[64,2048]{1,0:T(8,128)(2,1)S(1)}, bf16[64,2048]{1,0:T(8,128)(2,1)S(1)}, u32[]{:S(2)}, u32[]{:S(2)}) collective-permute-start(bf16[64,2048]{1,0:T(8,128)(2,1)S(1)} %get-tuple-element.62), channel_id=1, source_target_pairs={{0,7},{1,0},{2,1},{3,2},{4,3},{5,4},{6,5},{7,6},{8,15},{9,8},{10,9... | collective-permute-start | bytes 786440 | tf_op jit(solution)/shard_map/ppermute | solution.py:229
  47.1 9.5 %collective-permute-start.18 = (bf16[64,2048]{1,0:T(8,128)(2,1)S(1)}, bf16[64,2048]{1,0:T(8,128)(2,1)S(1)}, u32[]{:S(2)}, u32[]{:S(2)}) collective-permute-start(bf16[64,2048]{1,0:T(8,128)(2,1)S(1)} %get-tuple-element.52), channel_id=1, source_target_pairs={{0,1},{1,2},{2,3},{3,4},{4,5},{5,6},{6,7},{7,0},{8,9},{9,10},{10,1... | collective-permute-start | bytes 786440 | tf_op jit(solution)/shard_map/ppermute | solution.py:229
  47.2 9.4 %collective-permute-start.19 = (bf16[64,2048]{1,0:T(8,128)(2,1)S(1)}, bf16[64,2048]{1,0:T(8,128)(2,1)S(1)}, u32[]{:S(2)}, u32[]{:S(2)}) collective-permute-start(bf16[64,2048]{1,0:T(8,128)(2,1)S(1)} %get-tuple-element.53), channel_id=1, source_target_pairs={{0,7},{1,0},{2,1},{3,2},{4,3},{5,4},{6,5},{7,6},{8,15},{9,8},{10,9... | collective-permute-start | bytes 786440 | tf_op jit(solution)/shard_map/ppermute | solution.py:229
  51.3 10.9 %collective-permute-start.26 = (bf16[64,2048]{1,0:T(8,128)(2,1)S(1)}, bf16[64,2048]{1,0:T(8,128)(2,1)S(1)}, u32[]{:S(2)}, u32[]{:S(2)}) collective-permute-start(bf16[64,2048]{1,0:T(8,128)(2,1)S(1)} %get-tuple-element.63), channel_id=1, source_target_pairs={{0,1},{1,2},{2,3},{3,4},{4,5},{5,6},{6,7},{7,0},{8,9},{9,10},{10,1... | collective-permute-start | bytes 786440 | tf_op jit(solution)/shard_map/ppermute | solution.py:229
  51.4 10.8 %collective-permute-start.27 = (bf16[64,2048]{1,0:T(8,128)(2,1)S(1)}, bf16[64,2048]{1,0:T(8,128)(2,1)S(1)}, u32[]{:S(2)}, u32[]{:S(2)}) collective-permute-start(bf16[64,2048]{1,0:T(8,128)(2,1)S(1)} %get-tuple-element.64), channel_id=1, source_target_pairs={{0,7},{1,0},{2,1},{3,2},{4,3},{5,4},{6,5},{7,6},{8,15},{9,8},{10,9... | collective-permute-start | bytes 786440 | tf_op jit(solution)/shard_map/ppermute | solution.py:229
  56.8 11.1 %collective-permute-start.20 = (bf16[64,2048]{1,0:T(8,128)(2,1)S(1)}, bf16[64,2048]{1,0:T(8,128)(2,1)S(1)}, u32[]{:S(2)}, u32[]{:S(2)}) collective-permute-start(bf16[64,2048]{1,0:T(8,128)(2,1)S(1)} %get-tuple-element.54), channel_id=1, source_target_pairs={{0,1},{1,2},{2,3},{3,4},{4,5},{5,6},{6,7},{7,0},{8,9},{9,10},{10,1... | collective-permute-start | bytes 786440 | tf_op jit(solution)/shard_map/ppermute | solution.py:229
  56.8 11.1 %collective-permute-start.21 = (bf16[64,2048]{1,0:T(8,128)(2,1)S(1)}, bf16[64,2048]{1,0:T(8,128)(2,1)S(1)}, u32[]{:S(2)}, u32[]{:S(2)}) collective-permute-start(bf16[64,2048]{1,0:T(8,128)(2,1)S(1)} %get-tuple-element.55), channel_id=1, source_target_pairs={{0,7},{1,0},{2,1},{3,2},{4,3},{5,4},{6,5},{7,6},{8,15},{9,8},{10,9... | collective-permute-start | bytes 786440 | tf_op jit(solution)/shard_map/ppermute | solution.py:229
  62.4 11.1 %collective-permute-start.28 = (bf16[64,2048]{1,0:T(8,128)(2,1)S(1)}, bf16[64,2048]{1,0:T(8,128)(2,1)S(1)}, u32[]{:S(2)}, u32[]{:S(2)}) collective-permute-start(bf16[64,2048]{1,0:T(8,128)(2,1)S(1)} %get-tuple-element.65), channel_id=1, source_target_pairs={{0,1},{1,2},{2,3},{3,4},{4,5},{5,6},{6,7},{7,0},{8,9},{9,10},{10,1... | collective-permute-start | bytes 786440 | tf_op jit(solution)/shard_map/ppermute | solution.py:229
  62.5 11.1 %collective-permute-start.29 = (bf16[64,2048]{1,0:T(8,128)(2,1)S(1)}, bf16[64,2048]{1,0:T(8,128)(2,1)S(1)}, u32[]{:S(2)}, u32[]{:S(2)}) collective-permute-start(bf16[64,2048]{1,0:T(8,128)(2,1)S(1)} %get-tuple-element.66), channel_id=1, source_target_pairs={{0,7},{1,0},{2,1},{3,2},{4,3},{5,4},{6,5},{7,6},{8,15},{9,8},{10,9... | collective-permute-start | bytes 786440 | tf_op jit(solution)/shard_map/ppermute | solution.py:229
  68.0 11.1 %collective-permute-start.22 = (bf16[64,2048]{1,0:T(8,128)(2,1)S(1)}, bf16[64,2048]{1,0:T(8,128)(2,1)S(1)}, u32[]{:S(2)}, u32[]{:S(2)}) collective-permute-start(bf16[64,2048]{1,0:T(8,128)(2,1)S(1)} %get-tuple-element.56), channel_id=1, source_target_pairs={{0,1},{1,2},{2,3},{3,4},{4,5},{5,6},{6,7},{7,0},{8,9},{9,10},{10,1... | collective-permute-start | bytes 786440 | tf_op jit(solution)/shard_map/ppermute | solution.py:229
  68.3 10.8 %collective-permute-start.23 = (bf16[64,2048]{1,0:T(8,128)(2,1)S(1)}, bf16[64,2048]{1,0:T(8,128)(2,1)S(1)}, u32[]{:S(2)}, u32[]{:S(2)}) collective-permute-start(bf16[64,2048]{1,0:T(8,128)(2,1)S(1)} %get-tuple-element.57), channel_id=1, source_target_pairs={{0,7},{1,0},{2,1},{3,2},{4,3},{5,4},{6,5},{7,6},{8,15},{9,8},{10,9... | collective-permute-start | bytes 786440 | tf_op jit(solution)/shard_map/ppermute | solution.py:229
  73.6 11.1 %collective-permute-start.30 = (bf16[64,2048]{1,0:T(8,128)(2,1)S(1)}, bf16[64,2048]{1,0:T(8,128)(2,1)S(1)}, u32[]{:S(2)}, u32[]{:S(2)}) collective-permute-start(bf16[64,2048]{1,0:T(8,128)(2,1)S(1)} %get-tuple-element.67), channel_id=1, source_target_pairs={{0,1},{1,2},{2,3},{3,4},{4,5},{5,6},{6,7},{7,0},{8,9},{9,10},{10,1... | collective-permute-start | bytes 786440 | tf_op jit(solution)/shard_map/ppermute | solution.py:229
  73.7 11.1 %collective-permute-start.31 = (bf16[64,2048]{1,0:T(8,128)(2,1)S(1)}, bf16[64,2048]{1,0:T(8,128)(2,1)S(1)}, u32[]{:S(2)}, u32[]{:S(2)}) collective-permute-start(bf16[64,2048]{1,0:T(8,128)(2,1)S(1)} %get-tuple-element.68), channel_id=1, source_target_pairs={{0,7},{1,0},{2,1},{3,2},{4,3},{5,4},{6,5},{7,6},{8,15},{9,8},{10,9... | collective-permute-start | bytes 786440 | tf_op jit(solution)/shard_map/ppermute | solution.py:229

commit v3 on v2

--- a/solution.py
+++ b/solution.py
@@ -268,7 +268,8 @@
         10**9,
         16,
     )(qf, out_weight, *(parts[d, c] for c in range(2) for d in range(4)))
-    right1, left0 = along_z(right1, 1), along_z(left0, -1)
+    right1 = along_z(right1, 1)
+    left0 = along_z(left0, -1)
     term = jax.ShapeDtypeStruct((128, half), F32)
     right0, left1, f3, e2, f2, e1, f1, own, _ = call(
         project_kernel,
@@ -282,7 +283,9 @@
 
     def hop(term, from_left, from_right):
         right, left = call(hop_kernel, (piece, piece), 10**8, 4)(term, from_left, from_right)
-        return along_z(right, 1), along_z(left, -1)
+        right = along_z(right, 1)
+        left = along_z(left, -1)
+        return right, left
 
     right1, left0 = hop(f3, right1, left0)
     right0, left1 = hop(e2, right0, left1)

time: 86 us -> 86 us (level)
  no operation moved by 1% of the time
where the time goes in v3:
time: 86 us; the launch traced here: 85.8 us
  starting transfers between devices  44.3 us (52%)
  waiting for transfers between devices  31.7 us (37%)
  Pallas kernels  6.78 us (8%)
  other arithmetic  2.67 us (3%)
    ppermute x14, starting transfers between devices, per_device(): lax.ppermute(a, 'gz', [(i, (i + d) % 8) for i in range(8)])  21.6 us
    ppermute x14, waiting for transfers between devices, per_device(): lax.ppermute(a, 'gz', [(i, (i + d) % 8) for i in range(8)])  20.4 us
    ppermute x11, starting transfers between devices, by_role(): return lax.ppermute(a, ('gx', 'gy'), pairs)  13.6 us
    ppermute x11, waiting for transfers between devices, by_role(): return lax.ppermute(a, ('gx', 'gy'), pairs)  10.6 us
    ppermute x7, starting transfers between devices, per_device(): to_mate = lambda a: lax.ppermute(a, 'gy', [(i, i ^ 1) for i in range(8)])  9.08 us
    pallas_call x1, Pallas kernels, per_device(): call(project_kernel, (piece, piece) + (term,) * 5 + (jax.ShapeDtypeStruct...  2.48 us
  transfers between devices with their start and end apart: 32, of which 16 were waited for; matrix products, arithmetic and copies ran while one was open for 3% of the time, Pallas kernels for 3%

profile of v3, /device:TPU:1, one launch (start us, length us, event | category | flops | bytes accessed | tf_op | source)
XLA Modules:
  0.0 85.8 jit_solution(3960983487043087895)
XLA Ops:
  0.0 3.2 %collective-permute-start = (s32[2,4,8]{2,1,0:T(4,128)}, s32[2,4,8]{2,1,0:T(4,128)S(1)}, u32[]{:S(2)}, u32[]{:S(2)}) collective-permute-start(s32[2,4,8]{2,1,0:T(4,128)} %own_ref.1), channel_id=1, source_target_pairs={{0,8},{8,0},{16,24},{24,16},{32,40},{40,32},{48,56},{56,48},{1,9},... | collective-permute-start | bytes 776 | tf_op jit(solution)/shard_map/ppermute | solution.py:228
  3.2 1.3 %fusion.4 = bf16[512,512]{1,0:T(8,128)(2,1)S(1)} fusion(bf16[512,512]{1,0:T(8,128)(2,1)} %param.6), kind=kLoop, calls=%fused_computation.10 | loop fusion | flops 1572864 | bytes 1048576 | tf_op jit(solution)/shard_map/convert_element_type | solution.py:27
  4.5 1.1 %pad_maximum_fusion.kv_ref = bf16[1024,512]{1,0:T(8,128)(2,1)S(1)} fusion(bf16[512,512]{1,0:T(8,128)(2,1)} %param.7, bf16[512,512]{1,0:T(8,128)(2,1)S(1)} %fusion.4), kind=kLoop, calls=%fused_computation.12 | loop fusion | flops 2097152 | bytes 2097152 | tf_op jit(solution)/shard_map/concatenate | solution.py:232
  5.6 0.4 shard_map.55
  6.2 2.7 %collective-permute-start.5 = (bf16[528,128]{1,0:T(8,128)(2,1)S(1)}, bf16[528,128]{1,0:T(8,128)(2,1)S(1)}, u32[]{:S(2)}, u32[]{:S(2)}) collective-permute-start(bf16[528,128]{1,0:T(8,128)(2,1)S(1)} %get-tuple-element.38.refs_4_), channel_id=1, source_target_pairs={{0,48},{8,200},{16,0},{24,216},{32,16},{40,232},{48,32},{56,248},{... | collective-permute-start | bytes 405512 | tf_op jit(solution)/shard_map/ppermute | solution.py:226
  8.8 0.3 collective-permute-start.9
  9.1 0.9 %collective-permute-start.8 = (bf16[528,128]{1,0:T(8,128)(2,1)S(1)}, bf16[528,128]{1,0:T(8,128)(2,1)S(1)}, u32[]{:S(2)}, u32[]{:S(2)}) collective-permute-start(bf16[528,128]{1,0:T(8,128)(2,1)S(1)} %get-tuple-element.39), channel_id=1, source_target_pairs={{0,72},{8,16},{16,88},{24,32},{32,104},{40,48},{48,120},{56,0},{64... | collective-permute-start | bytes 405512 | tf_op jit(solution)/shard_map/ppermute | solution.py:226
  10.0 1.6 %collective-permute-done.1.refs_6_ = bf16[528,128]{1,0:T(8,128)(2,1)S(1)} collective-permute-done((bf16[528,128]{1,0:T(8,128)(2,1)S(1)}, bf16[528,128]{1,0:T(8,128)(2,1)S(1)}, u32[]{:S(2)}, u32[]{:S(2)}) %collective-permute-start.1) | collective-permute-done | bytes 135200 | tf_op jit(solution)/shard_map/ppermute | solution.py:226
  11.5 0.9 %collective-permute-start.7 = (bf16[528,128]{1,0:T(8,128)(2,1)S(1)}, bf16[528,128]{1,0:T(8,128)(2,1)S(1)}, u32[]{:S(2)}, u32[]{:S(2)}) collective-permute-start(bf16[528,128]{1,0:T(8,128)(2,1)S(1)} %get-tuple-element.39), channel_id=1, source_target_pairs={{0,8},{8,0},{16,24},{24,16},{32,40},{40,32},{48,56},{56,48},{1,9},... | collective-permute-start | bytes 405512 | tf_op jit(solution)/shard_map/ppermute | solution.py:228
  12.4 0.5 collective-permute-start.2
  12.9 0.7 collective-permute-done.9.refs_11_
  13.6 0.3 collective-permute-start.6
  13.8 0.9 %collective-permute-done.8.refs_7_ = bf16[528,128]{1,0:T(8,128)(2,1)S(1)} collective-permute-done((bf16[528,128]{1,0:T(8,128)(2,1)S(1)}, bf16[528,128]{1,0:T(8,128)(2,1)S(1)}, u32[]{:S(2)}, u32[]{:S(2)}) %collective-permute-start.8) | collective-permute-done | bytes 135200 | tf_op jit(solution)/shard_map/ppermute | solution.py:226
  14.7 2.1 %collective-permute-start.10 = (bf16[528,128]{1,0:T(8,128)(2,1)S(1)}, bf16[528,128]{1,0:T(8,128)(2,1)S(1)}, u32[]{:S(2)}, u32[]{:S(2)}) collective-permute-start(bf16[528,128]{1,0:T(8,128)(2,1)S(1)} %collective-permute-done.9.refs_11_), channel_id=1, source_target_pairs={{0,48},{8,200},{16,0},{24,216},{32,16},{40,232},{48,32},{56,248},{... | collective-permute-start | bytes 405512 | tf_op jit(solution)/shard_map/ppermute | solution.py:226
  16.9 1.7 %collective-permute-start.4 = (bf16[528,128]{1,0:T(8,128)(2,1)S(1)}, bf16[528,128]{1,0:T(8,128)(2,1)S(1)}, u32[]{:S(2)}, u32[]{:S(2)}) collective-permute-start(bf16[528,128]{1,0:T(8,128)(2,1)S(1)} %collective-permute-done.3.refs_8_), channel_id=1, source_target_pairs={{0,8},{8,0},{16,24},{24,16},{32,40},{40,32},{48,56},{56,48},{1,9},... | collective-permute-start | bytes 405512 | tf_op jit(solution)/shard_map/ppermute | solution.py:228
  18.6 0.3 collective-permute-done.10.refs_9_
  18.9 0.7 collective-permute-done.4.refs_2_
  19.6 1.1 %shard_map.56 = (bf16[528,128]{1,0:T(8,128)(2,1)S(1)}, bf16[528,128]{1,0:T(8,128)(2,1)S(1)}, bf16[528,128]{1,0:T(8,128)(2,1)S(1)}, bf16[528,128]{1,0:T(8,128)(2,...) custom-call(f32[16,128]{1,0:T(8,128)S(1)} %get-tuple-element.37.refs_0_, ...), custom_call_target="tpu_custom_call" | custom-call | flops 1000000000 | bytes 3906250 | tf_op jit(solution)/shard_map/pallas_call | solution.py:250
  20.7 0.3 collective-permute-start.12
  21.0 4.2 %collective-permute-start.11 = (bf16[528,128]{1,0:T(8,128)(2,1)S(1)}, bf16[528,128]{1,0:T(8,128)(2,1)S(1)}, u32[]{:S(2)}, u32[]{:S(2)}) collective-permute-start(bf16[528,128]{1,0:T(8,128)(2,1)S(1)} %get-tuple-element.41), channel_id=1, source_target_pairs={{0,192},{8,56},{16,208},{24,8},{32,224},{40,24},{48,240},{56,40},{... | collective-permute-start | bytes 405512 | tf_op jit(solution)/shard_map/ppermute | solution.py:226
  25.2 2.7 %collective-permute-done.12.refs_2_ = bf16[1056,128]{1,0:T(8,128)(2,1)S(1)} collective-permute-done((bf16[1056,128]{1,0:T(8,128)(2,1)S(1)}, bf16[1056,128]{1,0:T(8,128)(2,1)S(1)}, u32[]{:S(2)}, u32[]{:S(2)}) %collective-permute-start.12) | collective-permute-done | bytes 270368 | tf_op jit(solution)/shard_map/ppermute | solution.py:226
  27.9 1.3 %collective-permute-start.16 = (bf16[1056,128]{1,0:T(8,128)(2,1)S(1)}, bf16[1056,128]{1,0:T(8,128)(2,1)S(1)}, u32[]{:S(2)}, u32[]{:S(2)}) collective-permute-start(bf16[1056,128]{1,0:T(8,128)(2,1)S(1)} %collective-permute-done.12.refs_2_), channel_id=1, source_target_pairs={{0,8},{8,0},{16,24},{24,16},{32,40},{40,32},{48,56},{56,48},{1,9},... | collective-permute-start | bytes 811016 | tf_op jit(solution)/shard_map/ppermute | solution.py:228
  29.2 0.5 collective-permute-start.13
  29.7 1.2 %collective-permute-start.14 = (bf16[528,128]{1,0:T(8,128)(2,1)S(1)}, bf16[528,128]{1,0:T(8,128)(2,1)S(1)}, u32[]{:S(2)}, u32[]{:S(2)}) collective-permute-start(bf16[528,128]{1,0:T(8,128)(2,1)S(1)} %get-tuple-element.44), channel_id=1, source_target_pairs={{0,8},{8,0},{16,24},{24,16},{32,40},{40,32},{48,56},{56,48},{1,9},... | collective-permute-start | bytes 405512 | tf_op jit(solution)/shard_map/ppermute | solution.py:228
  30.9 1.7 %collective-permute-start.15 = (bf16[528,128]{1,0:T(8,128)(2,1)S(1)}, bf16[528,128]{1,0:T(8,128)(2,1)S(1)}, u32[]{:S(2)}, u32[]{:S(2)}) collective-permute-start(bf16[528,128]{1,0:T(8,128)(2,1)S(1)} %get-tuple-element.45), channel_id=1, source_target_pairs={{0,200},{8,48},{16,216},{24,0},{32,232},{40,16},{48,248},{56,32},{... | collective-permute-start | bytes 405512 | tf_op jit(solution)/shard_map/ppermute | solution.py:226
  32.6 0.8 collective-permute-start.17
  33.7 1.2 %collective-permute-done.13.refs_3_ = bf16[528,128]{1,0:T(8,128)(2,1)S(1)} collective-permute-done((bf16[528,128]{1,0:T(8,128)(2,1)S(1)}, bf16[528,128]{1,0:T(8,128)(2,1)S(1)}, u32[]{:S(2)}, u32[]{:S(2)}) %collective-permute-start.13) | collective-permute-done | bytes 135200 | tf_op jit(solution)/shard_map/ppermute | solution.py:226
  34.9 0.4 collective-permute-done.15.refs_5_
  35.3 2.9 %collective-permute-done.17.refs_7_ = bf16[528,128]{1,0:T(8,128)(2,1)S(1)} collective-permute-done((bf16[528,128]{1,0:T(8,128)(2,1)S(1)}, bf16[528,128]{1,0:T(8,128)(2,1)S(1)}, u32[]{:S(2)}, u32[]{:S(2)}) %collective-permute-start.17) | collective-permute-done | bytes 135200 | tf_op jit(solution)/shard_map/ppermute | solution.py:226
  38.2 1.5 %shard_map.57 = (bf16[64,2048]{1,0:T(8,128)(2,1)S(1)}, bf16[64,2048]{1,0:T(8,128)(2,1)S(1)}, bf16[1024,128]{1,0:T(8,128)(2,1)S(1)}, bf16[1024,128]{1,0:T(8,128)(2,1)S(1)}, bf16[64,512]{1,0:T(8,128)(2,1)}) custom-call(bf16[512,512]{1,0:T(8,128)(2,1)S(1)} %fusion.1.qf_ref, bf16[512,4096]{1,0:T(8,128)(2,1)S(1)} %copy-done, ...), custom_call_target="tpu_custom_call" | custom-call | flops 1000000000 | bytes 3906250 | tf_op jit(solution)/shard_map/pallas_call | solution.py:265
  39.7 1.0 %collective-permute-start.24 = (bf16[64,2048]{1,0:T(8,128)(2,1)S(1)}, bf16[64,2048]{1,0:T(8,128)(2,1)S(1)}, u32[]{:S(2)}, u32[]{:S(2)}) collective-permute-start(bf16[64,2048]{1,0:T(8,128)(2,1)S(1)} %get-tuple-element.61), channel_id=1, source_target_pairs={{0,1},{1,2},{2,3},{3,4},{4,5},{5,6},{6,7},{7,0},{8,9},{9,10},{10,1... | collective-permute-start | bytes 786440 | tf_op jit(solution)/shard_map/ppermute | solution.py:229
  40.7 3.9 %collective-permute-start.25 = (bf16[64,2048]{1,0:T(8,128)(2,1)S(1)}, bf16[64,2048]{1,0:T(8,128)(2,1)S(1)}, u32[]{:S(2)}, u32[]{:S(2)}) collective-permute-start(bf16[64,2048]{1,0:T(8,128)(2,1)S(1)} %get-tuple-element.62), channel_id=1, source_target_pairs={{0,7},{1,0},{2,1},{3,2},{4,3},{5,4},{6,5},{7,6},{8,15},{9,8},{10,9... | collective-permute-start | bytes 786440 | tf_op jit(solution)/shard_map/ppermute | solution.py:229
  44.7 2.5 %shard_map.58 = (bf16[64,2048]{1,0:T(8,128)(2,1)S(1)}, bf16[64,2048]{1,0:T(8,128)(2,1)S(1)}, f32[128,2048]{1,0:T(8,128)S(1)}, f32[128,2048]{1,0:T(8,128)S(1)}, f...) custom-call(bf16[512,512]{1,0:T(8,128)(2,1)S(1)} %fusion.1.qf_ref, ...), custom_call_target="tpu_custom_call" | custom-call | flops 4000000000 | bytes 15625000 | tf_op jit(solution)/shard_map/pallas_call | solution.py:274
  47.2 2.7 %collective-permute-start.19 = (bf16[64,2048]{1,0:T(8,128)(2,1)S(1)}, bf16[64,2048]{1,0:T(8,128)(2,1)S(1)}, u32[]{:S(2)}, u32[]{:S(2)}) collective-permute-start(bf16[64,2048]{1,0:T(8,128)(2,1)S(1)} %get-tuple-element.53), channel_id=1, source_target_pairs={{0,7},{1,0},{2,1},{3,2},{4,3},{5,4},{6,5},{7,6},{8,15},{9,8},{10,9... | collective-permute-start | bytes 786440 | tf_op jit(solution)/shard_map/ppermute | solution.py:229
  49.9 1.3 %collective-permute-done.24.from_left_ref = bf16[64,2048]{1,0:T(8,128)(2,1)S(1)} collective-permute-done((bf16[64,2048]{1,0:T(8,128)(2,1)S(1)}, bf16[64,2048]{1,0:T(8,128)(2,1)S(1)}, u32[]{:S(2)}, u32[]{:S(2)}) %collective-permute-start.24) | collective-permute-done | bytes 262176 | tf_op jit(solution)/shard_map/ppermute | solution.py:229
  51.4 2.7 %collective-permute-start.27 = (bf16[64,2048]{1,0:T(8,128)(2,1)S(1)}, bf16[64,2048]{1,0:T(8,128)(2,1)S(1)}, u32[]{:S(2)}, u32[]{:S(2)}) collective-permute-start(bf16[64,2048]{1,0:T(8,128)(2,1)S(1)} %get-tuple-element.64), channel_id=1, source_target_pairs={{0,7},{1,0},{2,1},{3,2},{4,3},{5,4},{6,5},{7,6},{8,15},{9,8},{10,9... | collective-permute-start | bytes 786440 | tf_op jit(solution)/shard_map/ppermute | solution.py:229
  54.1 2.6 %collective-permute-done.18.from_left_ref = bf16[64,2048]{1,0:T(8,128)(2,1)S(1)} collective-permute-done((bf16[64,2048]{1,0:T(8,128)(2,1)S(1)}, bf16[64,2048]{1,0:T(8,128)(2,1)S(1)}, u32[]{:S(2)}, u32[]{:S(2)}) %collective-permute-start.18) | collective-permute-done | bytes 262176 | tf_op jit(solution)/shard_map/ppermute | solution.py:229
  56.8 2.7 %collective-permute-start.21 = (bf16[64,2048]{1,0:T(8,128)(2,1)S(1)}, bf16[64,2048]{1,0:T(8,128)(2,1)S(1)}, u32[]{:S(2)}, u32[]{:S(2)}) collective-permute-start(bf16[64,2048]{1,0:T(8,128)(2,1)S(1)} %get-tuple-element.55), channel_id=1, source_target_pairs={{0,7},{1,0},{2,1},{3,2},{4,3},{5,4},{6,5},{7,6},{8,15},{9,8},{10,9... | collective-permute-start | bytes 786440 | tf_op jit(solution)/shard_map/ppermute | solution.py:229
  59.5 2.8 %collective-permute-done.26.from_left_ref = bf16[64,2048]{1,0:T(8,128)(2,1)S(1)} collective-permute-done((bf16[64,2048]{1,0:T(8,128)(2,1)S(1)}, bf16[64,2048]{1,0:T(8,128)(2,1)S(1)}, u32[]{:S(2)}, u32[]{:S(2)}) %collective-permute-start.26) | collective-permute-done | bytes 262176 | tf_op jit(solution)/shard_map/ppermute | solution.py:229
  62.5 2.7 %collective-permute-start.29 = (bf16[64,2048]{1,0:T(8,128)(2,1)S(1)}, bf16[64,2048]{1,0:T(8,128)(2,1)S(1)}, u32[]{:S(2)}, u32[]{:S(2)}) collective-permute-start(bf16[64,2048]{1,0:T(8,128)(2,1)S(1)} %get-tuple-element.66), channel_id=1, source_target_pairs={{0,7},{1,0},{2,1},{3,2},{4,3},{5,4},{6,5},{7,6},{8,15},{9,8},{10,9... | collective-permute-start | bytes 786440 | tf_op jit(solution)/shard_map/ppermute | solution.py:229
  65.1 2.8 %collective-permute-done.20.from_left_ref = bf16[64,2048]{1,0:T(8,128)(2,1)S(1)} collective-permute-done((bf16[64,2048]{1,0:T(8,128)(2,1)S(1)}, bf16[64,2048]{1,0:T(8,128)(2,1)S(1)}, u32[]{:S(2)}, u32[]{:S(2)}) %collective-permute-start.20) | collective-permute-done | bytes 262176 | tf_op jit(solution)/shard_map/ppermute | solution.py:229
  68.0 0.3 collective-permute-start.22
  68.3 2.7 %collective-permute-start.23 = (bf16[64,2048]{1,0:T(8,128)(2,1)S(1)}, bf16[64,2048]{1,0:T(8,128)(2,1)S(1)}, u32[]{:S(2)}, u32[]{:S(2)}) collective-permute-start(bf16[64,2048]{1,0:T(8,128)(2,1)S(1)} %get-tuple-element.57), channel_id=1, source_target_pairs={{0,7},{1,0},{2,1},{3,2},{4,3},{5,4},{6,5},{7,6},{8,15},{9,8},{10,9... | collective-permute-start | bytes 786440 | tf_op jit(solution)/shard_map/ppermute | solution.py:229
  71.0 2.5 %collective-permute-done.28.from_left_ref = bf16[64,2048]{1,0:T(8,128)(2,1)S(1)} collective-permute-done((bf16[64,2048]{1,0:T(8,128)(2,1)S(1)}, bf16[64,2048]{1,0:T(8,128)(2,1)S(1)}, u32[]{:S(2)}, u32[]{:S(2)}) %collective-permute-start.28) | collective-permute-done | bytes 262176 | tf_op jit(solution)/shard_map/ppermute | solution.py:229
  73.7 2.7 %collective-permute-start.31 = (bf16[64,2048]{1,0:T(8,128)(2,1)S(1)}, bf16[64,2048]{1,0:T(8,128)(2,1)S(1)}, u32[]{:S(2)}, u32[]{:S(2)}) collective-permute-start(bf16[64,2048]{1,0:T(8,128)(2,1)S(1)} %get-tuple-element.68), channel_id=1, source_target_pairs={{0,7},{1,0},{2,1},{3,2},{4,3},{5,4},{6,5},{7,6},{8,15},{9,8},{10,9... | collective-permute-start | bytes 786440 | tf_op jit(solution)/shard_map/ppermute | solution.py:229
  76.4 2.8 %collective-permute-done.22.right0 = bf16[64,2048]{1,0:T(8,128)(2,1)S(1)} collective-permute-done((bf16[64,2048]{1,0:T(8,128)(2,1)S(1)}, bf16[64,2048]{1,0:T(8,128)(2,1)S(1)}, u32[]{:S(2)}, u32[]{:S(2)}) %collective-permute-start.22) | collective-permute-done | bytes 262176 | tf_op jit(solution)/shard_map/ppermute | solution.py:229
  79.1 5.6 %collective-permute-done.30.right1 = bf16[64,2048]{1,0:T(8,128)(2,1)S(1)} collective-permute-done((bf16[64,2048]{1,0:T(8,128)(2,1)S(1)}, bf16[64,2048]{1,0:T(8,128)(2,1)S(1)}, u32[]{:S(2)}, u32[]{:S(2)}) %collective-permute-start.30) | collective-permute-done | bytes 262176 | tf_op jit(solution)/shard_map/ppermute | solution.py:229
  84.8 0.9 %last.1 = bf16[64,4096]{1,0:T(8,128)(2,1)} custom-call(f32[64,4096]{1,0:T(8,128)S(1)} %get-tuple-element.49.own_ref, bf16[64,2048]{1,0:T(8,128)(2,1)S(1)} %collective-permute-done.22.right0, bf16[64,2048]{1,0:T(8,128)(2,1)S(1)} %collective-permute-done.23.left1, bf16[64,2048]{1,0:T(8,128)(2,1)S(1)} %collective-permute-done.30.right1, ...), custom_call_target="tpu_custom_call" | custom-call | flops 100000000 | bytes 1000000 | tf_op jit(solution)/shard_map/last/pallas_call | solution.py:295
  (35 shorter events, 1.3 us)
Async XLA Ops:
  0.0 5.6 %copy-start.1 = (s32[2,4,8]{2,1,0:T(4,128)S(1)}, s32[2,4,8]{2,1,0:T(4,128)}, u32[]{:S(2)}) copy-start(s32[2,4,8]{2,1,0:T(4,128)} %own_ref.1) | copy-start | bytes 772
  0.0 5.6 %collective-permute-start = (s32[2,4,8]{2,1,0:T(4,128)}, s32[2,4,8]{2,1,0:T(4,128)S(1)}, u32[]{:S(2)}, u32[]{:S(2)}) collective-permute-start(s32[2,4,8]{2,1,0:T(4,128)} %own_ref.1), channel_id=1, source_target_pairs={{0,8},{8,0},{16,24},{24,16},{32,40},{40,32},{48,56},{56,48},{1,9},... | collective-permute-start | bytes 776 | tf_op jit(solution)/shard_map/ppermute | solution.py:228
  6.1 27.4 %copy-start.2 = (bf16[512,512]{1,0:T(8,128)(2,1)S(1)}, bf16[512,512]{1,0:T(8,128)(2,1)}, u32[]{:S(2)}) copy-start(bf16[512,512]{1,0:T(8,128)(2,1)} %param.5) | copy-start | bytes 1572868
  6.1 5.4 %collective-permute-start.1 = (bf16[528,128]{1,0:T(8,128)(2,1)S(1)}, bf16[528,128]{1,0:T(8,128)(2,1)S(1)}, u32[]{:S(2)}, u32[]{:S(2)}) collective-permute-start(bf16[528,128]{1,0:T(8,128)(2,1)S(1)} %get-tuple-element.38.refs_4_), channel_id=1, source_target_pairs={{0,16},{8,72},{16,32},{24,88},{32,48},{40,104},{48,0},{56,120},{64... | collective-permute-start | bytes 405512 | tf_op jit(solution)/shard_map/ppermute | solution.py:226
  6.2 6.2 %collective-permute-start.5 = (bf16[528,128]{1,0:T(8,128)(2,1)S(1)}, bf16[528,128]{1,0:T(8,128)(2,1)S(1)}, u32[]{:S(2)}, u32[]{:S(2)}) collective-permute-start(bf16[528,128]{1,0:T(8,128)(2,1)S(1)} %get-tuple-element.38.refs_4_), channel_id=1, source_target_pairs={{0,48},{8,200},{16,0},{24,216},{32,16},{40,232},{48,32},{56,248},{... | collective-permute-start | bytes 405512 | tf_op jit(solution)/shard_map/ppermute | solution.py:226
  8.8 4.7 %collective-permute-start.9 = (bf16[528,128]{1,0:T(8,128)(2,1)S(1)}, bf16[528,128]{1,0:T(8,128)(2,1)S(1)}, u32[]{:S(2)}, u32[]{:S(2)}) collective-permute-start(bf16[528,128]{1,0:T(8,128)(2,1)S(1)} %get-tuple-element.39), channel_id=1, source_target_pairs={{0,200},{8,48},{16,216},{24,0},{32,232},{40,16},{48,248},{56,32},{... | collective-permute-start | bytes 405512 | tf_op jit(solution)/shard_map/ppermute | solution.py:226
  9.1 5.6 %collective-permute-start.8 = (bf16[528,128]{1,0:T(8,128)(2,1)S(1)}, bf16[528,128]{1,0:T(8,128)(2,1)S(1)}, u32[]{:S(2)}, u32[]{:S(2)}) collective-permute-start(bf16[528,128]{1,0:T(8,128)(2,1)S(1)} %get-tuple-element.39), channel_id=1, source_target_pairs={{0,72},{8,16},{16,88},{24,32},{32,104},{40,48},{48,120},{56,0},{64... | collective-permute-start | bytes 405512 | tf_op jit(solution)/shard_map/ppermute | solution.py:226
  11.5 5.4 %collective-permute-start.3 = (bf16[528,128]{1,0:T(8,128)(2,1)S(1)}, bf16[528,128]{1,0:T(8,128)(2,1)S(1)}, u32[]{:S(2)}, u32[]{:S(2)}) collective-permute-start(bf16[528,128]{1,0:T(8,128)(2,1)S(1)} %collective-permute-done.1.refs_6_), channel_id=1, source_target_pairs={{0,16},{8,72},{16,32},{24,88},{32,48},{40,104},{48,0},{56,120},{64... | collective-permute-start | bytes 405512 | tf_op jit(solution)/shard_map/ppermute | solution.py:226
  11.5 7.1 %collective-permute-start.7 = (bf16[528,128]{1,0:T(8,128)(2,1)S(1)}, bf16[528,128]{1,0:T(8,128)(2,1)S(1)}, u32[]{:S(2)}, u32[]{:S(2)}) collective-permute-start(bf16[528,128]{1,0:T(8,128)(2,1)S(1)} %get-tuple-element.39), channel_id=1, source_target_pairs={{0,8},{8,0},{16,24},{24,16},{32,40},{40,32},{48,56},{56,48},{1,9},... | collective-permute-start | bytes 405512 | tf_op jit(solution)/shard_map/ppermute | solution.py:228
  12.4 6.2 %collective-permute-start.2 = (bf16[528,128]{1,0:T(8,128)(2,1)S(1)}, bf16[528,128]{1,0:T(8,128)(2,1)S(1)}, u32[]{:S(2)}, u32[]{:S(2)}) collective-permute-start(bf16[528,128]{1,0:T(8,128)(2,1)S(1)} %collective-permute-done.1.refs_6_), channel_id=1, source_target_pairs={{0,8},{8,0},{16,24},{24,16},{32,40},{40,32},{48,56},{56,48},{1,9},... | collective-permute-start | bytes 405512 | tf_op jit(solution)/shard_map/ppermute | solution.py:228
  13.6 5.1 %collective-permute-start.6 = (bf16[528,128]{1,0:T(8,128)(2,1)S(1)}, bf16[528,128]{1,0:T(8,128)(2,1)S(1)}, u32[]{:S(2)}, u32[]{:S(2)}) collective-permute-start(bf16[528,128]{1,0:T(8,128)(2,1)S(1)} %collective-permute-done.5.refs_10_), channel_id=1, source_target_pairs={{0,8},{8,0},{16,24},{24,16},{32,40},{40,32},{48,56},{56,48},{1,9},... | collective-permute-start | bytes 405512 | tf_op jit(solution)/shard_map/ppermute | solution.py:228
  14.7 4.2 %collective-permute-start.10 = (bf16[528,128]{1,0:T(8,128)(2,1)S(1)}, bf16[528,128]{1,0:T(8,128)(2,1)S(1)}, u32[]{:S(2)}, u32[]{:S(2)}) collective-permute-start(bf16[528,128]{1,0:T(8,128)(2,1)S(1)} %collective-permute-done.9.refs_11_), channel_id=1, source_target_pairs={{0,48},{8,200},{16,0},{24,216},{32,16},{40,232},{48,32},{56,248},{... | collective-permute-start | bytes 405512 | tf_op jit(solution)/shard_map/ppermute | solution.py:226
  16.9 2.7 %collective-permute-start.4 = (bf16[528,128]{1,0:T(8,128)(2,1)S(1)}, bf16[528,128]{1,0:T(8,128)(2,1)S(1)}, u32[]{:S(2)}, u32[]{:S(2)}) collective-permute-start(bf16[528,128]{1,0:T(8,128)(2,1)S(1)} %collective-permute-done.3.refs_8_), channel_id=1, source_target_pairs={{0,8},{8,0},{16,24},{24,16},{32,40},{40,32},{48,56},{56,48},{1,9},... | collective-permute-start | bytes 405512 | tf_op jit(solution)/shard_map/ppermute | solution.py:228
  19.6 18.6 %copy-start = (bf16[512,4096]{1,0:T(8,128)(2,1)S(1)}, bf16[512,4096]{1,0:T(8,128)(2,1)}, u32[]{:S(2)}) copy-start(bf16[512,4096]{1,0:T(8,128)(2,1)} %w_ref.3) | copy-start | bytes 12582916
  20.7 7.2 %collective-permute-start.12 = (bf16[1056,128]{1,0:T(8,128)(2,1)S(1)}, bf16[1056,128]{1,0:T(8,128)(2,1)S(1)}, u32[]{:S(2)}, u32[]{:S(2)}) collective-permute-start(bf16[1056,128]{1,0:T(8,128)(2,1)S(1)} %get-tuple-element.42), channel_id=1, source_target_pairs={{0,128},{8,40},{16,144},{24,56},{32,160},{40,8},{48,176},{56,24},{... | collective-permute-start | bytes 811016 | tf_op jit(solution)/shard_map/ppermute | solution.py:226
  21.0 11.6 %collective-permute-start.11 = (bf16[528,128]{1,0:T(8,128)(2,1)S(1)}, bf16[528,128]{1,0:T(8,128)(2,1)S(1)}, u32[]{:S(2)}, u32[]{:S(2)}) collective-permute-start(bf16[528,128]{1,0:T(8,128)(2,1)S(1)} %get-tuple-element.41), channel_id=1, source_target_pairs={{0,192},{8,56},{16,208},{24,8},{32,224},{40,24},{48,240},{56,40},{... | collective-permute-start | bytes 405512 | tf_op jit(solution)/shard_map/ppermute | solution.py:226
  27.9 10.4 %collective-permute-start.16 = (bf16[1056,128]{1,0:T(8,128)(2,1)S(1)}, bf16[1056,128]{1,0:T(8,128)(2,1)S(1)}, u32[]{:S(2)}, u32[]{:S(2)}) collective-permute-start(bf16[1056,128]{1,0:T(8,128)(2,1)S(1)} %collective-permute-done.12.refs_2_), channel_id=1, source_target_pairs={{0,8},{8,0},{16,24},{24,16},{32,40},{40,32},{48,56},{56,48},{1,9},... | collective-permute-start | bytes 811016 | tf_op jit(solution)/shard_map/ppermute | solution.py:228
  29.2 5.7 %collective-permute-start.13 = (bf16[528,128]{1,0:T(8,128)(2,1)S(1)}, bf16[528,128]{1,0:T(8,128)(2,1)S(1)}, u32[]{:S(2)}, u32[]{:S(2)}) collective-permute-start(bf16[528,128]{1,0:T(8,128)(2,1)S(1)} %get-tuple-element.43), channel_id=1, source_target_pairs={{0,64},{8,24},{16,80},{24,40},{32,96},{40,56},{48,112},{56,8},{64,... | collective-permute-start | bytes 405512 | tf_op jit(solution)/shard_map/ppermute | solution.py:226
  29.7 5.2 %collective-permute-start.14 = (bf16[528,128]{1,0:T(8,128)(2,1)S(1)}, bf16[528,128]{1,0:T(8,128)(2,1)S(1)}, u32[]{:S(2)}, u32[]{:S(2)}) collective-permute-start(bf16[528,128]{1,0:T(8,128)(2,1)S(1)} %get-tuple-element.44), channel_id=1, source_target_pairs={{0,8},{8,0},{16,24},{24,16},{32,40},{40,32},{48,56},{56,48},{1,9},... | collective-permute-start | bytes 405512 | tf_op jit(solution)/shard_map/ppermute | solution.py:228
  30.9 4.4 %collective-permute-start.15 = (bf16[528,128]{1,0:T(8,128)(2,1)S(1)}, bf16[528,128]{1,0:T(8,128)(2,1)S(1)}, u32[]{:S(2)}, u32[]{:S(2)}) collective-permute-start(bf16[528,128]{1,0:T(8,128)(2,1)S(1)} %get-tuple-element.45), channel_id=1, source_target_pairs={{0,200},{8,48},{16,216},{24,0},{32,232},{40,16},{48,248},{56,32},{... | collective-permute-start | bytes 405512 | tf_op jit(solution)/shard_map/ppermute | solution.py:226
  32.6 5.6 %collective-permute-start.17 = (bf16[528,128]{1,0:T(8,128)(2,1)S(1)}, bf16[528,128]{1,0:T(8,128)(2,1)S(1)}, u32[]{:S(2)}, u32[]{:S(2)}) collective-permute-start(bf16[528,128]{1,0:T(8,128)(2,1)S(1)} %get-tuple-element.46), channel_id=1, source_target_pairs={{0,72},{8,16},{16,88},{24,32},{32,104},{40,48},{48,120},{56,0},{64... | collective-permute-start | bytes 405512 | tf_op jit(solution)/shard_map/ppermute | solution.py:226
  39.7 11.5 %collective-permute-start.24 = (bf16[64,2048]{1,0:T(8,128)(2,1)S(1)}, bf16[64,2048]{1,0:T(8,128)(2,1)S(1)}, u32[]{:S(2)}, u32[]{:S(2)}) collective-permute-start(bf16[64,2048]{1,0:T(8,128)(2,1)S(1)} %get-tuple-element.61), channel_id=1, source_target_pairs={{0,1},{1,2},{2,3},{3,4},{4,5},{5,6},{6,7},{7,0},{8,9},{9,10},{10,1... | collective-permute-start | bytes 786440 | tf_op jit(solution)/shard_map/ppermute | solution.py:229
  40.7 10.5 %collective-permute-start.25 = (bf16[64,2048]{1,0:T(8,128)(2,1)S(1)}, bf16[64,2048]{1,0:T(8,128)(2,1)S(1)}, u32[]{:S(2)}, u32[]{:S(2)}) collective-permute-start(bf16[64,2048]{1,0:T(8,128)(2,1)S(1)} %get-tuple-element.62), channel_id=1, source_target_pairs={{0,7},{1,0},{2,1},{3,2},{4,3},{5,4},{6,5},{7,6},{8,15},{9,8},{10,9... | collective-permute-start | bytes 786440 | tf_op jit(solution)/shard_map/ppermute | solution.py:229
  47.1 9.5 %collective-permute-start.18 = (bf16[64,2048]{1,0:T(8,128)(2,1)S(1)}, bf16[64,2048]{1,0:T(8,128)(2,1)S(1)}, u32[]{:S(2)}, u32[]{:S(2)}) collective-permute-start(bf16[64,2048]{1,0:T(8,128)(2,1)S(1)} %get-tuple-element.52), channel_id=1, source_target_pairs={{0,1},{1,2},{2,3},{3,4},{4,5},{5,6},{6,7},{7,0},{8,9},{9,10},{10,1... | collective-permute-start | bytes 786440 | tf_op jit(solution)/shard_map/ppermute | solution.py:229
  47.2 9.4 %collective-permute-start.19 = (bf16[64,2048]{1,0:T(8,128)(2,1)S(1)}, bf16[64,2048]{1,0:T(8,128)(2,1)S(1)}, u32[]{:S(2)}, u32[]{:S(2)}) collective-permute-start(bf16[64,2048]{1,0:T(8,128)(2,1)S(1)} %get-tuple-element.53), channel_id=1, source_target_pairs={{0,7},{1,0},{2,1},{3,2},{4,3},{5,4},{6,5},{7,6},{8,15},{9,8},{10,9... | collective-permute-start | bytes 786440 | tf_op jit(solution)/shard_map/ppermute | solution.py:229
  51.3 10.9 %collective-permute-start.26 = (bf16[64,2048]{1,0:T(8,128)(2,1)S(1)}, bf16[64,2048]{1,0:T(8,128)(2,1)S(1)}, u32[]{:S(2)}, u32[]{:S(2)}) collective-permute-start(bf16[64,2048]{1,0:T(8,128)(2,1)S(1)} %get-tuple-element.63), channel_id=1, source_target_pairs={{0,1},{1,2},{2,3},{3,4},{4,5},{5,6},{6,7},{7,0},{8,9},{9,10},{10,1... | collective-permute-start | bytes 786440 | tf_op jit(solution)/shard_map/ppermute | solution.py:229
  51.4 10.8 %collective-permute-start.27 = (bf16[64,2048]{1,0:T(8,128)(2,1)S(1)}, bf16[64,2048]{1,0:T(8,128)(2,1)S(1)}, u32[]{:S(2)}, u32[]{:S(2)}) collective-permute-start(bf16[64,2048]{1,0:T(8,128)(2,1)S(1)} %get-tuple-element.64), channel_id=1, source_target_pairs={{0,7},{1,0},{2,1},{3,2},{4,3},{5,4},{6,5},{7,6},{8,15},{9,8},{10,9... | collective-permute-start | bytes 786440 | tf_op jit(solution)/shard_map/ppermute | solution.py:229
  56.8 11.1 %collective-permute-start.20 = (bf16[64,2048]{1,0:T(8,128)(2,1)S(1)}, bf16[64,2048]{1,0:T(8,128)(2,1)S(1)}, u32[]{:S(2)}, u32[]{:S(2)}) collective-permute-start(bf16[64,2048]{1,0:T(8,128)(2,1)S(1)} %get-tuple-element.54), channel_id=1, source_target_pairs={{0,1},{1,2},{2,3},{3,4},{4,5},{5,6},{6,7},{7,0},{8,9},{9,10},{10,1... | collective-permute-start | bytes 786440 | tf_op jit(solution)/shard_map/ppermute | solution.py:229
  56.8 11.1 %collective-permute-start.21 = (bf16[64,2048]{1,0:T(8,128)(2,1)S(1)}, bf16[64,2048]{1,0:T(8,128)(2,1)S(1)}, u32[]{:S(2)}, u32[]{:S(2)}) collective-permute-start(bf16[64,2048]{1,0:T(8,128)(2,1)S(1)} %get-tuple-element.55), channel_id=1, source_target_pairs={{0,7},{1,0},{2,1},{3,2},{4,3},{5,4},{6,5},{7,6},{8,15},{9,8},{10,9... | collective-permute-start | bytes 786440 | tf_op jit(solution)/shard_map/ppermute | solution.py:229
  62.4 11.1 %collective-permute-start.28 = (bf16[64,2048]{1,0:T(8,128)(2,1)S(1)}, bf16[64,2048]{1,0:T(8,128)(2,1)S(1)}, u32[]{:S(2)}, u32[]{:S(2)}) collective-permute-start(bf16[64,2048]{1,0:T(8,128)(2,1)S(1)} %get-tuple-element.65), channel_id=1, source_target_pairs={{0,1},{1,2},{2,3},{3,4},{4,5},{5,6},{6,7},{7,0},{8,9},{9,10},{10,1... | collective-permute-start | bytes 786440 | tf_op jit(solution)/shard_map/ppermute | solution.py:229
  62.5 11.1 %collective-permute-start.29 = (bf16[64,2048]{1,0:T(8,128)(2,1)S(1)}, bf16[64,2048]{1,0:T(8,128)(2,1)S(1)}, u32[]{:S(2)}, u32[]{:S(2)}) collective-permute-start(bf16[64,2048]{1,0:T(8,128)(2,1)S(1)} %get-tuple-element.66), channel_id=1, source_target_pairs={{0,7},{1,0},{2,1},{3,2},{4,3},{5,4},{6,5},{7,6},{8,15},{9,8},{10,9... | collective-permute-start | bytes 786440 | tf_op jit(solution)/shard_map/ppermute | solution.py:229
  68.0 11.1 %collective-permute-start.22 = (bf16[64,2048]{1,0:T(8,128)(2,1)S(1)}, bf16[64,2048]{1,0:T(8,128)(2,1)S(1)}, u32[]{:S(2)}, u32[]{:S(2)}) collective-permute-start(bf16[64,2048]{1,0:T(8,128)(2,1)S(1)} %get-tuple-element.56), channel_id=1, source_target_pairs={{0,1},{1,2},{2,3},{3,4},{4,5},{5,6},{6,7},{7,0},{8,9},{9,10},{10,1... | collective-permute-start | bytes 786440 | tf_op jit(solution)/shard_map/ppermute | solution.py:229
  68.3 10.8 %collective-permute-start.23 = (bf16[64,2048]{1,0:T(8,128)(2,1)S(1)}, bf16[64,2048]{1,0:T(8,128)(2,1)S(1)}, u32[]{:S(2)}, u32[]{:S(2)}) collective-permute-start(bf16[64,2048]{1,0:T(8,128)(2,1)S(1)} %get-tuple-element.57), channel_id=1, source_target_pairs={{0,7},{1,0},{2,1},{3,2},{4,3},{5,4},{6,5},{7,6},{8,15},{9,8},{10,9... | collective-permute-start | bytes 786440 | tf_op jit(solution)/shard_map/ppermute | solution.py:229
  73.6 11.1 %collective-permute-start.30 = (bf16[64,2048]{1,0:T(8,128)(2,1)S(1)}, bf16[64,2048]{1,0:T(8,128)(2,1)S(1)}, u32[]{:S(2)}, u32[]{:S(2)}) collective-permute-start(bf16[64,2048]{1,0:T(8,128)(2,1)S(1)} %get-tuple-element.67), channel_id=1, source_target_pairs={{0,1},{1,2},{2,3},{3,4},{4,5},{5,6},{6,7},{7,0},{8,9},{9,10},{10,1... | collective-permute-start | bytes 786440 | tf_op jit(solution)/shard_map/ppermute | solution.py:229
  73.7 11.1 %collective-permute-start.31 = (bf16[64,2048]{1,0:T(8,128)(2,1)S(1)}, bf16[64,2048]{1,0:T(8,128)(2,1)S(1)}, u32[]{:S(2)}, u32[]{:S(2)}) collective-permute-start(bf16[64,2048]{1,0:T(8,128)(2,1)S(1)} %get-tuple-element.68), channel_id=1, source_target_pairs={{0,7},{1,0},{2,1},{3,2},{4,3},{5,4},{6,5},{7,6},{8,15},{9,8},{10,9... | collective-permute-start | bytes 786440 | tf_op jit(solution)/shard_map/ppermute | solution.py:229

commit v4 on v3

--- a/solution.py
+++ b/solution.py
@@ -144,10 +144,39 @@
     return (num / lax.dot_general(q, sums, dims, preferred_element_type=F32)).astype(BF16)
 
 
+def both_sides(refs):
+    sides = (refs[:4], refs[4:8])
+    return [[*p[:2], p[2].at[side * ROWS : (side + 1) * ROWS], p[3]] for side, p in enumerate(sides)]
+
+
 def far_kernel(qf_ref, w_ref, *refs):
-    parts, (right_ref, left_ref, state_ref, sums_ref, att_ref) = (refs[:4], refs[4:8]), refs[8:]
+    parts, (right_ref, left_ref, state_ref, sums_ref, att_ref) = both_sides(refs[:8]), refs[8:]
     core, far = lax.rem(lax.axis_index("gy"), 2), lax.rem(lax.axis_index("gz") + 4, 8)
-    parts = [[*p[:2], p[2].at[side * ROWS : (side + 1) * ROWS], p[3]] for side, p in enumerate(parts)]
+    block = far // 4
+    for side in range(2):
+        role = core if side == 0 else 1 - core
+        tail = sum(p[STATES:, :].astype(F32) for p in parts[side])
+        for hh in range(2):
+            unit = pl.ds(pl.multiple_of((block * 2 + hh) * HD, HD), HD)
+            total = sum(p[unit, :].astype(F32) for p in parts[side])
+            to = pl.ds(pl.multiple_of((2 * role + hh) * HD, HD), HD)
+            state_ref[to, :] = total.astype(BF16)
+            first, second = (tail[2 * u : 2 * u + 1] + tail[2 * u + 1 : 2 * u + 2] for u in (hh, 2 + hh))
+            key_sum = jnp.where(block == 0, first, second)
+            sums_ref[to, :] = jnp.broadcast_to(key_sum, (HD, HD)).astype(BF16)
+    for h in range(4):
+        at, columns = pl.ds(h * HD, HD), slice(h * HD, (h + 1) * HD)
+        att_ref[:, columns] = attend(qf_ref, state_ref, sums_ref, at, chunk_rows(far), columns)
+    half = w_ref.shape[1] // 2
+    right_ref[...] = jnp.dot(att_ref[...], w_ref[:, half:], preferred_element_type=F32).astype(BF16)
+    left_ref[...] = jnp.dot(att_ref[...], w_ref[:, :half], preferred_element_type=F32).astype(BF16)
+
+
+def project_kernel(qf_ref, w_ref, far_ref, *refs):
+    parts = both_sides(refs[:8])
+    r3_ref, l3_ref, f3_ref, e2_ref, f2_ref, e1_ref, f1_ref, own_ref = refs[8:16]
+    att_ref, state_ref, sums_ref = refs[16:]
+    gz, core = lax.axis_index("gz"), lax.rem(lax.axis_index("gy"), 2)
     for side in range(2):
         role = core if side == 0 else 1 - core
         tail = sum(p[STATES:, :].astype(F32) for p in parts[side])
@@ -157,18 +186,6 @@
             state_ref[to, :] = total.astype(BF16)
             key_sum = tail[2 * u : 2 * u + 1] + tail[2 * u + 1 : 2 * u + 2]
             sums_ref[to, :] = jnp.broadcast_to(key_sum, (HD, HD)).astype(BF16)
-    for h in range(4):
-        at = pl.ds(pl.multiple_of((far // 4 * 4 + h) * HD, HD), HD)
-        columns = slice(h * HD, (h + 1) * HD)
-        att_ref[:, columns] = attend(qf_ref, state_ref, sums_ref, at, chunk_rows(far), columns)
-    half = w_ref.shape[1] // 2
-    right_ref[...] = jnp.dot(att_ref[...], w_ref[:, half:], preferred_element_type=F32).astype(BF16)
-    left_ref[...] = jnp.dot(att_ref[...], w_ref[:, :half], preferred_element_type=F32).astype(BF16)
-
-
-def project_kernel(qf_ref, w_ref, state_ref, sums_ref, *refs):
-    r3_ref, l3_ref, f3_ref, e2_ref, f2_ref, e1_ref, f1_ref, own_ref, att_ref = refs
-    gz = lax.axis_index("gz")
     for b in range(2):
         for h in range(4):
             at, columns = pl.ds((b * 4 + h) * HD, HD), slice(h * HD, (h + 1) * HD)
@@ -262,23 +279,25 @@
     half = out_weight.shape[1] // 2
     piece = jax.ShapeDtypeStruct((64, half), BF16)
     heads = jax.ShapeDtypeStruct((8 * HD, HD), BF16)
-    right1, left0, states, sums, _ = call(
+    few = jax.ShapeDtypeStruct((4 * HD, HD), BF16)
+    summed = [parts[d, c] for c in range(2) for d in range(4)]
+    right1, left0, states, _, _ = call(
         far_kernel,
-        (piece, piece, heads, heads, jax.ShapeDtypeStruct((64, queries.shape[1]), BF16)),
+        (piece, piece, few, few, jax.ShapeDtypeStruct((64, queries.shape[1]), BF16)),
         10**9,
         16,
-    )(qf, out_weight, *(parts[d, c] for c in range(2) for d in range(4)))
+    )(qf, out_weight, *summed)
     right1 = along_z(right1, 1)
     left0 = along_z(left0, -1)
     term = jax.ShapeDtypeStruct((128, half), F32)
-    right0, left1, f3, e2, f2, e1, f1, own, _ = call(
+    right0, left1, f3, e2, f2, e1, f1, own, *_ = call(
         project_kernel,
         (piece, piece)
         + (term,) * 5
-        + (jax.ShapeDtypeStruct((64, 2 * half), F32), jax.ShapeDtypeStruct(queries.shape, BF16)),
+        + (jax.ShapeDtypeStruct((64, 2 * half), F32), jax.ShapeDtypeStruct(queries.shape, BF16), heads, heads),
         4 * 10**9,
         20,
-    )(qf, out_weight, states, sums)
+    )(qf, out_weight, states, *summed)
     right0, left1 = along_z(right0, 1), along_z(left1, -1)
 
     def hop(term, from_left, from_right):

time: 86 us -> 85.8 us (level)
  waiting for transfers between devices: 31.7 us -> 30.8 us
  transfers between devices with their start and end apart: 32 -> 32, of which waited for: 16 -> 16; matrix products, arithmetic and copies ran while one was open for 3% -> 3% of each run, Pallas kernels for 3% -> 4%
where the time goes in v4:
time: 85.8 us; the launch traced here: 85.6 us
  starting transfers between devices  44.2 us (52%)
  waiting for transfers between devices  30.8 us (36%)
  Pallas kernels  7.53 us (9%)
  other arithmetic  2.67 us (3%)
    ppermute x14, starting transfers between devices, per_device(): lax.ppermute(a, 'gz', [(i, (i + d) % 8) for i in range(8)])  21.6 us
    ppermute x14, waiting for transfers between devices, per_device(): lax.ppermute(a, 'gz', [(i, (i + d) % 8) for i in range(8)])  19.5 us
    ppermute x11, starting transfers between devices, by_role(): return lax.ppermute(a, ('gx', 'gy'), pairs)  13.6 us
    ppermute x11, waiting for transfers between devices, by_role(): return lax.ppermute(a, ('gx', 'gy'), pairs)  10.6 us
    ppermute x7, starting transfers between devices, per_device(): to_mate = lambda a: lax.ppermute(a, 'gy', [(i, i ^ 1) for i in range(8)])  9.08 us
    pallas_call x1, Pallas kernels, per_device(): call(project_kernel, (piece, piece) + (term,) * 5 + (jax.ShapeDtypeStruct...  3.18 us
  transfers between devices with their start and end apart: 32, of which 16 were waited for; matrix products, arithmetic and copies ran while one was open for 3% of the time, Pallas kernels for 4%

profile of v4, /device:TPU:1, one launch (start us, length us, event | category | flops | bytes accessed | tf_op | source)
XLA Modules:
  0.0 85.6 jit_solution(14219163187256438011)
XLA Ops:
  0.0 3.2 %collective-permute-start = (s32[2,4,8]{2,1,0:T(4,128)}, s32[2,4,8]{2,1,0:T(4,128)S(1)}, u32[]{:S(2)}, u32[]{:S(2)}) collective-permute-start(s32[2,4,8]{2,1,0:T(4,128)} %own_ref.1), channel_id=1, source_target_pairs={{0,8},{8,0},{16,24},{24,16},{32,40},{40,32},{48,56},{56,48},{1,9},... | collective-permute-start | bytes 776 | tf_op jit(solution)/shard_map/ppermute | solution.py:245
  3.2 1.3 %fusion.4 = bf16[512,512]{1,0:T(8,128)(2,1)S(1)} fusion(bf16[512,512]{1,0:T(8,128)(2,1)} %param.6), kind=kLoop, calls=%fused_computation.10 | loop fusion | flops 1572864 | bytes 1048576 | tf_op jit(solution)/shard_map/convert_element_type | solution.py:27
  4.5 1.1 %pad_maximum_fusion.kv_ref = bf16[1024,512]{1,0:T(8,128)(2,1)S(1)} fusion(bf16[512,512]{1,0:T(8,128)(2,1)} %param.7, bf16[512,512]{1,0:T(8,128)(2,1)S(1)} %fusion.4), kind=kLoop, calls=%fused_computation.12 | loop fusion | flops 2097152 | bytes 2097152 | tf_op jit(solution)/shard_map/concatenate | solution.py:249
  5.6 0.4 shard_map.55
  6.2 2.7 %collective-permute-start.5 = (bf16[528,128]{1,0:T(8,128)(2,1)S(1)}, bf16[528,128]{1,0:T(8,128)(2,1)S(1)}, u32[]{:S(2)}, u32[]{:S(2)}) collective-permute-start(bf16[528,128]{1,0:T(8,128)(2,1)S(1)} %get-tuple-element.37.refs_4_), channel_id=1, source_target_pairs={{0,48},{8,200},{16,0},{24,216},{32,16},{40,232},{48,32},{56,248},{... | collective-permute-start | bytes 405512 | tf_op jit(solution)/shard_map/ppermute | solution.py:243
  8.8 0.3 collective-permute-start.9
  9.1 0.9 %collective-permute-start.8 = (bf16[528,128]{1,0:T(8,128)(2,1)S(1)}, bf16[528,128]{1,0:T(8,128)(2,1)S(1)}, u32[]{:S(2)}, u32[]{:S(2)}) collective-permute-start(bf16[528,128]{1,0:T(8,128)(2,1)S(1)} %get-tuple-element.38), channel_id=1, source_target_pairs={{0,72},{8,16},{16,88},{24,32},{32,104},{40,48},{48,120},{56,0},{64... | collective-permute-start | bytes 405512 | tf_op jit(solution)/shard_map/ppermute | solution.py:243
  10.0 1.6 %collective-permute-done.1.refs_6_ = bf16[528,128]{1,0:T(8,128)(2,1)S(1)} collective-permute-done((bf16[528,128]{1,0:T(8,128)(2,1)S(1)}, bf16[528,128]{1,0:T(8,128)(2,1)S(1)}, u32[]{:S(2)}, u32[]{:S(2)}) %collective-permute-start.1) | collective-permute-done | bytes 135200 | tf_op jit(solution)/shard_map/ppermute | solution.py:243
  11.5 0.9 %collective-permute-start.7 = (bf16[528,128]{1,0:T(8,128)(2,1)S(1)}, bf16[528,128]{1,0:T(8,128)(2,1)S(1)}, u32[]{:S(2)}, u32[]{:S(2)}) collective-permute-start(bf16[528,128]{1,0:T(8,128)(2,1)S(1)} %get-tuple-element.38), channel_id=1, source_target_pairs={{0,8},{8,0},{16,24},{24,16},{32,40},{40,32},{48,56},{56,48},{1,9},... | collective-permute-start | bytes 405512 | tf_op jit(solution)/shard_map/ppermute | solution.py:245
  12.4 0.5 collective-permute-start.2
  12.9 0.7 collective-permute-done.9.refs_11_
  13.6 0.3 collective-permute-start.6
  13.8 0.9 %collective-permute-done.8.refs_7_ = bf16[528,128]{1,0:T(8,128)(2,1)S(1)} collective-permute-done((bf16[528,128]{1,0:T(8,128)(2,1)S(1)}, bf16[528,128]{1,0:T(8,128)(2,1)S(1)}, u32[]{:S(2)}, u32[]{:S(2)}) %collective-permute-start.8) | collective-permute-done | bytes 135200 | tf_op jit(solution)/shard_map/ppermute | solution.py:243
  14.7 2.1 %collective-permute-start.10 = (bf16[528,128]{1,0:T(8,128)(2,1)S(1)}, bf16[528,128]{1,0:T(8,128)(2,1)S(1)}, u32[]{:S(2)}, u32[]{:S(2)}) collective-permute-start(bf16[528,128]{1,0:T(8,128)(2,1)S(1)} %collective-permute-done.9.refs_11_), channel_id=1, source_target_pairs={{0,48},{8,200},{16,0},{24,216},{32,16},{40,232},{48,32},{56,248},{... | collective-permute-start | bytes 405512 | tf_op jit(solution)/shard_map/ppermute | solution.py:243
  16.9 1.7 %collective-permute-start.4 = (bf16[528,128]{1,0:T(8,128)(2,1)S(1)}, bf16[528,128]{1,0:T(8,128)(2,1)S(1)}, u32[]{:S(2)}, u32[]{:S(2)}) collective-permute-start(bf16[528,128]{1,0:T(8,128)(2,1)S(1)} %collective-permute-done.3.refs_8_), channel_id=1, source_target_pairs={{0,8},{8,0},{16,24},{24,16},{32,40},{40,32},{48,56},{56,48},{1,9},... | collective-permute-start | bytes 405512 | tf_op jit(solution)/shard_map/ppermute | solution.py:245
  18.6 0.3 collective-permute-done.10.refs_9_
  18.9 0.7 collective-permute-done.4.refs_2_
  19.6 1.1 %shard_map.56 = (bf16[528,128]{1,0:T(8,128)(2,1)S(1)}, bf16[528,128]{1,0:T(8,128)(2,1)S(1)}, bf16[528,128]{1,0:T(8,128)(2,1)S(1)}, bf16[528,128]{1,0:T(8,128)(2,...) custom-call(f32[16,128]{1,0:T(8,128)S(1)} %get-tuple-element.36.refs_0_, ...), custom_call_target="tpu_custom_call" | custom-call | flops 1000000000 | bytes 3906250 | tf_op jit(solution)/shard_map/pallas_call | solution.py:267
  20.7 0.3 collective-permute-start.12
  21.0 4.2 %collective-permute-start.11 = (bf16[528,128]{1,0:T(8,128)(2,1)S(1)}, bf16[528,128]{1,0:T(8,128)(2,1)S(1)}, u32[]{:S(2)}, u32[]{:S(2)}) collective-permute-start(bf16[528,128]{1,0:T(8,128)(2,1)S(1)} %get-tuple-element.40), channel_id=1, source_target_pairs={{0,192},{8,56},{16,208},{24,8},{32,224},{40,24},{48,240},{56,40},{... | collective-permute-start | bytes 405512 | tf_op jit(solution)/shard_map/ppermute | solution.py:243
  25.2 2.7 %collective-permute-done.12.refs_2_ = bf16[1056,128]{1,0:T(8,128)(2,1)S(1)} collective-permute-done((bf16[1056,128]{1,0:T(8,128)(2,1)S(1)}, bf16[1056,128]{1,0:T(8,128)(2,1)S(1)}, u32[]{:S(2)}, u32[]{:S(2)}) %collective-permute-start.12) | collective-permute-done | bytes 270368 | tf_op jit(solution)/shard_map/ppermute | solution.py:243
  27.9 1.3 %collective-permute-start.16 = (bf16[1056,128]{1,0:T(8,128)(2,1)S(1)}, bf16[1056,128]{1,0:T(8,128)(2,1)S(1)}, u32[]{:S(2)}, u32[]{:S(2)}) collective-permute-start(bf16[1056,128]{1,0:T(8,128)(2,1)S(1)} %collective-permute-done.12.refs_2_), channel_id=1, source_target_pairs={{0,8},{8,0},{16,24},{24,16},{32,40},{40,32},{48,56},{56,48},{1,9},... | collective-permute-start | bytes 811016 | tf_op jit(solution)/shard_map/ppermute | solution.py:245
  29.2 0.5 collective-permute-start.13
  29.7 1.2 %collective-permute-start.14 = (bf16[528,128]{1,0:T(8,128)(2,1)S(1)}, bf16[528,128]{1,0:T(8,128)(2,1)S(1)}, u32[]{:S(2)}, u32[]{:S(2)}) collective-permute-start(bf16[528,128]{1,0:T(8,128)(2,1)S(1)} %get-tuple-element.43), channel_id=1, source_target_pairs={{0,8},{8,0},{16,24},{24,16},{32,40},{40,32},{48,56},{56,48},{1,9},... | collective-permute-start | bytes 405512 | tf_op jit(solution)/shard_map/ppermute | solution.py:245
  30.9 1.7 %collective-permute-start.15 = (bf16[528,128]{1,0:T(8,128)(2,1)S(1)}, bf16[528,128]{1,0:T(8,128)(2,1)S(1)}, u32[]{:S(2)}, u32[]{:S(2)}) collective-permute-start(bf16[528,128]{1,0:T(8,128)(2,1)S(1)} %get-tuple-element.44), channel_id=1, source_target_pairs={{0,200},{8,48},{16,216},{24,0},{32,232},{40,16},{48,248},{56,32},{... | collective-permute-start | bytes 405512 | tf_op jit(solution)/shard_map/ppermute | solution.py:243
  32.6 0.8 collective-permute-start.17
  33.7 1.2 %collective-permute-done.13.refs_3_ = bf16[528,128]{1,0:T(8,128)(2,1)S(1)} collective-permute-done((bf16[528,128]{1,0:T(8,128)(2,1)S(1)}, bf16[528,128]{1,0:T(8,128)(2,1)S(1)}, u32[]{:S(2)}, u32[]{:S(2)}) %collective-permute-start.13) | collective-permute-done | bytes 135200 | tf_op jit(solution)/shard_map/ppermute | solution.py:243
  34.9 0.4 collective-permute-done.15.refs_5_
  35.3 2.9 %collective-permute-done.17.refs_7_ = bf16[528,128]{1,0:T(8,128)(2,1)S(1)} collective-permute-done((bf16[528,128]{1,0:T(8,128)(2,1)S(1)}, bf16[528,128]{1,0:T(8,128)(2,1)S(1)}, u32[]{:S(2)}, u32[]{:S(2)}) %collective-permute-start.17) | collective-permute-done | bytes 135200 | tf_op jit(solution)/shard_map/ppermute | solution.py:243
  38.2 1.4 %shard_map.57 = (bf16[64,2048]{1,0:T(8,128)(2,1)S(1)}, bf16[64,2048]{1,0:T(8,128)(2,1)S(1)}, bf16[512,128]{1,0:T(8,128)(2,1)S(1)}, bf16[512,128]{1,0:T(8,128)(2,1)}, bf16[64,512]{1,0:T(8,128)(2,1)}) custom-call(bf16[512,512]{1,0:T(8,128)(2,1)S(1)} %fusion.1.qf_ref, bf16[512,4096]{1,0:T(8,128)(2,1)S(1)} %copy-done, ...), custom_call_target="tpu_custom_call" | custom-call | flops 1000000000 | bytes 3906250 | tf_op jit(solution)/shard_map/pallas_call | solution.py:284
  39.7 1.0 %collective-permute-start.24 = (bf16[64,2048]{1,0:T(8,128)(2,1)S(1)}, bf16[64,2048]{1,0:T(8,128)(2,1)S(1)}, u32[]{:S(2)}, u32[]{:S(2)}) collective-permute-start(bf16[64,2048]{1,0:T(8,128)(2,1)S(1)} %get-tuple-element.59), channel_id=1, source_target_pairs={{0,1},{1,2},{2,3},{3,4},{4,5},{5,6},{6,7},{7,0},{8,9},{9,10},{10,1... | collective-permute-start | bytes 786440 | tf_op jit(solution)/shard_map/ppermute | solution.py:246
  40.7 3.9 %collective-permute-start.25 = (bf16[64,2048]{1,0:T(8,128)(2,1)S(1)}, bf16[64,2048]{1,0:T(8,128)(2,1)S(1)}, u32[]{:S(2)}, u32[]{:S(2)}) collective-permute-start(bf16[64,2048]{1,0:T(8,128)(2,1)S(1)} %get-tuple-element.60), channel_id=1, source_target_pairs={{0,7},{1,0},{2,1},{3,2},{4,3},{5,4},{6,5},{7,6},{8,15},{9,8},{10,9... | collective-permute-start | bytes 786440 | tf_op jit(solution)/shard_map/ppermute | solution.py:246
  44.6 3.2 %shard_map.58 = (bf16[64,2048]{1,0:T(8,128)(2,1)S(1)}, bf16[64,2048]{1,0:T(8,128)(2,1)S(1)}, f32[128,2048]{1,0:T(8,128)S(1)}, f32[128,2048]{1,0:T(8,128)S(1)}, f...) custom-call(bf16[512,512]{1,0:T(8,128)(2,1)S(1)} %fusion.1.qf_ref, ...), custom_call_target="tpu_custom_call" | custom-call | flops 4000000000 | bytes 15625000 | tf_op jit(solution)/shard_map/pallas_call | solution.py:293
  47.8 2.7 %collective-permute-start.19 = (bf16[64,2048]{1,0:T(8,128)(2,1)S(1)}, bf16[64,2048]{1,0:T(8,128)(2,1)S(1)}, u32[]{:S(2)}, u32[]{:S(2)}) collective-permute-start(bf16[64,2048]{1,0:T(8,128)(2,1)S(1)} %get-tuple-element.51), channel_id=1, source_target_pairs={{0,7},{1,0},{2,1},{3,2},{4,3},{5,4},{6,5},{7,6},{8,15},{9,8},{10,9... | collective-permute-start | bytes 786440 | tf_op jit(solution)/shard_map/ppermute | solution.py:246
  50.4 0.7 collective-permute-done.24.from_left_ref
  51.4 2.7 %collective-permute-start.27 = (bf16[64,2048]{1,0:T(8,128)(2,1)S(1)}, bf16[64,2048]{1,0:T(8,128)(2,1)S(1)}, u32[]{:S(2)}, u32[]{:S(2)}) collective-permute-start(bf16[64,2048]{1,0:T(8,128)(2,1)S(1)} %get-tuple-element.62), channel_id=1, source_target_pairs={{0,7},{1,0},{2,1},{3,2},{4,3},{5,4},{6,5},{7,6},{8,15},{9,8},{10,9... | collective-permute-start | bytes 786440 | tf_op jit(solution)/shard_map/ppermute | solution.py:246
  54.1 2.4 %collective-permute-done.18.from_left_ref = bf16[64,2048]{1,0:T(8,128)(2,1)S(1)} collective-permute-done((bf16[64,2048]{1,0:T(8,128)(2,1)S(1)}, bf16[64,2048]{1,0:T(8,128)(2,1)S(1)}, u32[]{:S(2)}, u32[]{:S(2)}) %collective-permute-start.18) | collective-permute-done | bytes 262176 | tf_op jit(solution)/shard_map/ppermute | solution.py:246
  56.7 2.7 %collective-permute-start.21 = (bf16[64,2048]{1,0:T(8,128)(2,1)S(1)}, bf16[64,2048]{1,0:T(8,128)(2,1)S(1)}, u32[]{:S(2)}, u32[]{:S(2)}) collective-permute-start(bf16[64,2048]{1,0:T(8,128)(2,1)S(1)} %get-tuple-element.53), channel_id=1, source_target_pairs={{0,7},{1,0},{2,1},{3,2},{4,3},{5,4},{6,5},{7,6},{8,15},{9,8},{10,9... | collective-permute-start | bytes 786440 | tf_op jit(solution)/shard_map/ppermute | solution.py:246
  59.4 2.7 %collective-permute-done.26.from_left_ref = bf16[64,2048]{1,0:T(8,128)(2,1)S(1)} collective-permute-done((bf16[64,2048]{1,0:T(8,128)(2,1)S(1)}, bf16[64,2048]{1,0:T(8,128)(2,1)S(1)}, u32[]{:S(2)}, u32[]{:S(2)}) %collective-permute-start.26) | collective-permute-done | bytes 262176 | tf_op jit(solution)/shard_map/ppermute | solution.py:246
  62.3 2.7 %collective-permute-start.29 = (bf16[64,2048]{1,0:T(8,128)(2,1)S(1)}, bf16[64,2048]{1,0:T(8,128)(2,1)S(1)}, u32[]{:S(2)}, u32[]{:S(2)}) collective-permute-start(bf16[64,2048]{1,0:T(8,128)(2,1)S(1)} %get-tuple-element.64), channel_id=1, source_target_pairs={{0,7},{1,0},{2,1},{3,2},{4,3},{5,4},{6,5},{7,6},{8,15},{9,8},{10,9... | collective-permute-start | bytes 786440 | tf_op jit(solution)/shard_map/ppermute | solution.py:246
  65.0 2.8 %collective-permute-done.20.from_left_ref = bf16[64,2048]{1,0:T(8,128)(2,1)S(1)} collective-permute-done((bf16[64,2048]{1,0:T(8,128)(2,1)S(1)}, bf16[64,2048]{1,0:T(8,128)(2,1)S(1)}, u32[]{:S(2)}, u32[]{:S(2)}) %collective-permute-start.20) | collective-permute-done | bytes 262176 | tf_op jit(solution)/shard_map/ppermute | solution.py:246
  67.8 0.3 collective-permute-start.22
  68.1 2.7 %collective-permute-start.23 = (bf16[64,2048]{1,0:T(8,128)(2,1)S(1)}, bf16[64,2048]{1,0:T(8,128)(2,1)S(1)}, u32[]{:S(2)}, u32[]{:S(2)}) collective-permute-start(bf16[64,2048]{1,0:T(8,128)(2,1)S(1)} %get-tuple-element.55), channel_id=1, source_target_pairs={{0,7},{1,0},{2,1},{3,2},{4,3},{5,4},{6,5},{7,6},{8,15},{9,8},{10,9... | collective-permute-start | bytes 786440 | tf_op jit(solution)/shard_map/ppermute | solution.py:246
  70.8 2.5 %collective-permute-done.28.from_left_ref = bf16[64,2048]{1,0:T(8,128)(2,1)S(1)} collective-permute-done((bf16[64,2048]{1,0:T(8,128)(2,1)S(1)}, bf16[64,2048]{1,0:T(8,128)(2,1)S(1)}, u32[]{:S(2)}, u32[]{:S(2)}) %collective-permute-start.28) | collective-permute-done | bytes 262176 | tf_op jit(solution)/shard_map/ppermute | solution.py:246
  73.5 2.7 %collective-permute-start.31 = (bf16[64,2048]{1,0:T(8,128)(2,1)S(1)}, bf16[64,2048]{1,0:T(8,128)(2,1)S(1)}, u32[]{:S(2)}, u32[]{:S(2)}) collective-permute-start(bf16[64,2048]{1,0:T(8,128)(2,1)S(1)} %get-tuple-element.66), channel_id=1, source_target_pairs={{0,7},{1,0},{2,1},{3,2},{4,3},{5,4},{6,5},{7,6},{8,15},{9,8},{10,9... | collective-permute-start | bytes 786440 | tf_op jit(solution)/shard_map/ppermute | solution.py:246
  76.2 2.7 %collective-permute-done.22.right0 = bf16[64,2048]{1,0:T(8,128)(2,1)S(1)} collective-permute-done((bf16[64,2048]{1,0:T(8,128)(2,1)S(1)}, bf16[64,2048]{1,0:T(8,128)(2,1)S(1)}, u32[]{:S(2)}, u32[]{:S(2)}) %collective-permute-start.22) | collective-permute-done | bytes 262176 | tf_op jit(solution)/shard_map/ppermute | solution.py:246
  78.9 5.6 %collective-permute-done.30.right1 = bf16[64,2048]{1,0:T(8,128)(2,1)S(1)} collective-permute-done((bf16[64,2048]{1,0:T(8,128)(2,1)S(1)}, bf16[64,2048]{1,0:T(8,128)(2,1)S(1)}, u32[]{:S(2)}, u32[]{:S(2)}) %collective-permute-start.30) | collective-permute-done | bytes 262176 | tf_op jit(solution)/shard_map/ppermute | solution.py:246
  84.6 0.9 %last.1 = bf16[64,4096]{1,0:T(8,128)(2,1)} custom-call(f32[64,4096]{1,0:T(8,128)S(1)} %get-tuple-element.47.own_ref, bf16[64,2048]{1,0:T(8,128)(2,1)S(1)} %collective-permute-done.22.right0, bf16[64,2048]{1,0:T(8,128)(2,1)S(1)} %collective-permute-done.23.left1, bf16[64,2048]{1,0:T(8,128)(2,1)S(1)} %collective-permute-done.30.right1, ...), custom_call_target="tpu_custom_call" | custom-call | flops 100000000 | bytes 1000000 | tf_op jit(solution)/shard_map/last/pallas_call | solution.py:314
  (35 shorter events, 1.3 us)
Async XLA Ops:
  0.0 5.6 %copy-start.1 = (s32[2,4,8]{2,1,0:T(4,128)S(1)}, s32[2,4,8]{2,1,0:T(4,128)}, u32[]{:S(2)}) copy-start(s32[2,4,8]{2,1,0:T(4,128)} %own_ref.1) | copy-start | bytes 772
  0.0 5.6 %collective-permute-start = (s32[2,4,8]{2,1,0:T(4,128)}, s32[2,4,8]{2,1,0:T(4,128)S(1)}, u32[]{:S(2)}, u32[]{:S(2)}) collective-permute-start(s32[2,4,8]{2,1,0:T(4,128)} %own_ref.1), channel_id=1, source_target_pairs={{0,8},{8,0},{16,24},{24,16},{32,40},{40,32},{48,56},{56,48},{1,9},... | collective-permute-start | bytes 776 | tf_op jit(solution)/shard_map/ppermute | solution.py:245
  6.1 27.4 %copy-start.2 = (bf16[512,512]{1,0:T(8,128)(2,1)S(1)}, bf16[512,512]{1,0:T(8,128)(2,1)}, u32[]{:S(2)}) copy-start(bf16[512,512]{1,0:T(8,128)(2,1)} %param.5) | copy-start | bytes 1572868
  6.1 5.4 %collective-permute-start.1 = (bf16[528,128]{1,0:T(8,128)(2,1)S(1)}, bf16[528,128]{1,0:T(8,128)(2,1)S(1)}, u32[]{:S(2)}, u32[]{:S(2)}) collective-permute-start(bf16[528,128]{1,0:T(8,128)(2,1)S(1)} %get-tuple-element.37.refs_4_), channel_id=1, source_target_pairs={{0,16},{8,72},{16,32},{24,88},{32,48},{40,104},{48,0},{56,120},{64... | collective-permute-start | bytes 405512 | tf_op jit(solution)/shard_map/ppermute | solution.py:243
  6.2 6.2 %collective-permute-start.5 = (bf16[528,128]{1,0:T(8,128)(2,1)S(1)}, bf16[528,128]{1,0:T(8,128)(2,1)S(1)}, u32[]{:S(2)}, u32[]{:S(2)}) collective-permute-start(bf16[528,128]{1,0:T(8,128)(2,1)S(1)} %get-tuple-element.37.refs_4_), channel_id=1, source_target_pairs={{0,48},{8,200},{16,0},{24,216},{32,16},{40,232},{48,32},{56,248},{... | collective-permute-start | bytes 405512 | tf_op jit(solution)/shard_map/ppermute | solution.py:243
  8.8 4.7 %collective-permute-start.9 = (bf16[528,128]{1,0:T(8,128)(2,1)S(1)}, bf16[528,128]{1,0:T(8,128)(2,1)S(1)}, u32[]{:S(2)}, u32[]{:S(2)}) collective-permute-start(bf16[528,128]{1,0:T(8,128)(2,1)S(1)} %get-tuple-element.38), channel_id=1, source_target_pairs={{0,200},{8,48},{16,216},{24,0},{32,232},{40,16},{48,248},{56,32},{... | collective-permute-start | bytes 405512 | tf_op jit(solution)/shard_map/ppermute | solution.py:243
  9.1 5.6 %collective-permute-start.8 = (bf16[528,128]{1,0:T(8,128)(2,1)S(1)}, bf16[528,128]{1,0:T(8,128)(2,1)S(1)}, u32[]{:S(2)}, u32[]{:S(2)}) collective-permute-start(bf16[528,128]{1,0:T(8,128)(2,1)S(1)} %get-tuple-element.38), channel_id=1, source_target_pairs={{0,72},{8,16},{16,88},{24,32},{32,104},{40,48},{48,120},{56,0},{64... | collective-permute-start | bytes 405512 | tf_op jit(solution)/shard_map/ppermute | solution.py:243
  11.5 5.4 %collective-permute-start.3 = (bf16[528,128]{1,0:T(8,128)(2,1)S(1)}, bf16[528,128]{1,0:T(8,128)(2,1)S(1)}, u32[]{:S(2)}, u32[]{:S(2)}) collective-permute-start(bf16[528,128]{1,0:T(8,128)(2,1)S(1)} %collective-permute-done.1.refs_6_), channel_id=1, source_target_pairs={{0,16},{8,72},{16,32},{24,88},{32,48},{40,104},{48,0},{56,120},{64... | collective-permute-start | bytes 405512 | tf_op jit(solution)/shard_map/ppermute | solution.py:243
  11.5 7.1 %collective-permute-start.7 = (bf16[528,128]{1,0:T(8,128)(2,1)S(1)}, bf16[528,128]{1,0:T(8,128)(2,1)S(1)}, u32[]{:S(2)}, u32[]{:S(2)}) collective-permute-start(bf16[528,128]{1,0:T(8,128)(2,1)S(1)} %get-tuple-element.38), channel_id=1, source_target_pairs={{0,8},{8,0},{16,24},{24,16},{32,40},{40,32},{48,56},{56,48},{1,9},... | collective-permute-start | bytes 405512 | tf_op jit(solution)/shard_map/ppermute | solution.py:245
  12.4 6.2 %collective-permute-start.2 = (bf16[528,128]{1,0:T(8,128)(2,1)S(1)}, bf16[528,128]{1,0:T(8,128)(2,1)S(1)}, u32[]{:S(2)}, u32[]{:S(2)}) collective-permute-start(bf16[528,128]{1,0:T(8,128)(2,1)S(1)} %collective-permute-done.1.refs_6_), channel_id=1, source_target_pairs={{0,8},{8,0},{16,24},{24,16},{32,40},{40,32},{48,56},{56,48},{1,9},... | collective-permute-start | bytes 405512 | tf_op jit(solution)/shard_map/ppermute | solution.py:245
  13.6 5.1 %collective-permute-start.6 = (bf16[528,128]{1,0:T(8,128)(2,1)S(1)}, bf16[528,128]{1,0:T(8,128)(2,1)S(1)}, u32[]{:S(2)}, u32[]{:S(2)}) collective-permute-start(bf16[528,128]{1,0:T(8,128)(2,1)S(1)} %collective-permute-done.5.refs_10_), channel_id=1, source_target_pairs={{0,8},{8,0},{16,24},{24,16},{32,40},{40,32},{48,56},{56,48},{1,9},... | collective-permute-start | bytes 405512 | tf_op jit(solution)/shard_map/ppermute | solution.py:245
  14.7 4.2 %collective-permute-start.10 = (bf16[528,128]{1,0:T(8,128)(2,1)S(1)}, bf16[528,128]{1,0:T(8,128)(2,1)S(1)}, u32[]{:S(2)}, u32[]{:S(2)}) collective-permute-start(bf16[528,128]{1,0:T(8,128)(2,1)S(1)} %collective-permute-done.9.refs_11_), channel_id=1, source_target_pairs={{0,48},{8,200},{16,0},{24,216},{32,16},{40,232},{48,32},{56,248},{... | collective-permute-start | bytes 405512 | tf_op jit(solution)/shard_map/ppermute | solution.py:243
  16.9 2.7 %collective-permute-start.4 = (bf16[528,128]{1,0:T(8,128)(2,1)S(1)}, bf16[528,128]{1,0:T(8,128)(2,1)S(1)}, u32[]{:S(2)}, u32[]{:S(2)}) collective-permute-start(bf16[528,128]{1,0:T(8,128)(2,1)S(1)} %collective-permute-done.3.refs_8_), channel_id=1, source_target_pairs={{0,8},{8,0},{16,24},{24,16},{32,40},{40,32},{48,56},{56,48},{1,9},... | collective-permute-start | bytes 405512 | tf_op jit(solution)/shard_map/ppermute | solution.py:245
  19.6 18.6 %copy-start = (bf16[512,4096]{1,0:T(8,128)(2,1)S(1)}, bf16[512,4096]{1,0:T(8,128)(2,1)}, u32[]{:S(2)}) copy-start(bf16[512,4096]{1,0:T(8,128)(2,1)} %w_ref.3) | copy-start | bytes 12582916
  20.7 7.2 %collective-permute-start.12 = (bf16[1056,128]{1,0:T(8,128)(2,1)S(1)}, bf16[1056,128]{1,0:T(8,128)(2,1)S(1)}, u32[]{:S(2)}, u32[]{:S(2)}) collective-permute-start(bf16[1056,128]{1,0:T(8,128)(2,1)S(1)} %get-tuple-element.41), channel_id=1, source_target_pairs={{0,128},{8,40},{16,144},{24,56},{32,160},{40,8},{48,176},{56,24},{... | collective-permute-start | bytes 811016 | tf_op jit(solution)/shard_map/ppermute | solution.py:243
  21.0 11.6 %collective-permute-start.11 = (bf16[528,128]{1,0:T(8,128)(2,1)S(1)}, bf16[528,128]{1,0:T(8,128)(2,1)S(1)}, u32[]{:S(2)}, u32[]{:S(2)}) collective-permute-start(bf16[528,128]{1,0:T(8,128)(2,1)S(1)} %get-tuple-element.40), channel_id=1, source_target_pairs={{0,192},{8,56},{16,208},{24,8},{32,224},{40,24},{48,240},{56,40},{... | collective-permute-start | bytes 405512 | tf_op jit(solution)/shard_map/ppermute | solution.py:243
  27.9 10.4 %collective-permute-start.16 = (bf16[1056,128]{1,0:T(8,128)(2,1)S(1)}, bf16[1056,128]{1,0:T(8,128)(2,1)S(1)}, u32[]{:S(2)}, u32[]{:S(2)}) collective-permute-start(bf16[1056,128]{1,0:T(8,128)(2,1)S(1)} %collective-permute-done.12.refs_2_), channel_id=1, source_target_pairs={{0,8},{8,0},{16,24},{24,16},{32,40},{40,32},{48,56},{56,48},{1,9},... | collective-permute-start | bytes 811016 | tf_op jit(solution)/shard_map/ppermute | solution.py:245
  29.2 5.7 %collective-permute-start.13 = (bf16[528,128]{1,0:T(8,128)(2,1)S(1)}, bf16[528,128]{1,0:T(8,128)(2,1)S(1)}, u32[]{:S(2)}, u32[]{:S(2)}) collective-permute-start(bf16[528,128]{1,0:T(8,128)(2,1)S(1)} %get-tuple-element.42), channel_id=1, source_target_pairs={{0,64},{8,24},{16,80},{24,40},{32,96},{40,56},{48,112},{56,8},{64,... | collective-permute-start | bytes 405512 | tf_op jit(solution)/shard_map/ppermute | solution.py:243
  29.7 5.2 %collective-permute-start.14 = (bf16[528,128]{1,0:T(8,128)(2,1)S(1)}, bf16[528,128]{1,0:T(8,128)(2,1)S(1)}, u32[]{:S(2)}, u32[]{:S(2)}) collective-permute-start(bf16[528,128]{1,0:T(8,128)(2,1)S(1)} %get-tuple-element.43), channel_id=1, source_target_pairs={{0,8},{8,0},{16,24},{24,16},{32,40},{40,32},{48,56},{56,48},{1,9},... | collective-permute-start | bytes 405512 | tf_op jit(solution)/shard_map/ppermute | solution.py:245
  30.9 4.4 %collective-permute-start.15 = (bf16[528,128]{1,0:T(8,128)(2,1)S(1)}, bf16[528,128]{1,0:T(8,128)(2,1)S(1)}, u32[]{:S(2)}, u32[]{:S(2)}) collective-permute-start(bf16[528,128]{1,0:T(8,128)(2,1)S(1)} %get-tuple-element.44), channel_id=1, source_target_pairs={{0,200},{8,48},{16,216},{24,0},{32,232},{40,16},{48,248},{56,32},{... | collective-permute-start | bytes 405512 | tf_op jit(solution)/shard_map/ppermute | solution.py:243
  32.6 5.6 %collective-permute-start.17 = (bf16[528,128]{1,0:T(8,128)(2,1)S(1)}, bf16[528,128]{1,0:T(8,128)(2,1)S(1)}, u32[]{:S(2)}, u32[]{:S(2)}) collective-permute-start(bf16[528,128]{1,0:T(8,128)(2,1)S(1)} %get-tuple-element.45), channel_id=1, source_target_pairs={{0,72},{8,16},{16,88},{24,32},{32,104},{40,48},{48,120},{56,0},{64... | collective-permute-start | bytes 405512 | tf_op jit(solution)/shard_map/ppermute | solution.py:243
  39.7 11.5 %collective-permute-start.24 = (bf16[64,2048]{1,0:T(8,128)(2,1)S(1)}, bf16[64,2048]{1,0:T(8,128)(2,1)S(1)}, u32[]{:S(2)}, u32[]{:S(2)}) collective-permute-start(bf16[64,2048]{1,0:T(8,128)(2,1)S(1)} %get-tuple-element.59), channel_id=1, source_target_pairs={{0,1},{1,2},{2,3},{3,4},{4,5},{5,6},{6,7},{7,0},{8,9},{9,10},{10,1... | collective-permute-start | bytes 786440 | tf_op jit(solution)/shard_map/ppermute | solution.py:246
  40.7 10.5 %collective-permute-start.25 = (bf16[64,2048]{1,0:T(8,128)(2,1)S(1)}, bf16[64,2048]{1,0:T(8,128)(2,1)S(1)}, u32[]{:S(2)}, u32[]{:S(2)}) collective-permute-start(bf16[64,2048]{1,0:T(8,128)(2,1)S(1)} %get-tuple-element.60), channel_id=1, source_target_pairs={{0,7},{1,0},{2,1},{3,2},{4,3},{5,4},{6,5},{7,6},{8,15},{9,8},{10,9... | collective-permute-start | bytes 786440 | tf_op jit(solution)/shard_map/ppermute | solution.py:246
  47.8 8.7 %collective-permute-start.18 = (bf16[64,2048]{1,0:T(8,128)(2,1)S(1)}, bf16[64,2048]{1,0:T(8,128)(2,1)S(1)}, u32[]{:S(2)}, u32[]{:S(2)}) collective-permute-start(bf16[64,2048]{1,0:T(8,128)(2,1)S(1)} %get-tuple-element.50), channel_id=1, source_target_pairs={{0,1},{1,2},{2,3},{3,4},{4,5},{5,6},{6,7},{7,0},{8,9},{9,10},{10,1... | collective-permute-start | bytes 786440 | tf_op jit(solution)/shard_map/ppermute | solution.py:246
  47.8 8.7 %collective-permute-start.19 = (bf16[64,2048]{1,0:T(8,128)(2,1)S(1)}, bf16[64,2048]{1,0:T(8,128)(2,1)S(1)}, u32[]{:S(2)}, u32[]{:S(2)}) collective-permute-start(bf16[64,2048]{1,0:T(8,128)(2,1)S(1)} %get-tuple-element.51), channel_id=1, source_target_pairs={{0,7},{1,0},{2,1},{3,2},{4,3},{5,4},{6,5},{7,6},{8,15},{9,8},{10,9... | collective-permute-start | bytes 786440 | tf_op jit(solution)/shard_map/ppermute | solution.py:246
  51.3 10.8 %collective-permute-start.26 = (bf16[64,2048]{1,0:T(8,128)(2,1)S(1)}, bf16[64,2048]{1,0:T(8,128)(2,1)S(1)}, u32[]{:S(2)}, u32[]{:S(2)}) collective-permute-start(bf16[64,2048]{1,0:T(8,128)(2,1)S(1)} %get-tuple-element.61), channel_id=1, source_target_pairs={{0,1},{1,2},{2,3},{3,4},{4,5},{5,6},{6,7},{7,0},{8,9},{9,10},{10,1... | collective-permute-start | bytes 786440 | tf_op jit(solution)/shard_map/ppermute | solution.py:246
  51.4 10.7 %collective-permute-start.27 = (bf16[64,2048]{1,0:T(8,128)(2,1)S(1)}, bf16[64,2048]{1,0:T(8,128)(2,1)S(1)}, u32[]{:S(2)}, u32[]{:S(2)}) collective-permute-start(bf16[64,2048]{1,0:T(8,128)(2,1)S(1)} %get-tuple-element.62), channel_id=1, source_target_pairs={{0,7},{1,0},{2,1},{3,2},{4,3},{5,4},{6,5},{7,6},{8,15},{9,8},{10,9... | collective-permute-start | bytes 786440 | tf_op jit(solution)/shard_map/ppermute | solution.py:246
  56.6 11.1 %collective-permute-start.20 = (bf16[64,2048]{1,0:T(8,128)(2,1)S(1)}, bf16[64,2048]{1,0:T(8,128)(2,1)S(1)}, u32[]{:S(2)}, u32[]{:S(2)}) collective-permute-start(bf16[64,2048]{1,0:T(8,128)(2,1)S(1)} %get-tuple-element.52), channel_id=1, source_target_pairs={{0,1},{1,2},{2,3},{3,4},{4,5},{5,6},{6,7},{7,0},{8,9},{9,10},{10,1... | collective-permute-start | bytes 786440 | tf_op jit(solution)/shard_map/ppermute | solution.py:246
  56.7 11.0 %collective-permute-start.21 = (bf16[64,2048]{1,0:T(8,128)(2,1)S(1)}, bf16[64,2048]{1,0:T(8,128)(2,1)S(1)}, u32[]{:S(2)}, u32[]{:S(2)}) collective-permute-start(bf16[64,2048]{1,0:T(8,128)(2,1)S(1)} %get-tuple-element.53), channel_id=1, source_target_pairs={{0,7},{1,0},{2,1},{3,2},{4,3},{5,4},{6,5},{7,6},{8,15},{9,8},{10,9... | collective-permute-start | bytes 786440 | tf_op jit(solution)/shard_map/ppermute | solution.py:246
  62.2 11.1 %collective-permute-start.28 = (bf16[64,2048]{1,0:T(8,128)(2,1)S(1)}, bf16[64,2048]{1,0:T(8,128)(2,1)S(1)}, u32[]{:S(2)}, u32[]{:S(2)}) collective-permute-start(bf16[64,2048]{1,0:T(8,128)(2,1)S(1)} %get-tuple-element.63), channel_id=1, source_target_pairs={{0,1},{1,2},{2,3},{3,4},{4,5},{5,6},{6,7},{7,0},{8,9},{9,10},{10,1... | collective-permute-start | bytes 786440 | tf_op jit(solution)/shard_map/ppermute | solution.py:246
  62.3 11.0 %collective-permute-start.29 = (bf16[64,2048]{1,0:T(8,128)(2,1)S(1)}, bf16[64,2048]{1,0:T(8,128)(2,1)S(1)}, u32[]{:S(2)}, u32[]{:S(2)}) collective-permute-start(bf16[64,2048]{1,0:T(8,128)(2,1)S(1)} %get-tuple-element.64), channel_id=1, source_target_pairs={{0,7},{1,0},{2,1},{3,2},{4,3},{5,4},{6,5},{7,6},{8,15},{9,8},{10,9... | collective-permute-start | bytes 786440 | tf_op jit(solution)/shard_map/ppermute | solution.py:246
  67.8 11.1 %collective-permute-start.22 = (bf16[64,2048]{1,0:T(8,128)(2,1)S(1)}, bf16[64,2048]{1,0:T(8,128)(2,1)S(1)}, u32[]{:S(2)}, u32[]{:S(2)}) collective-permute-start(bf16[64,2048]{1,0:T(8,128)(2,1)S(1)} %get-tuple-element.54), channel_id=1, source_target_pairs={{0,1},{1,2},{2,3},{3,4},{4,5},{5,6},{6,7},{7,0},{8,9},{9,10},{10,1... | collective-permute-start | bytes 786440 | tf_op jit(solution)/shard_map/ppermute | solution.py:246
  68.1 10.8 %collective-permute-start.23 = (bf16[64,2048]{1,0:T(8,128)(2,1)S(1)}, bf16[64,2048]{1,0:T(8,128)(2,1)S(1)}, u32[]{:S(2)}, u32[]{:S(2)}) collective-permute-start(bf16[64,2048]{1,0:T(8,128)(2,1)S(1)} %get-tuple-element.55), channel_id=1, source_target_pairs={{0,7},{1,0},{2,1},{3,2},{4,3},{5,4},{6,5},{7,6},{8,15},{9,8},{10,9... | collective-permute-start | bytes 786440 | tf_op jit(solution)/shard_map/ppermute | solution.py:246
  73.4 11.1 %collective-permute-start.30 = (bf16[64,2048]{1,0:T(8,128)(2,1)S(1)}, bf16[64,2048]{1,0:T(8,128)(2,1)S(1)}, u32[]{:S(2)}, u32[]{:S(2)}) collective-permute-start(bf16[64,2048]{1,0:T(8,128)(2,1)S(1)} %get-tuple-element.65), channel_id=1, source_target_pairs={{0,1},{1,2},{2,3},{3,4},{4,5},{5,6},{6,7},{7,0},{8,9},{9,10},{10,1... | collective-permute-start | bytes 786440 | tf_op jit(solution)/shard_map/ppermute | solution.py:246
  73.5 11.0 %collective-permute-start.31 = (bf16[64,2048]{1,0:T(8,128)(2,1)S(1)}, bf16[64,2048]{1,0:T(8,128)(2,1)S(1)}, u32[]{:S(2)}, u32[]{:S(2)}) collective-permute-start(bf16[64,2048]{1,0:T(8,128)(2,1)S(1)} %get-tuple-element.66), channel_id=1, source_target_pairs={{0,7},{1,0},{2,1},{3,2},{4,3},{5,4},{6,5},{7,6},{8,15},{9,8},{10,9... | collective-permute-start | bytes 786440 | tf_op jit(solution)/shard_map/ppermute | solution.py:246
